TPU v7x, 256 devices: a whole 4x4x8 slice. The times are simulated.
256 devices in a mesh: row: 8 (over x, core), col: 32 (over y, z).
Axes of the slice: x: 4, y: 4, z: 8, core: 2. Of those that a mesh axis runs over, the one named last changes fastest.
Arguments:
- pooled: bfloat16 [16384, 1152], P(('row', 'col')), may hold values from -32 to 32
- hidden: bfloat16 [16384, 4304], P(('row', 'col')), may hold values from -6 to 6
- text: bfloat16 [16384, 1152], P(('row', 'col')), may hold values from -12 to 12
- weight: float32 [1152, 4304], P('col', 'row'), may hold values from -0.09375 to 0.09375
- row_moment: float32 [1152], P('col'), may hold values from 1e-07 to 1e-05
- col_moment: float32 [4304], P('row'), may hold values from 1e-07 to 1e-05
- log_scale: float32 [], replicated, may hold values from 4.2 to 4.8
- bias: float32 [], replicated, may hold values from -16 to -12
Outputs:
- update: float32 [1152, 4304], P('col', 'row')
- new_row: float32 [1152], P('col')
- new_col: float32 [4304], P('row')
- loss: float32 [], replicated
All inputs are finite; a program needn't handle non-finite values.
Results may differ from a plain program's by a relative error of at most 0.004.
Values may be sent and summed in bfloat16 or wider, within the bound.
A program may use at most 128 MiB of HBM per device.

v0:
```python
import functools

import jax
import jax.numpy as jnp
from jax import lax
from jax.sharding import Mesh
from jax.sharding import PartitionSpec as P

D = 1152
FF = 4304
ROW = ("row_0", "row_1")
COL = ("col_0", "col_1")
ROW_COL = ("row_0", "row_1", "col_0", "col_1")


EPSILON = 1e-06
DECAY_RATE = 0.8
CLIP_LEVEL = 1.0
FLOOR_VALUE = 1e-30


def laid_out(pieces, dim):
    dims = list(pieces.shape[1:])
    dims[dim] *= pieces.shape[0]
    return jnp.moveaxis(pieces, 0, dim).reshape(dims)


def sent_to_all(array, axis):
    copies = jnp.broadcast_to(array, (lax.axis_size(axis), *array.shape))
    return lax.all_to_all(copies, axis, split_axis=0, concat_axis=0, tiled=True)


def collect(array, axis, dim):
    return laid_out(sent_to_all(array, axis), dim)


def split_up(array, dim, devices):
    dims = array.shape
    pieces = array.reshape(*dims[:dim], devices, dims[dim] // devices, *dims[dim + 1 :])
    return jnp.moveaxis(pieces, dim, 0)


def sum_at_owner(array, axis, dim):
    pieces = split_up(array, dim, lax.axis_size(axis))
    arrived = lax.all_to_all(pieces, axis, split_axis=0, concat_axis=0, tiled=True)
    return arrived.sum(axis=0)


def sum_by_axis(running, axes):
    for axis in axes:
        running = lax.psum_scatter(running, axis, scatter_dimension=0, tiled=True)
    return running


def of_everyone(array, axis):
    everything = sent_to_all(array, axis)
    return jnp.sum(everything, axis=0)


def one_axis_at_a_time(array, axes):
    return functools.reduce(lax.psum, axes, array)


def over_row_index(positions, column, tokens, columns):
    return (positions // tokens * columns + column) * tokens + positions % tokens


def over_col_index(positions, row_place, tokens, columns):
    return row_place * columns * tokens + positions


def pair_tile(images, image_ids, texts, text_ids, logit_scale, bias, batch_total):
    logits = logit_scale * jnp.dot(images, texts.T, preferred_element_type=jnp.float32) + bias
    label_sign = jnp.where(
        image_ids[:, None] == text_ids[None, :], jnp.float32(1.0), jnp.float32(-1.0)
    )
    loss_sum = jnp.sum(jax.nn.softplus(-label_sign * logits))
    grad_logits = (-label_sign * jax.nn.sigmoid(-label_sign * logits) / batch_total).astype(
        jnp.bfloat16
    )
    return (loss_sum, logit_scale * jnp.dot(grad_logits, texts, preferred_element_type=jnp.float32))


def per_device(pooled, hidden, text, weight, row_moment, col_moment, log_scale, bias):
    rows_count = lax.axis_size(ROW)
    cols_count = lax.axis_size(COL)
    row_place = lax.axis_index(ROW)
    col_place = lax.axis_index(COL)
    tokens = pooled.shape[0]
    batch_total = tokens * rows_count * cols_count
    split_hidden = lax.all_to_all(hidden, ROW, split_axis=1, concat_axis=0, tiled=True)
    weight_half = weight.astype(jnp.bfloat16)
    partial_proj = lax.dot_general(
        split_hidden,
        collect(weight_half, COL, 0),
        (((1,), (1,)), ((), ())),
        preferred_element_type=jnp.float32,
    )
    projected = sum_at_owner(partial_proj, ROW, 0)
    mixed_rows = pooled.astype(jnp.float32) + projected
    length = jnp.sqrt(jnp.sum(mixed_rows * mixed_rows, axis=1, keepdims=True) + EPSILON)
    image_unit = mixed_rows / length
    images = image_unit.astype(jnp.bfloat16)
    text_float = text.astype(jnp.float32)
    text_units = (
        text_float / jnp.sqrt(jnp.sum(text_float * text_float, axis=1, keepdims=True) + EPSILON)
    ).astype(jnp.bfloat16)
    logit_scale = jnp.exp(log_scale)
    image_rows = collect(images, ROW, 0)
    image_ids = over_row_index(
        jnp.arange(image_rows.shape[0], dtype=jnp.int32), col_place, tokens, cols_count
    )
    piece = lax.all_gather(text_units, COL, axis=0, tiled=True)
    text_ids = over_col_index(
        jnp.arange(piece.shape[0], dtype=jnp.int32), row_place, tokens, cols_count
    )
    loss_local, unit_part = pair_tile(
        image_rows, image_ids, piece, text_ids, logit_scale, bias, batch_total
    )
    unit_grad = sum_at_owner(unit_part, ROW, 0)
    mixed_grad = (
        (unit_grad - image_unit * jnp.sum(image_unit * unit_grad, axis=1, keepdims=True)) / length
    ).astype(jnp.bfloat16)
    grad_rows = collect(mixed_grad, ROW, 0)
    gradient = sum_by_axis(
        lax.dot_general(
            grad_rows, split_hidden, (((0,), (0,)), ((), ())), preferred_element_type=jnp.float32
        ),
        COL,
    )
    squared = gradient * gradient + FLOOR_VALUE
    row_sum = of_everyone(jnp.sum(squared, axis=1), ROW)
    col_sum = of_everyone(jnp.sum(squared, axis=0), COL)
    new_row = DECAY_RATE * row_moment + (1.0 - DECAY_RATE) * row_sum / FF
    new_col = DECAY_RATE * col_moment + (1.0 - DECAY_RATE) * col_sum / D
    second = new_row[:, None] * new_col[None, :]
    raw_update = gradient / jnp.sqrt(second)
    loss_total, update_total = (
        one_axis_at_a_time(loss_local, ROW_COL),
        one_axis_at_a_time(jnp.sum(raw_update * raw_update), ROW_COL),
    )
    update_rms = jnp.sqrt(update_total / (D * FF))
    update = raw_update / jnp.maximum(1.0, update_rms / CLIP_LEVEL)
    loss = loss_total / batch_total
    return (update, new_row, new_col, loss)


def solution(mesh):
    finer = Mesh(mesh.devices.reshape(4, 2, 4, 8), ("row_0", "row_1", "col_0", "col_1"))
    return jax.shard_map(
        per_device,
        mesh=finer,
        in_specs=(
            P(ROW_COL, None),
            P(ROW_COL, None),
            P(ROW_COL, None),
            P(COL, ROW),
            P(COL),
            P(ROW),
            P(),
            P(),
        ),
        out_specs=(P(COL, ROW), P(COL), P(ROW), P()),
        check_vma=False,
    )
```

profile of v0, /device:TPU:1, one launch (start us, length us, event | category | flops | bytes accessed | tf_op | source)
XLA Modules:
  0.0 353.6 jit_solution(11246897454921141489)
XLA Ops:
  7.2 0.0 all-gather.2.cloned.1.call-start
  7.2 1.1 fusion.10
  8.3 1.7 fusion.11
  10.0 0.9 convert_element_type.22
  10.9 1.3 broadcast_in_dim.32
  12.2 12.0 %all-to-all-start.1 = ((bf16[32,36,538]{2,1,0:T(8,128)(2,1)}), bf16[32,36,538]{2,1,0:T(8,128)(2,1)S(1)}, u32[]{:S(2)}, u32[]{:S(2)}) async-start(bf16[32,36,538]{2,1,0:T(8,128)(2,1)} %broadcast_in_dim.32), calls=%async_computation.1 | async-start | bytes 3276800 | tf_op jit(solution)/shard_map/all_to_all | solution.py:30
  24.3 0.8 all_to_all.35
  25.1 0.9 copy.19
  26.0 42.2 %all-to-all-done.1 = bf16[32,36,538]{2,1,0:T(8,128)(2,1)S(1)} async-done(((bf16[32,36,538]{2,1,0:T(8,128)(2,1)}), bf16[32,36,538]{2,1,0:T(8,128)(2,1)S(1)}, u32[]{:S(2)}, u32[]{:S(2)}) %all-to-all-start.1) | async-done | bytes 1239584 | tf_op jit(solution)/shard_map/all_to_all | solution.py:30
  68.2 7.5 %all-to-all-start = ((bf16[64,8,538]{2,0,1:T(8,128)(2,1)}), bf16[64,8,538]{2,0,1:T(8,128)(2,1)}, u32[]{:S(2)}, u32[]{:S(2)}) async-start(bf16[64,8,538]{2,0,1:T(8,128)(2,1)} %copy.19), calls=%async_computation | async-start | bytes 1310720 | tf_op jit(solution)/shard_map/all_to_all | solution.py:91
  75.7 0.6 reshape.75
  76.4 10.2 %all-to-all-done = bf16[64,8,538]{2,0,1:T(8,128)(2,1)} async-done(((bf16[64,8,538]{2,0,1:T(8,128)(2,1)}), bf16[64,8,538]{2,0,1:T(8,128)(2,1)}, u32[]{:S(2)}, u32[]{:S(2)}) %all-to-all-start) | async-done | bytes 550944 | tf_op jit(solution)/shard_map/all_to_all | solution.py:91
  86.6 2.3 fusion.6
  88.9 32.6 %all_to_all.53 = f32[8,64,1152]{2,1,0:T(8,128)S(1)} all-to-all(f32[8,64,1152]{2,1,0:T(8,128)S(1)} %fusion.6), channel_id=1, replica_groups=mesh['row_0'=4,'row_1'=2,'col_0'=4,'col_1'=8] {'row_0','row_1'}, dimensions={0} | all-to-all | bytes 4718592 | tf_op jit(solution)/shard_map/all_to_all | solution.py:45
  121.5 0.1 reduce_sum.99
  121.6 0.1 multiply_reduce_fusion.1
  121.8 0.1 fusion.30
  121.9 1.2 broadcast_in_dim.33
  123.1 4.5 %all-to-all-start.3 = ((bf16[8,64,1152]{2,1,0:T(8,128)(2,1)}), bf16[8,64,1152]{2,1,0:T(8,128)(2,1)S(1)}, u32[]{:S(2)}, u32[]{:S(2)}) async-start(bf16[8,64,1152]{2,1,0:T(8,128)(2,1)} %broadcast_in_dim.33), calls=%async_computation.3 | async-start | bytes 2359296 | tf_op jit(solution)/shard_map/all_to_all | solution.py:30
  129.0 15.0 %all-to-all-done.3 = bf16[8,64,1152]{2,1,0:T(8,128)(2,1)S(1)} async-done(((bf16[8,64,1152]{2,1,0:T(8,128)(2,1)}), bf16[8,64,1152]{2,1,0:T(8,128)(2,1)S(1)}, u32[]{:S(2)}, u32[]{:S(2)}) %all-to-all-start.3) | async-done | bytes 1179680 | tf_op jit(solution)/shard_map/all_to_all | solution.py:30
  144.0 8.2 %fusion.1 = (f32[]{:T(128)}, f32[512,2048]{1,0:T(8,128)S(1)}) fusion(f32[]{:T(128)S(6)} %copy.27, bf16[512,1152]{1,0:T(8,128)(2,1)S(1)} %bitcast.21, bf16[2048,1152]{1,0:T(8,128)(2,1)} %all-gather.2.cloned.1.call-done, f32[]{:T(128)S(6)} %exp.10, s32[2048]{0:T(1024)S(1)} %iota_add_fusion, s32[512]{0:T(512)S(1)} %fusion.23), kind=kOutput, calls=%fused_computation.1 | convolution fusion | flops 2429550592 | bytes 10102796 | tf_op jit(solution)/shard_map/dot_general | solution.py:73
  152.2 3.7 %convolution_multiply_fusion = f32[512,1152]{1,0:T(8,128)S(1)} fusion(bf16[2048,1152]{1,0:T(8,128)(2,1)S(1)} %copy-done.6, f32[512,2048]{1,0:T(8,128)S(1)} %get-tuple-element.15, s32[2048]{0:T(1024)S(1)} %iota_add_fusion, s32[512]{0:T(512)S(1)} %fusion.23, f32[]{:T(128)S(6)} %exp.10), kind=kOutput, calls=%fused_computation.6 | convolution fusion | flops 2425946112 | bytes 11282436 | tf_op jit(solution)/shard_map/dot_general | solution.py:81
  155.9 32.4 %all_to_all.54 = f32[8,64,1152]{2,1,0:T(8,128)S(1)} all-to-all(f32[8,64,1152]{2,1,0:T(8,128)S(1)} %bitcast.20), channel_id=1, replica_groups=mesh['row_0'=4,'row_1'=2,'col_0'=4,'col_1'=8] {'row_0','row_1'}, dimensions={0} | all-to-all | bytes 4718592 | tf_op jit(solution)/shard_map/all_to_all | solution.py:45
  188.3 0.1 reduce_sum.102
  188.4 0.2 multiply_reduce_fusion
  188.6 0.1 divide_convert_fusion
  188.8 0.1 broadcast_in_dim.34
  188.9 20.0 %all_to_all.55 = bf16[8,64,1152]{2,1,0:T(8,128)(2,1)S(1)} all-to-all(bf16[8,64,1152]{2,1,0:T(8,128)(2,1)S(1)} %broadcast_in_dim.34), channel_id=1, replica_groups=mesh['row_0'=4,'row_1'=2,'col_0'=4,'col_1'=8] {'row_0','row_1'}, dimensions={0} | all-to-all | bytes 2359296 | tf_op jit(solution)/shard_map/all_to_all | solution.py:30
  208.9 3.8 %convolution_bitcast_fusion = f32[1152,538]{1,0:T(8,128)} fusion(bf16[8,64,1152]{2,1,0:T(8,128)(2,1)S(1)} %all_to_all.55, bf16[64,8,538]{2,0,1:T(8,128)(2,1)} %all-to-all-done), kind=kOutput, calls=%fused_computation.5 | convolution fusion | flops 634650624 | bytes 4209664 | tf_op jit(solution)/shard_map/dot_general | solution.py:126
  212.7 34.8 %reduce-scatter.4.cloned.1.call-done = f32[288,538]{1,0:T(8,128)} async-done(((f32[1152,538]{1,0:T(8,128)}), f32[288,538]{1,0:T(8,128)}) %reduce-scatter.4.cloned.1.call-update) | async-done | bytes 619792 | tf_op jit(solution)/shard_map/reduce_scatter | solution.py:51
  247.5 20.8 %fusion = f32[48,538]{1,0:T(8,128)S(1)} fusion(f32[288,538]{1,0:T(8,128)} %reduce-scatter.4.cloned.1.call-done), kind=kCustom, calls=%all-reduce-scatter | all-reduce-scatter fusion | flops 206593 | bytes 724096
  268.3 2.1 collective-permute-start
  270.5 3.3 collective-permute-start.1
  273.8 0.6 dynamic-slice.4
  275.0 0.4 collective-permute-done.1
  275.4 0.4 concatenate
  275.8 0.1 fusion.14
  276.0 12.7 %all_to_all.56 = f32[8,1,36]{2,1,0:T(1,128)S(1)} all-to-all(f32[8,1,36]{2,1,0:T(1,128)S(1)} %broadcast_in_dim.35), channel_id=1, replica_groups=mesh['row_0'=4,'row_1'=2,'col_0'=4,'col_1'=8] {'row_0','row_1'}, dimensions={0} | all-to-all | bytes 2304 | tf_op jit(solution)/shard_map/all_to_all | solution.py:30
  288.7 0.7 broadcast_in_dim.36
  289.3 10.6 %all-to-all-start.7 = ((f32[32,1,538]{2,1,0:T(1,128)}), f32[32,1,538]{2,1,0:T(1,128)S(1)}, u32[]{:S(2)}, u32[]{:S(2)}) async-start(f32[32,1,538]{2,1,0:T(1,128)} %broadcast_in_dim.36), calls=%async_computation.8 | async-start | bytes 163840 | tf_op jit(solution)/shard_map/all_to_all | solution.py:30
  300.0 8.9 %all-to-all-done.7 = f32[32,1,538]{2,1,0:T(1,128)S(1)} async-done(((f32[32,1,538]{2,1,0:T(1,128)}), f32[32,1,538]{2,1,0:T(1,128)S(1)}, u32[]{:S(2)}, u32[]{:S(2)}) %all-to-all-start.7) | async-done | bytes 68896 | tf_op jit(solution)/shard_map/all_to_all | solution.py:30
  308.9 0.1 reduce_sum.107
  309.0 0.7 multiply_reduce_fusion.2
  309.7 7.5 %all-reduce.4 = (f32[]{:T(128)}, f32[]{:T(128)}) all-reduce(f32[]{:T(128)} %multiply_reduce_fusion.2, f32[]{:T(128)} %get-tuple-element.14), channel_id=1, replica_groups=mesh['row_0'=4,'row_1'=2,'col_0'=4,'col_1'=8] {'row_0'}, use_global_device_ids=true, to_apply=%region_12.13 | all-reduce | flops 2 | bytes 16 | tf_op jit(solution)/shard_map/psum | solution.py:61
  317.2 6.9 %all-reduce.5 = (f32[]{:T(128)}, f32[]{:T(128)}) all-reduce(f32[]{:T(128)} %get-tuple-element.10, f32[]{:T(128)} %get-tuple-element.11), channel_id=1, replica_groups=mesh['row_0'=4,'row_1'=2,'col_0'=4,'col_1'=8] {'row_1'}, use_global_device_ids=true, to_apply=%region_13.14 | all-reduce | flops 2 | bytes 16 | tf_op jit(solution)/shard_map/psum | solution.py:61
  324.1 7.5 %all-reduce.3 = (f32[]{:T(128)}, f32[]{:T(128)}) all-reduce(f32[]{:T(128)} %get-tuple-element.12, f32[]{:T(128)} %get-tuple-element.13), channel_id=1, replica_groups=mesh['row_0'=4,'row_1'=2,'col_0'=4,'col_1'=8] {'col_0'}, use_global_device_ids=true, to_apply=%region_14.15 | all-reduce | flops 2 | bytes 16 | tf_op jit(solution)/shard_map/psum | solution.py:61
  331.6 12.0 %all-reduce.2 = (f32[]{:T(128)}, f32[]{:T(128)}) all-reduce(f32[]{:T(128)} %get-tuple-element.8, f32[]{:T(128)} %get-tuple-element.9), channel_id=1, replica_groups=mesh['row_0'=4,'row_1'=2,'col_0'=4,'col_1'=8] {'col_1'}, use_global_device_ids=true, to_apply=%region_15.16 | all-reduce | flops 2 | bytes 16 | tf_op jit(solution)/shard_map/psum | solution.py:61
  344.2 0.7 fusion.15
  (30 shorter events, 0.2 us)
Async XLA Ops:
  7.2 17.1 %copy-start.1 = (bf16[64,4304]{1,0:T(8,128)(2,1)S(1)}, bf16[64,4304]{1,0:T(8,128)(2,1)}, u32[]{:S(2)}) copy-start(bf16[64,4304]{1,0:T(8,128)(2,1)} %param.9) | copy-start | bytes 1652740
  7.2 136.8 %all-gather.2.cloned.1.call-start = ((), (), s32[]{:S(2)}) async-start(), calls=%async_computation.9 | async-start | bytes 4866048 | tf_op jit(solution)/shard_map/all_gather | solution.py:113
  12.2 56.0 %all-to-all-start.1 = ((bf16[32,36,538]{2,1,0:T(8,128)(2,1)}), bf16[32,36,538]{2,1,0:T(8,128)(2,1)S(1)}, u32[]{:S(2)}, u32[]{:S(2)}) async-start(bf16[32,36,538]{2,1,0:T(8,128)(2,1)} %broadcast_in_dim.32), calls=%async_computation.1 | async-start | bytes 3276800 | tf_op jit(solution)/shard_map/all_to_all | solution.py:30
  68.2 18.4 %all-to-all-start = ((bf16[64,8,538]{2,0,1:T(8,128)(2,1)}), bf16[64,8,538]{2,0,1:T(8,128)(2,1)}, u32[]{:S(2)}, u32[]{:S(2)}) async-start(bf16[64,8,538]{2,0,1:T(8,128)(2,1)} %copy.19), calls=%async_computation | async-start | bytes 1310720 | tf_op jit(solution)/shard_map/all_to_all | solution.py:91
  88.9 32.7 %copy-start = (bf16[64,1152]{1,0:T(8,128)(2,1)S(1)}, bf16[64,1152]{1,0:T(8,128)(2,1)}, u32[]{:S(2)}) copy-start(bf16[64,1152]{1,0:T(8,128)(2,1)} %param.8) | copy-start | bytes 442372
  123.1 20.9 %all-to-all-start.3 = ((bf16[8,64,1152]{2,1,0:T(8,128)(2,1)}), bf16[8,64,1152]{2,1,0:T(8,128)(2,1)S(1)}, u32[]{:S(2)}, u32[]{:S(2)}) async-start(bf16[8,64,1152]{2,1,0:T(8,128)(2,1)} %broadcast_in_dim.33), calls=%async_computation.3 | async-start | bytes 2359296 | tf_op jit(solution)/shard_map/all_to_all | solution.py:30
  127.6 119.9 %reduce-scatter.4.cloned.1.call-start = ((), (), s32[]{:S(2)}) async-start(), calls=%async_computation.10 | async-start | bytes 3686400 | tf_op jit(solution)/shard_map/reduce_scatter | solution.py:51
  144.0 8.2 %copy-start.6 = (bf16[2048,1152]{1,0:T(8,128)(2,1)S(1)}, bf16[2048,1152]{1,0:T(8,128)(2,1)}, u32[]{:S(2)}) copy-start(bf16[2048,1152]{1,0:T(8,128)(2,1)} %all-gather.2.cloned.1.call-done) | copy-start | bytes 14155780
  208.9 64.9 %copy-start.5 = (u32[256]{0:T(256)S(1)}, u32[256]{0:T(256)}, u32[]{:S(2)}) copy-start(u32[256]{0:T(256)} %constant.101) | copy-start | bytes 3076
  212.7 87.3 %copy-start.7 = (f32[36]{0:T(128)S(1)}, f32[36]{0:T(128)}, u32[]{:S(2)}) copy-start(f32[36]{0:T(128)} %param.12) | copy-start | bytes 436
  212.7 96.3 %copy-start.3 = (f32[538]{0:T(1024)S(1)}, f32[538]{0:T(1024)}, u32[]{:S(2)}) copy-start(f32[538]{0:T(1024)} %param.13) | copy-start | bytes 6460
  268.3 7.1 %collective-permute-start = (f32[48,538]{1,0:T(8,128)S(1)}, f32[48,538]{1,0:T(8,128)S(1)}, u32[]{:S(2)}, u32[]{:S(2)}) collective-permute-start(f32[48,538]{1,0:T(8,128)S(1)} %fusion), channel_id=1, source_target_pairs={{0,1},{1,2},{2,3},{3,4},{4,5},{5,6},{6,7},{8,9},{9,10},{10,11},{11... | collective-permute-start | bytes 309896
  270.5 5.0 %collective-permute-start.1 = (f32[36,538]{1,0:T(8,128)S(1)}, f32[36,538]{1,0:T(8,128)S(1)}, u32[]{:S(2)}, u32[]{:S(2)}) collective-permute-start(f32[36,538]{1,0:T(8,128)S(1)} %slice), channel_id=1, source_target_pairs={{0,2},{1,3},{2,4},{3,5},{4,6},{5,7},{8,10},{9,11},{10,12},{11,13},... | collective-permute-start | bytes 232424
  289.3 19.6 %all-to-all-start.7 = ((f32[32,1,538]{2,1,0:T(1,128)}), f32[32,1,538]{2,1,0:T(1,128)S(1)}, u32[]{:S(2)}, u32[]{:S(2)}) async-start(f32[32,1,538]{2,1,0:T(1,128)} %broadcast_in_dim.36), calls=%async_computation.8 | async-start | bytes 163840 | tf_op jit(solution)/shard_map/all_to_all | solution.py:30
  300.0 45.6 %copy-start.4 = (f32[36]{0:T(128)}, f32[36]{0:T(128)S(1)}, u32[]{:S(2)}) copy-start(f32[36]{0:T(128)S(1)} %multiply_add_fusion.2) | copy-start | bytes 436
  309.0 36.6 %copy-start.2 = (f32[538]{0:T(1024)}, f32[538]{0:T(1024)S(1)}, u32[]{:S(2)}) copy-start(f32[538]{0:T(1024)S(1)} %multiply_add_fusion.1) | copy-start | bytes 6460
Sparse Core Ops, SparseCore 0:
  10.6 89.5 all-gather.1
  212.8 34.6 reduce-scatter.3
where the time goes:
time: 358 us; the launch traced here: 354 us
  blocking collectives  152 us (42%)
  waiting for transfers between devices  112 us (31%)
  starting transfers between devices  40.2 us (11%)
  between operations  18.7 us (5%)
  matrix products  18 us (5%)
  local copies, waits for them, and re-layouts  6.69 us (2%)
  other arithmetic  6.23 us (2%)
    all_to_all x3, waiting for transfers between devices, sent_to_all(): return lax.all_to_all(copies, axis, split_axis=0, concat_axis=0, tiled=True)  66.1 us
    all_to_all x2, blocking collectives, sum_at_owner(): lax.all_to_all(pieces, axis, split_axis=0, concat_axis=0, tiled=True)  65 us
    reduce_scatter x1, waiting for transfers between devices, sum_by_axis(): running = lax.psum_scatter(running, axis, scatter_dimension=0, tiled=True)  34.8 us
    psum x4, blocking collectives, one_axis_at_a_time(): return functools.reduce(lax.psum, axes, array)  33.8 us
    all_to_all x2, blocking collectives, sent_to_all(): return lax.all_to_all(copies, axis, split_axis=0, concat_axis=0, tiled=True)  32.7 us
    all_to_all x3, starting transfers between devices, sent_to_all(): return lax.all_to_all(copies, axis, split_axis=0, concat_axis=0, tiled=True)  27.2 us
    unnamed x1, blocking collectives  20.8 us
    all_to_all x1, waiting for transfers between devices, per_device(): lax.all_to_all(hidden, ROW, split_axis=1, concat_axis=0, tiled=True)  10.2 us
  transfers between devices with their start and end apart: 8, of which 6 were waited for; matrix products, arithmetic and copies ran while one was open for 2% of the time, Pallas kernels for 0%

commit v1 on v0

--- a/solution.py
+++ b/solution.py
@@ -41,9 +41,9 @@
 
 
 def sum_at_owner(array, axis, dim):
-    pieces = split_up(array, dim, lax.axis_size(axis))
+    pieces = split_up(array.astype(jnp.bfloat16), dim, lax.axis_size(axis))
     arrived = lax.all_to_all(pieces, axis, split_axis=0, concat_axis=0, tiled=True)
-    return arrived.sum(axis=0)
+    return arrived.astype(jnp.float32).sum(axis=0)
 
 
 def sum_by_axis(running, axes):
@@ -122,11 +122,12 @@
         (unit_grad - image_unit * jnp.sum(image_unit * unit_grad, axis=1, keepdims=True)) / length
     ).astype(jnp.bfloat16)
     grad_rows = collect(mixed_grad, ROW, 0)
-    gradient = sum_by_axis(
+    gradient = sum_at_owner(
         lax.dot_general(
             grad_rows, split_hidden, (((0,), (0,)), ((), ())), preferred_element_type=jnp.float32
         ),
         COL,
+        0,
     )
     squared = gradient * gradient + FLOOR_VALUE
     row_sum = of_everyone(jnp.sum(squared, axis=1), ROW)
@@ -135,9 +136,8 @@
     new_col = DECAY_RATE * col_moment + (1.0 - DECAY_RATE) * col_sum / D
     second = new_row[:, None] * new_col[None, :]
     raw_update = gradient / jnp.sqrt(second)
-    loss_total, update_total = (
-        one_axis_at_a_time(loss_local, ROW_COL),
-        one_axis_at_a_time(jnp.sum(raw_update * raw_update), ROW_COL),
+    loss_total, update_total = lax.psum(
+        (loss_local, jnp.sum(raw_update * raw_update)), ROW_COL
     )
     update_rms = jnp.sqrt(update_total / (D * FF))
     update = raw_update / jnp.maximum(1.0, update_rms / CLIP_LEVEL)

time: 358 us -> 341 us (0.953); the launches traced: 354 us -> 341 us
  waiting for transfers between devices: 112 us -> 76.3 us
  blocking collectives: 152 us -> 187 us
  starting transfers between devices: 40.2 us -> 29.2 us
    psum x4 -> x1, blocking collectives: 33.8 us -> 73.3 us  [per_device(): lax.psum((loss_local, jnp.sum(raw_update * raw_update)), ROW_COL)]
    reduce_scatter x1 -> x0, waiting for transfers between devices: 34.8 us -> none  [sum_by_axis(): running = lax.psum_scatter(running, axis, scatter_dimension=0, tiled=True)]
    unnamed x1 -> x0, blocking collectives: 20.8 us -> none
    all_to_all x2 -> x3, blocking collectives: 65 us -> 83.1 us  [sum_at_owner(): lax.all_to_all(pieces, axis, split_axis=0, concat_axis=0, tiled=True)]
    all_to_all x3, starting transfers between devices: 27.2 us -> 21.7 us  [sent_to_all(): return lax.all_to_all(copies, axis, split_axis=0, concat_axis=0, tiled=True)]
    unnamed x2 -> x0, starting transfers between devices: 5.42 us -> none
  transfers between devices with their start and end apart: 8 -> 5, of which waited for: 6 -> 4; matrix products, arithmetic and copies ran while one was open for 2% -> 2% of each run, Pallas kernels for 0% -> 0%
where the time goes in v1:
time: 341 us
  blocking collectives  187 us (55%)
  waiting for transfers between devices  76.3 us (22%)
  starting transfers between devices  29.2 us (9%)
  between operations  18.1 us (5%)
  matrix products  16.2 us (5%)
  local copies, waits for them, and re-layouts  7.25 us (2%)
  other arithmetic  6.52 us (2%)
    all_to_all x3, blocking collectives, sum_at_owner(): lax.all_to_all(pieces, axis, split_axis=0, concat_axis=0, tiled=True)  83.1 us
    psum x1, blocking collectives, per_device(): lax.psum((loss_local, jnp.sum(raw_update * raw_update)), ROW_COL)  73.3 us
    all_to_all x3, waiting for transfers between devices, sent_to_all(): return lax.all_to_all(copies, axis, split_axis=0, concat_axis=0, tiled=True)  66.1 us
    all_to_all x2, blocking collectives, sent_to_all(): return lax.all_to_all(copies, axis, split_axis=0, concat_axis=0, tiled=True)  30.5 us
    all_to_all x3, starting transfers between devices, sent_to_all(): return lax.all_to_all(copies, axis, split_axis=0, concat_axis=0, tiled=True)  21.7 us
    all_to_all x1, waiting for transfers between devices, per_device(): lax.all_to_all(hidden, ROW, split_axis=1, concat_axis=0, tiled=True)  10.2 us
    dot_general x1, matrix products, pair_tile(): jnp.dot(images, texts.T, preferred_element_type=jnp.float32)  8.21 us
    all_to_all x1, starting transfers between devices, per_device(): lax.all_to_all(hidden, ROW, split_axis=1, concat_axis=0, tiled=True)  7.52 us
  transfers between devices with their start and end apart: 5, of which 4 were waited for; matrix products, arithmetic and copies ran while one was open for 2% of the time, Pallas kernels for 0%

profile of v1, /device:TPU:1, one launch (start us, length us, event | category | flops | bytes accessed | tf_op | source)
XLA Modules:
  0.0 340.5 jit_solution(13322253287306691034)
XLA Ops:
  7.2 0.0 all-gather.2.cloned.1.call-start
  7.2 1.1 fusion.8
  8.3 1.7 fusion.9
  10.0 0.0 all-gather.2.cloned.1.call-update
  10.0 0.9 convert_element_type.40
  10.9 1.3 broadcast_in_dim.32
  12.2 12.0 %all-to-all-start.1 = ((bf16[32,36,538]{2,1,0:T(8,128)(2,1)}), bf16[32,36,538]{2,1,0:T(8,128)(2,1)S(1)}, u32[]{:S(2)}, u32[]{:S(2)}) async-start(bf16[32,36,538]{2,1,0:T(8,128)(2,1)} %broadcast_in_dim.32), calls=%async_computation.1 | async-start | bytes 3276800 | tf_op jit(solution)/shard_map/all_to_all | solution.py:30
  24.3 0.8 all_to_all.40
  25.1 0.9 copy.16
  26.0 42.2 %all-to-all-done.1 = bf16[32,36,538]{2,1,0:T(8,128)(2,1)S(1)} async-done(((bf16[32,36,538]{2,1,0:T(8,128)(2,1)}), bf16[32,36,538]{2,1,0:T(8,128)(2,1)S(1)}, u32[]{:S(2)}, u32[]{:S(2)}) %all-to-all-start.1) | async-done | bytes 1239584 | tf_op jit(solution)/shard_map/all_to_all | solution.py:30
  68.2 7.5 %all-to-all-start = ((bf16[64,8,538]{2,0,1:T(8,128)(2,1)}), bf16[64,8,538]{2,0,1:T(8,128)(2,1)}, u32[]{:S(2)}, u32[]{:S(2)}) async-start(bf16[64,8,538]{2,0,1:T(8,128)(2,1)} %copy.16), calls=%async_computation | async-start | bytes 1310720 | tf_op jit(solution)/shard_map/all_to_all | solution.py:91
  75.7 0.6 reshape.78
  76.4 0.0 copy-start
  76.4 10.2 %all-to-all-done = bf16[64,8,538]{2,0,1:T(8,128)(2,1)} async-done(((bf16[64,8,538]{2,0,1:T(8,128)(2,1)}), bf16[64,8,538]{2,0,1:T(8,128)(2,1)}, u32[]{:S(2)}, u32[]{:S(2)}) %all-to-all-start) | async-done | bytes 550944 | tf_op jit(solution)/shard_map/all_to_all | solution.py:91
  86.6 2.3 convolution_convert_fusion
  88.9 19.9 %all_to_all.61 = bf16[8,64,1152]{2,1,0:T(8,128)(2,1)S(1)} all-to-all(bf16[8,64,1152]{2,1,0:T(8,128)(2,1)S(1)} %bitcast.21), channel_id=1, replica_groups=mesh['row_0'=4,'row_1'=2,'col_0'=4,'col_1'=8] {'row_0','row_1'}, dimensions={0} | all-to-all | bytes 2359296 | tf_op jit(solution)/shard_map/all_to_all | solution.py:45
  108.8 0.2 convert_reduce_fusion.2
  109.0 0.1 multiply_reduce_fusion.1
  109.1 0.1 fusion.28
  109.2 1.2 broadcast_in_dim.33
  110.4 4.3 %all-to-all-start.3 = ((bf16[8,64,1152]{2,1,0:T(8,128)(2,1)}), bf16[8,64,1152]{2,1,0:T(8,128)(2,1)S(1)}, u32[]{:S(2)}, u32[]{:S(2)}) async-start(bf16[8,64,1152]{2,1,0:T(8,128)(2,1)} %broadcast_in_dim.33), calls=%async_computation.3 | async-start | bytes 2359296 | tf_op jit(solution)/shard_map/all_to_all | solution.py:30
  116.1 15.0 %all-to-all-done.3 = bf16[8,64,1152]{2,1,0:T(8,128)(2,1)S(1)} async-done(((bf16[8,64,1152]{2,1,0:T(8,128)(2,1)}), bf16[8,64,1152]{2,1,0:T(8,128)(2,1)S(1)}, u32[]{:S(2)}, u32[]{:S(2)}) %all-to-all-start.3) | async-done | bytes 1179680 | tf_op jit(solution)/shard_map/all_to_all | solution.py:30
  131.2 8.2 %fusion = (f32[]{:T(128)}, f32[512,2048]{1,0:T(8,128)S(1)}) fusion(f32[]{:T(128)S(6)} %copy.22, bf16[512,1152]{1,0:T(8,128)(2,1)S(1)} %bitcast.19, bf16[2048,1152]{1,0:T(8,128)(2,1)} %all-gather.2.cloned.1.call-done, f32[]{:T(128)S(6)} %exp.10, s32[2048]{0:T(1024)S(1)} %iota_add_fusion, s32[512]{0:T(512)S(1)} %fusion.21), kind=kOutput, calls=%fused_computation.1 | convolution fusion | flops 2429550592 | bytes 10102796 | tf_op jit(solution)/shard_map/dot_general | solution.py:73
  139.4 3.7 %fusion.2 = bf16[512,1152]{1,0:T(8,128)(2,1)S(1)} fusion(bf16[2048,1152]{1,0:T(8,128)(2,1)S(1)} %copy-done.5, f32[512,2048]{1,0:T(8,128)S(1)} %get-tuple-element.9, s32[2048]{0:T(1024)S(1)} %iota_add_fusion, s32[512]{0:T(512)S(1)} %fusion.21, f32[]{:T(128)S(6)} %exp.10), kind=kOutput, calls=%fused_computation.9 | convolution fusion | flops 2426535936 | bytes 10102788 | tf_op jit(solution)/shard_map/dot_general | solution.py:81
  143.1 19.9 %all_to_all.62 = bf16[8,64,1152]{2,1,0:T(8,128)(2,1)S(1)} all-to-all(bf16[8,64,1152]{2,1,0:T(8,128)(2,1)S(1)} %bitcast.20), channel_id=1, replica_groups=mesh['row_0'=4,'row_1'=2,'col_0'=4,'col_1'=8] {'row_0','row_1'}, dimensions={0} | all-to-all | bytes 2359296 | tf_op jit(solution)/shard_map/all_to_all | solution.py:45
  163.0 0.2 convert_reduce_fusion.1
  163.1 0.2 multiply_reduce_fusion
  163.3 0.1 divide_convert_fusion
  163.5 0.1 broadcast_in_dim.34
  163.6 19.8 %all_to_all.63 = bf16[8,64,1152]{2,1,0:T(8,128)(2,1)S(1)} all-to-all(bf16[8,64,1152]{2,1,0:T(8,128)(2,1)S(1)} %broadcast_in_dim.34), channel_id=1, replica_groups=mesh['row_0'=4,'row_1'=2,'col_0'=4,'col_1'=8] {'row_0','row_1'}, dimensions={0} | all-to-all | bytes 2359296 | tf_op jit(solution)/shard_map/all_to_all | solution.py:30
  183.4 2.0 fusion.1
  185.5 1.1 copy.17
  186.6 0.0 copy-start.6
  186.6 0.0 copy-start.3
  186.6 0.4 reshape.82
  187.0 43.3 %all_to_all.64 = bf16[32,36,538]{2,1,0:T(8,128)(2,1)S(1)} all-to-all(bf16[32,36,538]{2,1,0:T(8,128)(2,1)S(1)} %reshape.82), channel_id=1, replica_groups=mesh['row_0'=4,'row_1'=2,'col_0'=4,'col_1'=8] {'col_0','col_1'}, dimensions={0} | all-to-all | bytes 2479104 | tf_op jit(solution)/shard_map/all_to_all | solution.py:45
  230.3 0.3 convert_reduce_fusion
  230.5 0.1 fusion.12
  230.7 10.8 %all_to_all.65 = f32[8,1,36]{2,1,0:T(1,128)S(1)} all-to-all(f32[8,1,36]{2,1,0:T(1,128)S(1)} %broadcast_in_dim.35), channel_id=1, replica_groups=mesh['row_0'=4,'row_1'=2,'col_0'=4,'col_1'=8] {'row_0','row_1'}, dimensions={0} | all-to-all | bytes 2304 | tf_op jit(solution)/shard_map/all_to_all | solution.py:30
  241.4 0.7 broadcast_in_dim.36
  242.1 5.3 %all-to-all-start.8 = ((f32[32,1,538]{2,1,0:T(1,128)}), f32[32,1,538]{2,1,0:T(1,128)S(1)}, u32[]{:S(2)}, u32[]{:S(2)}) async-start(f32[32,1,538]{2,1,0:T(1,128)} %broadcast_in_dim.36), calls=%async_computation.8 | async-start | bytes 163840 | tf_op jit(solution)/shard_map/all_to_all | solution.py:30
  247.5 0.0 copy-start.4
  247.5 8.9 %all-to-all-done.8 = f32[32,1,538]{2,1,0:T(1,128)S(1)} async-done(((f32[32,1,538]{2,1,0:T(1,128)}), f32[32,1,538]{2,1,0:T(1,128)S(1)}, u32[]{:S(2)}, u32[]{:S(2)}) %all-to-all-start.8) | async-done | bytes 68896 | tf_op jit(solution)/shard_map/all_to_all | solution.py:30
  256.4 0.1 reduce_sum.117
  256.4 0.0 copy-start.2
  256.5 0.7 multiply_reduce_fusion.2
  257.2 73.3 %all-reduce = (f32[]{:T(128)}, f32[]{:T(128)}) all-reduce(f32[]{:T(128)} %multiply_reduce_fusion.2, f32[]{:T(128)} %get-tuple-element.8), channel_id=1, replica_groups=mesh['row_0'=4,'row_1'=2,'col_0'=4,'col_1'=8] {'row_0','row_1','col_0','..., use_global_device_ids=true, to_apply=%region_11.12 | all-reduce | flops 2 | bytes 16 | tf_op jit(solution)/shard_map/psum | solution.py:139
  331.2 0.7 fusion.13
  (18 shorter events, 0.1 us)
Async XLA Ops:
  7.2 17.1 %copy-start.1 = (bf16[64,4304]{1,0:T(8,128)(2,1)S(1)}, bf16[64,4304]{1,0:T(8,128)(2,1)}, u32[]{:S(2)}) copy-start(bf16[64,4304]{1,0:T(8,128)(2,1)} %param.9) | copy-start | bytes 1652740
  7.2 124.0 %all-gather.2.cloned.1.call-start = ((), (), s32[]{:S(2)}) async-start(), calls=%async_computation.9 | async-start | bytes 4866048 | tf_op jit(solution)/shard_map/all_gather | solution.py:113
  12.2 56.0 %all-to-all-start.1 = ((bf16[32,36,538]{2,1,0:T(8,128)(2,1)}), bf16[32,36,538]{2,1,0:T(8,128)(2,1)S(1)}, u32[]{:S(2)}, u32[]{:S(2)}) async-start(bf16[32,36,538]{2,1,0:T(8,128)(2,1)} %broadcast_in_dim.32), calls=%async_computation.1 | async-start | bytes 3276800 | tf_op jit(solution)/shard_map/all_to_all | solution.py:30
  68.2 18.4 %all-to-all-start = ((bf16[64,8,538]{2,0,1:T(8,128)(2,1)}), bf16[64,8,538]{2,0,1:T(8,128)(2,1)}, u32[]{:S(2)}, u32[]{:S(2)}) async-start(bf16[64,8,538]{2,0,1:T(8,128)(2,1)} %copy.16), calls=%async_computation | async-start | bytes 1310720 | tf_op jit(solution)/shard_map/all_to_all | solution.py:91
  76.4 32.6 %copy-start = (bf16[64,1152]{1,0:T(8,128)(2,1)S(1)}, bf16[64,1152]{1,0:T(8,128)(2,1)}, u32[]{:S(2)}) copy-start(bf16[64,1152]{1,0:T(8,128)(2,1)} %param.8) | copy-start | bytes 442372
  110.4 20.7 %all-to-all-start.3 = ((bf16[8,64,1152]{2,1,0:T(8,128)(2,1)}), bf16[8,64,1152]{2,1,0:T(8,128)(2,1)S(1)}, u32[]{:S(2)}, u32[]{:S(2)}) async-start(bf16[8,64,1152]{2,1,0:T(8,128)(2,1)} %broadcast_in_dim.33), calls=%async_computation.3 | async-start | bytes 2359296 | tf_op jit(solution)/shard_map/all_to_all | solution.py:30
  131.2 8.2 %copy-start.5 = (bf16[2048,1152]{1,0:T(8,128)(2,1)S(1)}, bf16[2048,1152]{1,0:T(8,128)(2,1)}, u32[]{:S(2)}) copy-start(bf16[2048,1152]{1,0:T(8,128)(2,1)} %all-gather.2.cloned.1.call-done) | copy-start | bytes 14155780
  186.6 60.9 %copy-start.6 = (f32[36]{0:T(128)S(1)}, f32[36]{0:T(128)}, u32[]{:S(2)}) copy-start(f32[36]{0:T(128)} %param.12) | copy-start | bytes 436
  186.6 69.8 %copy-start.3 = (f32[538]{0:T(1024)S(1)}, f32[538]{0:T(1024)}, u32[]{:S(2)}) copy-start(f32[538]{0:T(1024)} %param.13) | copy-start | bytes 6460
  242.1 14.2 %all-to-all-start.8 = ((f32[32,1,538]{2,1,0:T(1,128)}), f32[32,1,538]{2,1,0:T(1,128)S(1)}, u32[]{:S(2)}, u32[]{:S(2)}) async-start(f32[32,1,538]{2,1,0:T(1,128)} %broadcast_in_dim.36), calls=%async_computation.8 | async-start | bytes 163840 | tf_op jit(solution)/shard_map/all_to_all | solution.py:30
  247.5 85.1 %copy-start.4 = (f32[36]{0:T(128)}, f32[36]{0:T(128)S(1)}, u32[]{:S(2)}) copy-start(f32[36]{0:T(128)S(1)} %multiply_add_fusion.2) | copy-start | bytes 436
  256.4 76.1 %copy-start.2 = (f32[538]{0:T(1024)}, f32[538]{0:T(1024)S(1)}, u32[]{:S(2)}) copy-start(f32[538]{0:T(1024)S(1)} %multiply_add_fusion.1) | copy-start | bytes 6460
Sparse Core Ops, SparseCore 0:
  10.6 89.5 all-gather.1

commit v2 on v1

v2 whole, which is shorter than its diff:
```python
import functools

import jax
import jax.numpy as jnp
from jax import lax
from jax.experimental import pallas as pl
from jax.experimental.pallas import tpu as pltpu
from jax.sharding import Mesh
from jax.sharding import PartitionSpec as P

D = 1152
FF = 4304
NX, NC, NY, NZ = 4, 2, 4, 8
TOK = 64
KD = FF // (NX * NC)
KP = 640
ED = D // (NY * NZ)
EP = 48
WLA = 256
TLA = 512
ROW = ("x", "c")
COL = ("y", "z")
ALL = ("x", "c", "y", "z")
BATCH = TOK * NX * NC * NY * NZ

EPSILON = 1e-06
DECAY_RATE = 0.8
CLIP_LEVEL = 1.0
FLOOR_VALUE = 1e-30

MESH = pl.DeviceIdType.MESH
F32 = jnp.float32
BF16 = jnp.bfloat16


def mod(value, size):
    return lax.rem(value + 2 * size, size)


class Copies:
    def __init__(self):
        self.sent = []

    def send(self, src, dst, ssem, rsem, device):
        copy = pltpu.make_async_remote_copy(src, dst, ssem, rsem, device_id=device, device_id_type=MESH)
        copy.start()
        self.sent.append(copy)

    def arrived(self, dst, ssem, rsem, device):
        pltpu.make_async_remote_copy(
            dst, dst, ssem, rsem, device_id=device, device_id_type=MESH
        ).wait_recv()

    def finish(self):
        for copy in self.sent:
            copy.wait_send()


A0, AP, AM, BP, BM, YP, YM, Y2 = 0, 4, 20, 36, 40, 44, 52, 60
N_MSG = 68
OFFSETS = [0, -1, 1, -2, 2, -3, 3, -4]


class PlaneGather:
    def __init__(self, copies, piece, a, b, la, ssem, rsem, y, z):
        self.copies, self.piece, self.a, self.b, self.la = copies, piece, a, b, la
        self.ssem, self.rsem, self.y, self.z = ssem, rsem, y, z

    def _send(self, src, dst, i, device):
        self.copies.send(src, dst, self.ssem.at[i], self.rsem.at[i], device)

    def _wait(self, dst, i, device):
        self.copies.arrived(dst, self.ssem.at[i], self.rsem.at[i], device)

    def own(self):
        self.a[self.z, self.y] = self.piece[:, : self.la]
        self.b[self.y, self.z] = self.piece[:, self.la :]

    def _a(self, zo, dy):
        return self.a.at[mod(self.z + zo, NZ), mod(self.y - dy, NY)]

    def _b(self, yo, zo):
        return self.b.at[mod(self.y + yo, NY), mod(self.z + zo, NZ)]

    def _zdev(self, o):
        return {"z": mod(self.z + o, NZ)}

    def _ydev(self, o):
        return {"y": mod(self.y + o, NY)}

    @staticmethod
    def _has(sign, s, dy):
        if s < NZ // 2:
            return s >= 1
        return s == NZ // 2 and (dy < NY // 2) == (sign > 0)

    def _ring_a(self, s, dy, sign):
        if not self._has(sign, s, dy):
            return
        src = self._a(-sign * (s - 1), dy)
        dst = src
        if s == 1 and dy == 0:
            src = self.piece.at[:, pl.ds(0, self.la)]
        self._send(src, dst, (AP if sign > 0 else AM) + (s - 1) * 4 + dy, self._zdev(sign))

    def _ring_b(self, s, sign):
        if s > (NZ // 2 if sign > 0 else NZ // 2 - 1):
            return
        dst = self._b(0, -sign * (s - 1))
        src = self.piece.at[:, pl.ds(self.la, self.piece.shape[1] - self.la)] if s == 1 else dst
        self._send(src, dst, (BP if sign > 0 else BM) + s - 1, self._zdev(sign))

    def _spread_b(self, j):
        dst = self._b(0, OFFSETS[j])
        src = self.piece.at[:, pl.ds(self.la, self.piece.shape[1] - self.la)] if j == 0 else dst
        self._send(src, dst, YP + j, self._ydev(1))
        self._send(src, dst, YM + j, self._ydev(-1))

    def _near_b(self, j):
        o = OFFSETS[j]
        self._wait(self._b(-1, o), YP + j, self._ydev(-1))
        if j % 2 == 0:
            self._send(self._b(-1, o), self._b(-1, o), Y2 + j, self._ydev(1))
        self._wait(self._b(1, o), YM + j, self._ydev(1))
        if j % 2 == 1:
            self._send(self._b(1, o), self._b(1, o), Y2 + j, self._ydev(-1))

    def far(self, j):
        o = OFFSETS[j]
        yo = -2 if j % 2 == 0 else 2
        self._wait(self._b(yo, o), Y2 + j, self._ydev(-1 if j % 2 == 0 else 1))

    def start(self):
        for dy in range(1, NY):
            self._send(self.piece.at[:, pl.ds(0, self.la)], self._a(0, 0), A0 + dy - 1, self._ydev(dy))
        for sign in (1, -1):
            self._ring_b(1, sign)
            self._ring_a(1, 0, sign)
        self._spread_b(0)

    def step(self, k):
        for s_sign in (1, -1):
            if k <= (NZ // 2 if s_sign > 0 else NZ // 2 - 1):
                self._wait(self._b(0, -s_sign * k), (BP if s_sign > 0 else BM) + k - 1, self._zdev(-s_sign))
                self._ring_b(k + 1, s_sign)
                self._spread_b(OFFSETS.index(-s_sign * k))
        for dy in range(NY):
            if k == 1:
                if dy == 0:
                    continue
                self._wait(self._a(0, dy), A0 + dy - 1, self._ydev(-dy))
                self._ring_a(1, dy, 1)
                self._ring_a(1, dy, -1)
                continue
            s = k - 1
            for sign in (1, -1):
                if self._has(sign, s, dy):
                    self._wait(
                        self._a(-sign * s, dy), (AP if sign > 0 else AM) + (s - 1) * 4 + dy, self._zdev(-sign)
                    )
                    self._ring_a(s + 1, dy, sign)
        for j, o in enumerate(OFFSETS):
            if abs(o) == k - 1:
                self._near_b(j)


def front_kernel(
    hid, wp, text, pooled, scale_ref, bias_ref,
    h_out, mg_out, loss_out,
    wa, wb, wc, ta, tb, tn, part, give, take, share, got, img, unit, length,
    acc, give2, take2, share2, got2,
    w_s, w_r, t_s, t_r, h_s, h_r, p_s, p_r, i_s, i_r, u_s, u_r, m_s, m_r,
):
    x, c = lax.axis_index("x"), lax.axis_index("c")
    y, z = lax.axis_index("y"), lax.axis_index("z")
    me = c * NX + x
    other = 1 - c

    barrier = pltpu.get_barrier_semaphore()
    peers = [{"z": mod(z + 1, NZ)}, {"z": mod(z - 1, NZ)}]
    peers += [{"y": mod(y + dy, NY)} for dy in range(1, NY)]
    peers += [
        {"x": mod(x + dx, NX), "c": lax.rem(c + dc, NC)}
        for dx in range(NX) for dc in range(NC) if dx + dc > 0
    ]
    for peer in peers:
        pl.semaphore_signal(barrier, inc=1, device_id=peer, device_id_type=MESH)
    pl.semaphore_wait(barrier, len(peers))

    copies = Copies()
    w = PlaneGather(copies, wp, wa, wb, WLA, w_s, w_r, y, z)
    t = PlaneGather(copies, tn, ta, tb, TLA, t_s, t_r, y, z)

    w.start()
    row_peers = [(dx, dc) for dx in range(NX) for dc in range(NC) if dx + dc > 0]
    for i, (dx, dc) in enumerate(row_peers):
        xx, cc = mod(x + dx, NX), lax.rem(c + dc, NC)
        copies.send(hid.at[cc * NX + xx], h_out.at[me], h_s.at[i], h_r.at[i], {"x": xx, "c": cc})
    h_out[me] = hid[me]
    w.own()
    tf = text[...].astype(F32)
    tn[...] = (tf / jnp.sqrt(jnp.sum(tf * tf, axis=1, keepdims=True) + EPSILON)).astype(BF16)
    w.step(1)
    w.step(2)
    w.step(3)
    t.own()
    t.start()
    w.step(4)
    w.step(5)
    for j in range(8):
        w.far(j)

    r_id = lax.broadcasted_iota(jnp.int32, (4 * ED, 4 * EP), 0)
    c_id = lax.broadcasted_iota(jnp.int32, (4 * ED, 4 * EP), 1)
    pick = jnp.zeros((4 * ED, 4 * EP), F32)
    for g in range(4):
        hit = (r_id >= ED * g) & (r_id < ED * (g + 1)) & (c_id - r_id == (EP - ED) * g)
        pick = jnp.where(hit, 1.0, pick)
    pick = pick.astype(BF16)
    for g in range(8):
        yy, z0 = g // 2, 4 * (g % 2)
        wc[pl.ds(4 * ED * g, 4 * ED), 0:WLA] = jnp.dot(
            pick, wa[z0 : z0 + 4, yy].reshape(4 * EP, WLA), preferred_element_type=F32
        ).astype(BF16)
        wc[pl.ds(4 * ED * g, 4 * ED), WLA:KP] = jnp.dot(
            pick, wb[yy, z0 : z0 + 4].reshape(4 * EP, KP - WLA), preferred_element_type=F32
        ).astype(BF16)

    for i, (dx, dc) in enumerate(row_peers):
        xx, cc = mod(x - dx, NX), lax.rem(c + dc, NC)
        copies.arrived(h_out.at[cc * NX + xx], h_s.at[i], h_r.at[i], {"x": xx, "c": cc})

    def project(half):
        rows = h_out[pl.ds(half * NX, NX)].reshape(NX * TOK, KP)
        for n in range(3):
            part[pl.ds(half * NX, NX), :, 384 * n : 384 * (n + 1)] = lax.dot_general(
                rows, wc[384 * n : 384 * (n + 1), :], (((1,), (1,)), ((), ())), preferred_element_type=F32
            ).reshape(NX, TOK, 384)

    def reduce_rows(val, gv, tk, sh, gt, ss, rs, between):
        gv[...] = val[pl.ds(other * NX, NX)].astype(BF16)
        between()
        copies.send(gv, tk, ss.at[0], rs.at[0], {"c": other})
        yield
        copies.arrived(tk, ss.at[0], rs.at[0], {"c": other})
        for dx in (2, 1, 3):
            xx = mod(x + dx, NX)
            sh[dx - 1] = (val[c * NX + xx] + tk[xx].astype(F32)).astype(BF16)
        for dx in (2, 1, 3):
            copies.send(sh.at[dx - 1], gt.at[dx - 1], ss.at[dx], rs.at[dx], {"x": mod(x + dx, NX)})
        yield
        total = val[me] + tk[x].astype(F32)
        for dx in (1, 3, 2):
            copies.arrived(gt.at[dx - 1], ss.at[dx], rs.at[dx], {"x": mod(x - dx, NX)})
        for dx in (1, 2, 3):
            total = total + gt[dx - 1].astype(F32)
        yield total

    def share_rows(buf, ss, rs):
        copies.send(buf.at[me], buf.at[me], ss.at[4], rs.at[4], {"c": other})
        for dx in (2, 1, 3):
            copies.send(buf.at[me], buf.at[me], ss.at[dx], rs.at[dx], {"x": mod(x + dx, NX)})
        for dx in (1, 3, 2):
            got_at = buf.at[c * NX + mod(x - dx, NX)]
            copies.arrived(got_at, ss.at[dx], rs.at[dx], {"x": mod(x - dx, NX)})
            copies.send(got_at, got_at, ss.at[4 + dx], rs.at[4 + dx], {"c": other})
        for dx in range(NX):
            copies.arrived(
                buf.at[other * NX + mod(x - dx, NX)], ss.at[4 + dx], rs.at[4 + dx], {"c": other}
            )

    project(other)
    red = reduce_rows(part, give, take, share, got, p_s, p_r, lambda: None)
    next(red)
    project(c)
    t.step(1)
    next(red)
    t.step(2)
    mixed = pooled[...].astype(F32) + next(red)
    ln = jnp.sqrt(jnp.sum(mixed * mixed, axis=1, keepdims=True) + EPSILON)
    length[...] = jnp.broadcast_to(ln, length.shape)
    un = mixed / ln
    unit[...] = un
    img[me] = un.astype(BF16)
    share_rows(img, i_s, i_r)
    t.step(3)
    t.step(4)
    t.step(5)
    for j in range(8):
        t.far(j)

    scale = scale_ref[0]
    bias = bias_ref[0]
    acc[...] = jnp.zeros_like(acc)
    loss_out[...] = jnp.zeros_like(loss_out)
    tile = 256
    col = lax.broadcasted_iota(jnp.int32, (tile, 4 * TOK), 1)
    row = lax.broadcasted_iota(jnp.int32, (tile, 4 * TOK), 0)
    n_tile = NX * NC * TOK // tile
    per = tile // TOK

    def pair(step, carry):
        g = step // n_tile
        h = lax.rem(step, n_tile)
        images = img[pl.ds(h * per, per)].reshape(tile, D)
        t_a = ta[g].reshape(NY * TOK, TLA)
        t_b = tb[:, g].reshape(NY * TOK, D - TLA)
        dims = (((1,), (1,)), ((), ()))
        logits = lax.dot_general(images[:, :TLA], t_a, dims, preferred_element_type=F32)
        logits += lax.dot_general(images[:, TLA:], t_b, dims, preferred_element_type=F32)
        logits = scale * logits + bias
        delta = TOK * (me - h * per - y) + jnp.where(g == z, 0, 1 << 20)
        same = (row - col == delta) & (col >= TOK * y) & (col < TOK * y + TOK)
        m = jnp.where(same, -logits, logits)
        e = jnp.exp(-jnp.abs(m))
        loss_out[...] += jnp.sum(
            (jnp.maximum(m, 0.0) + jnp.log1p(e)).reshape(tile // 8, 8, NY * TOK), axis=0
        )
        sig = jnp.where(m >= 0.0, 1.0, e) / (1.0 + e)
        pg = (jnp.where(same, -sig, sig) * (1.0 / BATCH)).astype(BF16)
        acc[pl.ds(h * per, per), :, :TLA] += jnp.dot(pg, t_a, preferred_element_type=F32).reshape(per, TOK, TLA)
        acc[pl.ds(h * per, per), :, TLA:] += jnp.dot(pg, t_b, preferred_element_type=F32).reshape(per, TOK, D - TLA)
        return carry

    lax.fori_loop(0, NZ * n_tile, pair, 0)

    red = reduce_rows(acc, give2, take2, share2, got2, u_s, u_r, lambda: None)
    next(red)
    next(red)
    ug = scale * next(red)
    un = unit[...]
    ln = length[:, 0:1]
    mg_out[me] = ((ug - un * jnp.sum(un * ug, axis=1, keepdims=True)) / ln).astype(BF16)
    share_rows(mg_out, m_s, m_r)
    copies.finish()


def front(hid, wp, text, pooled, scale, bias):
    vmem = pl.BlockSpec(memory_space=pltpu.VMEM)
    smem = pl.BlockSpec(memory_space=pltpu.SMEM)
    n_row = NX * NC
    dma = pltpu.SemaphoreType.DMA
    return pl.pallas_call(
        front_kernel,
        out_shape=(
            jax.ShapeDtypeStruct((n_row, TOK, KP), BF16),
            jax.ShapeDtypeStruct((n_row, TOK, D), BF16),
            jax.ShapeDtypeStruct((8, NY * TOK), F32),
        ),
        in_specs=[vmem, vmem, vmem, vmem, smem, smem],
        out_specs=(vmem, vmem, vmem),
        scratch_shapes=[
            pltpu.VMEM((NZ, NY, EP, WLA), BF16),
            pltpu.VMEM((NY, NZ, EP, KP - WLA), BF16),
            pltpu.VMEM((D, KP), BF16),
            pltpu.VMEM((NZ, NY, TOK, TLA), BF16),
            pltpu.VMEM((NY, NZ, TOK, D - TLA), BF16),
            pltpu.VMEM((TOK, D), BF16),
            pltpu.VMEM((n_row, TOK, D), F32),
            pltpu.VMEM((NX, TOK, D), BF16),
            pltpu.VMEM((NX, TOK, D), BF16),
            pltpu.VMEM((NX - 1, TOK, D), BF16),
            pltpu.VMEM((NX - 1, TOK, D), BF16),
            pltpu.VMEM((n_row, TOK, D), BF16),
            pltpu.VMEM((TOK, D), F32),
            pltpu.VMEM((TOK, 128), F32),
            pltpu.VMEM((n_row, TOK, D), F32),
            pltpu.VMEM((NX, TOK, D), BF16),
            pltpu.VMEM((NX, TOK, D), BF16),
            pltpu.VMEM((NX - 1, TOK, D), BF16),
            pltpu.VMEM((NX - 1, TOK, D), BF16),
            dma((N_MSG,)), dma((N_MSG,)), dma((N_MSG,)), dma((N_MSG,)),
            dma((8,)), dma((8,)), dma((4,)), dma((4,)), dma((8,)), dma((8,)),
            dma((4,)), dma((4,)), dma((8,)), dma((8,)),
        ],
        compiler_params=pltpu.CompilerParams(
            collective_id=0, has_side_effects=True, vmem_limit_bytes=60 * 1024 * 1024
        ),
        name="front",
    )(hid, wp, text, pooled, scale, bias)


def split_up(array, dim, devices):
    dims = array.shape
    pieces = array.reshape(*dims[:dim], devices, dims[dim] // devices, *dims[dim + 1 :])
    return jnp.moveaxis(pieces, dim, 0)


def sum_at_owner(array, axis, dim):
    pieces = split_up(array.astype(BF16), dim, lax.axis_size(axis))
    arrived = lax.all_to_all(pieces, axis, split_axis=0, concat_axis=0, tiled=True)
    return arrived.astype(F32).sum(axis=0)


def of_everyone(array, axis):
    copies = jnp.broadcast_to(array, (lax.axis_size(axis), *array.shape))
    return jnp.sum(lax.all_to_all(copies, axis, split_axis=0, concat_axis=0, tiled=True), axis=0)


def per_device(pooled, hidden, text, weight, row_moment, col_moment, log_scale, bias):
    hid = hidden.reshape(TOK, NX, NC, KD).transpose(2, 1, 0, 3).reshape(NX * NC, TOK, KD)
    hid = jnp.pad(hid, ((0, 0), (0, 0), (0, KP - KD)))
    wp = jnp.pad(weight.astype(BF16), ((0, EP - ED), (0, KP - KD)))
    h_all, mg_all, loss_tile = front(
        hid, wp, text, pooled, jnp.exp(log_scale).reshape(1), bias.reshape(1)
    )
    loss_local = jnp.sum(loss_tile)
    full = lax.dot_general(
        mg_all.reshape(-1, D), h_all.reshape(-1, KP)[:, :KD], (((0,), (0,)), ((), ())), preferred_element_type=F32
    )
    gradient = sum_at_owner(full, COL, 0)
    squared = gradient * gradient + FLOOR_VALUE
    row_sum = of_everyone(jnp.sum(squared, axis=1), ROW)
    col_sum = of_everyone(jnp.sum(squared, axis=0), COL)
    new_row = DECAY_RATE * row_moment + (1.0 - DECAY_RATE) * row_sum / FF
    new_col = DECAY_RATE * col_moment + (1.0 - DECAY_RATE) * col_sum / D
    second = new_row[:, None] * new_col[None, :]
    raw_update = gradient / jnp.sqrt(second)
    loss_total, update_total = lax.psum((loss_local, jnp.sum(raw_update * raw_update)), ALL)
    update_rms = jnp.sqrt(update_total / (D * FF))
    update = raw_update / jnp.maximum(1.0, update_rms / CLIP_LEVEL)
    return (update, new_row, new_col, loss_total / BATCH)


def solution(mesh):
    finer = Mesh(mesh.devices.reshape(NX, NC, NY, NZ), ALL)
    return jax.shard_map(
        per_device,
        mesh=finer,
        in_specs=(
            P(ALL, None), P(ALL, None), P(ALL, None), P(COL, ROW), P(COL), P(ROW), P(), P(),
        ),
        out_specs=(P(COL, ROW), P(COL), P(ROW), P()),
        check_vma=False,
    )
```

time: 341 us -> 276 us (0.81)
  Pallas kernels: 0 us -> 115 us
  blocking collectives: 187 us -> 118 us
  waiting for transfers between devices: 76.3 us -> 12.7 us
  starting transfers between devices: 29.2 us -> 12.3 us
  matrix products: 16.2 us -> 2.38 us
  between operations: 18.1 us -> 4.6 us
    pallas_call x0 -> x1, Pallas kernels: none -> 115 us  [front(): pl.pallas_call(front_kernel, out_shape=(jax.ShapeDtypeStruct((n_row, TOK,...]
    all_to_all x4 -> x2, waiting for transfers between devices: 76.3 us -> 12.7 us  [of_everyone(): lax.all_to_all(copies, axis, split_axis=0, concat_axis=0, tiled=True)]
    all_to_all x3 -> x1, blocking collectives: 83.1 us -> 44.6 us  [sum_at_owner(): lax.all_to_all(pieces, axis, split_axis=0, concat_axis=0, tiled=True)]
    all_to_all x2 -> x0, blocking collectives: 30.5 us -> none  [sent_to_all(): return lax.all_to_all(copies, axis, split_axis=0, concat_axis=0, tiled=True)]
    all_to_all x4 -> x2, starting transfers between devices: 29.2 us -> 12.3 us  [of_everyone(): lax.all_to_all(copies, axis, split_axis=0, concat_axis=0, tiled=True)]
    dot_general x4 -> x1, matrix products: 16.2 us -> 2.38 us  [per_device(): lax.dot_general(mg_all.reshape(-1, D), h_all.reshape(-1, KP)[:, :KD], (((...]
  transfers between devices with their start and end apart: 5 -> 2, of which waited for: 4 -> 2; matrix products, arithmetic and copies ran while one was open for 2% -> 0% of each run, Pallas kernels for 0% -> 0%
where the time goes in v2:
time: 276 us; the launch traced here: 275 us
  blocking collectives  118 us (43%)
  Pallas kernels  115 us (42%)
  waiting for transfers between devices  12.7 us (5%)
  starting transfers between devices  12.3 us (4%)
  local copies, waits for them, and re-layouts  7.32 us (3%)
  between operations  4.6 us (2%)
  other arithmetic  3.51 us (1%)
    pallas_call x1, Pallas kernels, front(): pl.pallas_call(front_kernel, out_shape=(jax.ShapeDtypeStruct((n_row, TOK,...  115 us
    psum x1, blocking collectives, per_device(): lax.psum((loss_local, jnp.sum(raw_update * raw_update)), ALL)  73.3 us
    all_to_all x1, blocking collectives, sum_at_owner(): lax.all_to_all(pieces, axis, split_axis=0, concat_axis=0, tiled=True)  44.6 us
    all_to_all x2, waiting for transfers between devices, of_everyone(): lax.all_to_all(copies, axis, split_axis=0, concat_axis=0, tiled=True)  12.7 us
    all_to_all x2, starting transfers between devices, of_everyone(): lax.all_to_all(copies, axis, split_axis=0, concat_axis=0, tiled=True)  12.3 us
  transfers between devices with their start and end apart: 2, of which 2 were waited for; matrix products, arithmetic and copies ran while one was open for 0% of the time, Pallas kernels for 0%

profile of v2, /device:TPU:1, one launch (start us, length us, event | category | flops | bytes accessed | tf_op | source)
XLA Modules:
  0.0 275.4 jit_solution(12561285762041439796)
XLA Ops:
  2.0 0.9 convert_element_type.13
  2.9 2.8 %reshape.39 = bf16[64,4,2,538]{3,2,1,0:T(2,128)(2,1)S(1)} reshape(bf16[64,4304]{1,0:T(8,128)(2,1)} %param.9) | data formatting | bytes 1101824 | tf_op jit(solution)/shard_map/reshape | solution.py:401
  5.7 0.1 copy.17
  5.8 0.6 pad.9.wp
  6.4 0.9 pad.8.hid
  7.4 114.7 %front.1 = (bf16[8,64,640]{2,1,0:T(8,128)(2,1)}, bf16[8,64,1152]{2,1,0:T(8,128)(2,1)}, f32[8,256]{1,0:T(8,128)}) custom-call(bf16[8,64,640]{2,1,0:T(8,128)(2,1)} %pad.8.hid, bf16[48,640]{1,0:T(8,128)(2,1)} %pad.9.wp, bf16[64,1152]{1,0:T(8,128)(2,1)} %text.1, bf16[64,1152]{1,0:T(8,128)(2,1)} %pooled.1, f32[1]{0:T(128)} %bitcast.2.scale_ref, f32[1]{0:T(128)} %bitcast.9.bias_ref), custom_call_target="tpu_custom_call" | custom-call | tf_op jit(solution)/shard_map/front/pallas_call | solution.py:343
  122.1 2.4 convolution_convert_fusion
  124.5 1.1 copy.18
  125.6 0.4 reshape.45
  126.0 44.6 %all_to_all.17 = bf16[32,36,538]{2,1,0:T(8,128)(2,1)S(1)} all-to-all(bf16[32,36,538]{2,1,0:T(8,128)(2,1)S(1)} %reshape.45), channel_id=1, replica_groups=mesh['x'=4,'c'=2,'y'=4,'z'=8] {'y','z'}, dimensions={0} | all-to-all | bytes 2479104 | tf_op jit(solution)/shard_map/all_to_all | solution.py:391
  170.6 0.0 copy-start.1
  170.6 0.0 copy-start.4
  170.6 0.0 copy-start.2
  170.6 0.3 convert_reduce_fusion
  170.9 0.1 fusion.2
  171.0 0.6 broadcast_in_dim.8
  171.6 6.8 %all-to-all-start.1 = ((f32[8,1,36]{2,1,0:T(1,128)}), f32[8,1,36]{2,1,0:T(1,128)S(1)}, u32[]{:S(2)}, u32[]{:S(2)}) async-start(f32[8,1,36]{2,1,0:T(1,128)} %broadcast_in_dim.8), calls=%async_computation.1 | async-start | bytes 8192 | tf_op jit(solution)/shard_map/all_to_all | solution.py:397
  178.5 0.0 copy-done.1
  178.5 0.7 reduce_sum.69
  179.1 3.8 %all-to-all-done.1 = f32[8,1,36]{2,1,0:T(1,128)S(1)} async-done(((f32[8,1,36]{2,1,0:T(1,128)}), f32[8,1,36]{2,1,0:T(1,128)S(1)}, u32[]{:S(2)}, u32[]{:S(2)}) %all-to-all-start.1) | async-done | bytes 1184 | tf_op jit(solution)/shard_map/all_to_all | solution.py:397
  183.0 0.7 broadcast_in_dim.9
  183.7 5.5 %all-to-all-start.2 = ((f32[32,1,538]{2,1,0:T(1,128)}), f32[32,1,538]{2,1,0:T(1,128)S(1)}, u32[]{:S(2)}, u32[]{:S(2)}) async-start(f32[32,1,538]{2,1,0:T(1,128)} %broadcast_in_dim.9), calls=%async_computation.2 | async-start | bytes 163840 | tf_op jit(solution)/shard_map/all_to_all | solution.py:397
  189.2 0.0 copy-done.4
  189.2 0.0 copy-start.3
  189.2 8.9 %all-to-all-done.2 = f32[32,1,538]{2,1,0:T(1,128)S(1)} async-done(((f32[32,1,538]{2,1,0:T(1,128)}), f32[32,1,538]{2,1,0:T(1,128)S(1)}, u32[]{:S(2)}, u32[]{:S(2)}) %all-to-all-start.2) | async-done | bytes 68896 | tf_op jit(solution)/shard_map/all_to_all | solution.py:397
  198.1 0.1 reduce_sum.67
  198.1 0.0 copy-done.2
  198.2 0.0 copy-start
  198.2 0.7 multiply_reduce_fusion
  198.9 73.3 %all-reduce.2 = (f32[]{:T(128)}, f32[]{:T(128)}) all-reduce(f32[]{:T(128)} %multiply_reduce_fusion, f32[]{:T(128)} %reduce_sum.69), channel_id=1, replica_groups=mesh['x'=4,'c'=2,'y'=4,'z'=8] {'x','c','y','z'}, use_global_device_ids=true, to_apply=%region_6.7 | all-reduce | flops 2 | bytes 16 | tf_op jit(solution)/shard_map/psum | solution.py:419
  272.9 0.7 fusion.3
  274.3 0.0 copy-done.3
  274.3 0.0 copy-done
  (3 shorter events, 0.0 us)
Async XLA Ops:
  170.6 7.8 %copy-start.1 = (f32[8,256]{1,0:T(8,128)S(1)}, f32[8,256]{1,0:T(8,128)}, u32[]{:S(2)}) copy-start(f32[8,256]{1,0:T(8,128)} %get-tuple-element.9) | copy-start | bytes 24580
  170.6 18.5 %copy-start.4 = (f32[36]{0:T(128)S(1)}, f32[36]{0:T(128)}, u32[]{:S(2)}) copy-start(f32[36]{0:T(128)} %param.12) | copy-start | bytes 436
  170.6 27.5 %copy-start.2 = (f32[538]{0:T(1024)S(1)}, f32[538]{0:T(1024)}, u32[]{:S(2)}) copy-start(f32[538]{0:T(1024)} %param.13) | copy-start | bytes 6460
  171.6 11.4 %all-to-all-start.1 = ((f32[8,1,36]{2,1,0:T(1,128)}), f32[8,1,36]{2,1,0:T(1,128)S(1)}, u32[]{:S(2)}, u32[]{:S(2)}) async-start(f32[8,1,36]{2,1,0:T(1,128)} %broadcast_in_dim.8), calls=%async_computation.1 | async-start | bytes 8192 | tf_op jit(solution)/shard_map/all_to_all | solution.py:397
  183.7 14.4 %all-to-all-start.2 = ((f32[32,1,538]{2,1,0:T(1,128)}), f32[32,1,538]{2,1,0:T(1,128)S(1)}, u32[]{:S(2)}, u32[]{:S(2)}) async-start(f32[32,1,538]{2,1,0:T(1,128)} %broadcast_in_dim.9), calls=%async_computation.2 | async-start | bytes 163840 | tf_op jit(solution)/shard_map/all_to_all | solution.py:397
  189.2 85.1 %copy-start.3 = (f32[36]{0:T(128)}, f32[36]{0:T(128)S(1)}, u32[]{:S(2)}) copy-start(f32[36]{0:T(128)S(1)} %multiply_add_fusion.2) | copy-start | bytes 436
  198.2 76.2 %copy-start = (f32[538]{0:T(1024)}, f32[538]{0:T(1024)S(1)}, u32[]{:S(2)}) copy-start(f32[538]{0:T(1024)S(1)} %multiply_add_fusion.1) | copy-start | bytes 6460

commit v3 on v2

--- a/solution.py
+++ b/solution.py
@@ -18,6 +18,8 @@
 EP = 48
 WLA = 256
 TLA = 512
+EG = 40
+GLA = 512
 ROW = ("x", "c")
 COL = ("y", "z")
 ALL = ("x", "c", "y", "z")
@@ -164,12 +166,19 @@
                 self._near_b(j)
 
 
-def front_kernel(
-    hid, wp, text, pooled, scale_ref, bias_ref,
+def whole_kernel(
+    hid, wp, text, pooled, row_moment, col_moment, scale_ref, bias_ref,
+    update_out, row_out, col_out, total_out,
     h_out, mg_out, loss_out,
     wa, wb, wc, ta, tb, tn, part, give, take, share, got, img, unit, length,
     acc, give2, take2, share2, got2,
+    grad, far_p, far_m, near_p, near_m, relay_p, relay_m,
+    r_far_p, r_far_m, r_near_p, r_near_m, r_relay_p, r_relay_m,
+    z_give, z_take, b_give, b_take, yb_give, yb_take,
+    row_give, row_take, cy_give, cy_take, cz_give, cz_take,
+    s_give, s_take, sy_give, sy_take, sz_give, sz_take,
     w_s, w_r, t_s, t_r, h_s, h_r, p_s, p_r, i_s, i_r, u_s, u_r, m_s, m_r,
+    g_s, g_r, z_s, z_r, b_s, b_r, yb_s, yb_r, st_s, st_r,
 ):
     x, c = lax.axis_index("x"), lax.axis_index("c")
     y, z = lax.axis_index("y"), lax.axis_index("z")
@@ -177,7 +186,7 @@
     other = 1 - c
 
     barrier = pltpu.get_barrier_semaphore()
-    peers = [{"z": mod(z + 1, NZ)}, {"z": mod(z - 1, NZ)}]
+    peers = [{"z": mod(z + dz, NZ)} for dz in range(1, NZ)]
     peers += [{"y": mod(y + dy, NY)} for dy in range(1, NY)]
     peers += [
         {"x": mod(x + dx, NX), "c": lax.rem(c + dc, NC)}
@@ -332,24 +341,152 @@
     ln = length[:, 0:1]
     mg_out[me] = ((ug - un * jnp.sum(un * ug, axis=1, keepdims=True)) / ln).astype(BF16)
     share_rows(mg_out, m_s, m_r)
+
+    zi = lax.broadcasted_iota(jnp.int32, (NZ, EG, 384), 0)
+    ji = lax.broadcasted_iota(jnp.int32, (NZ, EG, 384), 1)
+    li = lax.broadcasted_iota(jnp.int32, (NZ, EG, 384), 2)
+    h_all = h_out[...].reshape(NX * NC * TOK, KP)
+
+    def gradient_of(yy):
+        choose = jnp.where((ji < ED) & (li == 32 * yy + ED * zi + ji), 1.0, 0.0)
+        choose = choose.reshape(NZ * EG, 384).astype(BF16)
+        mg = mg_out[:, :, pl.ds(pl.multiple_of(256 * yy, 128), 384)].reshape(NX * NC * TOK, 384)
+        mg_t = lax.dot_general(choose, mg, (((1,), (1,)), ((), ())), preferred_element_type=F32).astype(BF16)
+        grad[yy] = jnp.dot(mg_t, h_all, preferred_element_type=F32).reshape(NZ, EG, KP)
+        b_give[:, yy] = grad[yy, :, :, GLA:].astype(BF16)
+
+    half = NZ // 2
+    y_far, y_up, y_down = mod(y + 2, NY), mod(y + 1, NY), mod(y - 1, NY)
+    up, down = {"y": y_up}, {"y": y_down}
+    gradient_of(y_far)
+    far_p[...] = grad[y_far, :half, :, :GLA].astype(BF16)
+    far_m[...] = grad[y_far, half:, :, :GLA].astype(BF16)
+    copies.send(far_p, r_far_p, g_s.at[0], g_r.at[0], up)
+    copies.send(far_m, r_far_m, g_s.at[1], g_r.at[1], down)
+    gradient_of(y_up)
+    near_p[...] = grad[y_up, half:, :, :GLA].astype(BF16)
+    copies.send(near_p, r_near_p, g_s.at[2], g_r.at[2], up)
+    gradient_of(y_down)
+    near_m[...] = grad[y_down, :half, :, :GLA].astype(BF16)
+    copies.send(near_m, r_near_m, g_s.at[3], g_r.at[3], down)
+    gradient_of(y)
+    copies.arrived(r_far_p, g_s.at[0], g_r.at[0], down)
+    relay_p[...] = (grad[y_up, :half, :, :GLA] + r_far_p[...].astype(F32)).astype(BF16)
+    copies.send(relay_p, r_relay_p, g_s.at[4], g_r.at[4], up)
+    copies.arrived(r_far_m, g_s.at[1], g_r.at[1], up)
+    relay_m[...] = (grad[y_down, half:, :, :GLA] + r_far_m[...].astype(F32)).astype(BF16)
+    copies.send(relay_m, r_relay_m, g_s.at[5], g_r.at[5], down)
+    z_order = (4, 3, 5, 2, 6, 1, 7)
+    z_near = (1, 7, 2, 6, 3, 5, 4)
+    for dz in z_order:
+        zz = mod(z + dz, NZ)
+        copies.send(b_give.at[zz], b_take.at[dz - 1], b_s.at[dz - 1], b_r.at[dz - 1], {"z": zz})
+    copies.arrived(r_near_p, g_s.at[2], g_r.at[2], down)
+    copies.arrived(r_near_m, g_s.at[3], g_r.at[3], up)
+    copies.arrived(r_relay_p, g_s.at[4], g_r.at[4], down)
+    copies.arrived(r_relay_m, g_s.at[5], g_r.at[5], up)
+    grad[y, :half, :, :GLA] += r_relay_p[...].astype(F32) + r_near_m[...].astype(F32)
+    grad[y, half:, :, :GLA] += r_near_p[...].astype(F32) + r_relay_m[...].astype(F32)
+    z_give[...] = grad[y, :, :, :GLA].astype(z_give.dtype)
+    for dz in z_order:
+        zz = mod(z + dz, NZ)
+        copies.send(z_give.at[zz], z_take.at[dz - 1], z_s.at[dz - 1], z_r.at[dz - 1], {"z": zz})
+    part_b = grad[:, pl.ds(z, 1), :, GLA:].reshape(NY, EG, KP - GLA)
+    for dz in z_near:
+        copies.arrived(b_take.at[dz - 1], b_s.at[dz - 1], b_r.at[dz - 1], {"z": mod(z - dz, NZ)})
+        part_b = part_b + b_take[dz - 1].astype(F32)
+    yb_give[...] = part_b
+    for dy in (2, 1, 3):
+        yy = mod(y + dy, NY)
+        copies.send(yb_give.at[yy], yb_take.at[dy - 1], yb_s.at[dy - 1], yb_r.at[dy - 1], {"y": yy})
+    right = yb_give[y]
+    for dy in (1, 3, 2):
+        copies.arrived(yb_take.at[dy - 1], yb_s.at[dy - 1], yb_r.at[dy - 1], {"y": mod(y - dy, NY)})
+        right = right + yb_take[dy - 1]
+    left = grad[y, pl.ds(z, 1), :, :GLA].reshape(EG, GLA)
+    for dz in z_near:
+        copies.arrived(z_take.at[dz - 1], z_s.at[dz - 1], z_r.at[dz - 1], {"z": mod(z - dz, NZ)})
+        left = left + z_take[dz - 1].astype(F32)
+    grad[y, pl.ds(z, 1), :, :GLA] = left.reshape(1, EG, GLA)
+    grad[y, pl.ds(z, 1), :, GLA:] = right.reshape(1, EG, KP - GLA)
+
+    g = grad[y, pl.ds(z, 1)].reshape(EG, KP)
+    e_id = lax.broadcasted_iota(jnp.int32, (EG, KP), 0)
+    k_id = lax.broadcasted_iota(jnp.int32, (EG, KP), 1)
+    squared = jnp.where((e_id < ED) & (k_id < KD), g * g + FLOOR_VALUE, 0.0)
+
+    def exchange(give_ref, take_ref, base, value, kind):
+        give_ref[...] = value
+        sizes = {"row": row_peers, "y": range(1, NY), "z": range(1, NZ)}[kind]
+        for i, d in enumerate(sizes):
+            if kind == "row":
+                device = {"x": mod(x + d[0], NX), "c": lax.rem(c + d[1], NC)}
+            else:
+                device = {kind: mod((y if kind == "y" else z) + d, NY if kind == "y" else NZ)}
+            copies.send(give_ref, take_ref.at[i], st_s.at[base + i], st_r.at[base + i], device)
+
+    def collected(take_ref, base, value, kind):
+        sizes = {"row": row_peers, "y": range(1, NY), "z": range(1, NZ)}[kind]
+        for i, d in enumerate(sizes):
+            if kind == "row":
+                device = {"x": mod(x - d[0], NX), "c": lax.rem(c + d[1], NC)}
+            else:
+                device = {kind: mod((y if kind == "y" else z) - d, NY if kind == "y" else NZ)}
+            copies.arrived(take_ref.at[i], st_s.at[base + i], st_r.at[base + i], device)
+            value = value + take_ref[i]
+        return value
+
+    cols = jnp.sum(squared, axis=0, keepdims=True)
+    rows = jnp.broadcast_to(jnp.sum(squared, axis=1, keepdims=True), (EG, 128))
+    exchange(cy_give, cy_take, 7, cols, "y")
+    exchange(row_give, row_take, 0, rows, "row")
+    cols = collected(cy_take, 7, cols, "y")
+    exchange(cz_give, cz_take, 10, cols, "z")
+    rows = collected(row_take, 0, rows, "row")
+    new_row = DECAY_RATE * row_moment[...] + (1.0 - DECAY_RATE) * rows / FF
+    row_out[...] = new_row
+    new_row = jnp.where(e_id[:, 0:128] < ED, new_row, 1.0)[:, 0:1]
+    cols = collected(cz_take, 10, cols, "z")
+    new_col = DECAY_RATE * col_moment[...] + (1.0 - DECAY_RATE) * cols / D
+    col_out[...] = new_col
+    new_col = jnp.where(k_id[0:1] < KD, new_col, 1.0)
+    raw = g / jnp.sqrt(new_row * new_col)
+    raw_sum = jnp.sum(jnp.sum(raw * raw, axis=0, keepdims=True), axis=1, keepdims=True)
+    loss_sum = jnp.sum(jnp.sum(loss_out[...], axis=0, keepdims=True), axis=1, keepdims=True)
+    lane = k_id[0:1, 0:128]
+    both = jnp.where(lane == 0, raw_sum, jnp.where(lane == 1, loss_sum, 0.0))
+    exchange(s_give, s_take, 17, both, "row")
+    both = collected(s_take, 17, both, "row")
+    exchange(sy_give, sy_take, 24, both, "y")
+    both = collected(sy_take, 24, both, "y")
+    exchange(sz_give, sz_take, 27, both, "z")
+    both = collected(sz_take, 27, both, "z")
+    total_out[...] = both / BATCH
+    rms = jnp.sqrt(both[:, 0:1] / (D * FF))
+    upd = raw / jnp.maximum(1.0, rms / CLIP_LEVEL)
+    update_out[...] = upd[:ED, :KD]
     copies.finish()
 
 
-def front(hid, wp, text, pooled, scale, bias):
+def step_kernel(hid, wp, text, pooled, row_moment, col_moment, scale, bias):
     vmem = pl.BlockSpec(memory_space=pltpu.VMEM)
     smem = pl.BlockSpec(memory_space=pltpu.SMEM)
     n_row = NX * NC
     dma = pltpu.SemaphoreType.DMA
     return pl.pallas_call(
-        front_kernel,
+        whole_kernel,
         out_shape=(
-            jax.ShapeDtypeStruct((n_row, TOK, KP), BF16),
-            jax.ShapeDtypeStruct((n_row, TOK, D), BF16),
-            jax.ShapeDtypeStruct((8, NY * TOK), F32),
+            jax.ShapeDtypeStruct((ED, KD), F32),
+            jax.ShapeDtypeStruct((EG, 128), F32),
+            jax.ShapeDtypeStruct((1, KP), F32),
+            jax.ShapeDtypeStruct((1, 128), F32),
         ),
-        in_specs=[vmem, vmem, vmem, vmem, smem, smem],
-        out_specs=(vmem, vmem, vmem),
+        in_specs=[vmem] * 6 + [smem] * 2,
+        out_specs=(vmem,) * 4,
         scratch_shapes=[
+            pltpu.VMEM((n_row, TOK, KP), BF16),
+            pltpu.VMEM((n_row, TOK, D), BF16),
+            pltpu.VMEM((8, NY * TOK), F32),
             pltpu.VMEM((NZ, NY, EP, WLA), BF16),
             pltpu.VMEM((NY, NZ, EP, KP - WLA), BF16),
             pltpu.VMEM((D, KP), BF16),
@@ -369,57 +506,49 @@
             pltpu.VMEM((NX, TOK, D), BF16),
             pltpu.VMEM((NX - 1, TOK, D), BF16),
             pltpu.VMEM((NX - 1, TOK, D), BF16),
+            pltpu.VMEM((NY, NZ, EG, KP), F32),
+            *[pltpu.VMEM((NZ // 2, EG, GLA), BF16)] * 12,
+            pltpu.VMEM((NZ, EG, GLA), BF16),
+            pltpu.VMEM((NZ - 1, EG, GLA), BF16),
+            pltpu.VMEM((NZ, NY, EG, KP - GLA), BF16),
+            pltpu.VMEM((NZ - 1, NY, EG, KP - GLA), BF16),
+            pltpu.VMEM((NY, EG, KP - GLA), F32),
+            pltpu.VMEM((NY - 1, EG, KP - GLA), F32),
+            pltpu.VMEM((EG, 128), F32),
+            pltpu.VMEM((n_row - 1, EG, 128), F32),
+            pltpu.VMEM((1, KP), F32),
+            pltpu.VMEM((NY - 1, 1, KP), F32),
+            pltpu.VMEM((1, KP), F32),
+            pltpu.VMEM((NZ - 1, 1, KP), F32),
+            pltpu.VMEM((1, 128), F32),
+            pltpu.VMEM((n_row - 1, 1, 128), F32),
+            pltpu.VMEM((1, 128), F32),
+            pltpu.VMEM((NY - 1, 1, 128), F32),
+            pltpu.VMEM((1, 128), F32),
+            pltpu.VMEM((NZ - 1, 1, 128), F32),
             dma((N_MSG,)), dma((N_MSG,)), dma((N_MSG,)), dma((N_MSG,)),
             dma((8,)), dma((8,)), dma((4,)), dma((4,)), dma((8,)), dma((8,)),
             dma((4,)), dma((4,)), dma((8,)), dma((8,)),
+            dma((6,)), dma((6,)), dma((7,)), dma((7,)), dma((7,)), dma((7,)),
+            dma((3,)), dma((3,)), dma((34,)), dma((34,)),
         ],
         compiler_params=pltpu.CompilerParams(
             collective_id=0, has_side_effects=True, vmem_limit_bytes=60 * 1024 * 1024
         ),
-        name="front",
-    )(hid, wp, text, pooled, scale, bias)
-
-
-def split_up(array, dim, devices):
-    dims = array.shape
-    pieces = array.reshape(*dims[:dim], devices, dims[dim] // devices, *dims[dim + 1 :])
-    return jnp.moveaxis(pieces, dim, 0)
-
-
-def sum_at_owner(array, axis, dim):
-    pieces = split_up(array.astype(BF16), dim, lax.axis_size(axis))
-    arrived = lax.all_to_all(pieces, axis, split_axis=0, concat_axis=0, tiled=True)
-    return arrived.astype(F32).sum(axis=0)
-
-
-def of_everyone(array, axis):
-    copies = jnp.broadcast_to(array, (lax.axis_size(axis), *array.shape))
-    return jnp.sum(lax.all_to_all(copies, axis, split_axis=0, concat_axis=0, tiled=True), axis=0)
+        name="step",
+    )(hid, wp, text, pooled, row_moment, col_moment, scale, bias)
 
 
 def per_device(pooled, hidden, text, weight, row_moment, col_moment, log_scale, bias):
     hid = hidden.reshape(TOK, NX, NC, KD).transpose(2, 1, 0, 3).reshape(NX * NC, TOK, KD)
     hid = jnp.pad(hid, ((0, 0), (0, 0), (0, KP - KD)))
     wp = jnp.pad(weight.astype(BF16), ((0, EP - ED), (0, KP - KD)))
-    h_all, mg_all, loss_tile = front(
-        hid, wp, text, pooled, jnp.exp(log_scale).reshape(1), bias.reshape(1)
+    row_tile = jnp.broadcast_to(jnp.pad(row_moment, (0, EG - ED))[:, None], (EG, 128))
+    col_tile = jnp.pad(col_moment, (0, KP - KD)).reshape(1, KP)
+    update, new_row, new_col, total = step_kernel(
+        hid, wp, text, pooled, row_tile, col_tile, jnp.exp(log_scale).reshape(1), bias.reshape(1)
     )
-    loss_local = jnp.sum(loss_tile)
-    full = lax.dot_general(
-        mg_all.reshape(-1, D), h_all.reshape(-1, KP)[:, :KD], (((0,), (0,)), ((), ())), preferred_element_type=F32
-    )
-    gradient = sum_at_owner(full, COL, 0)
-    squared = gradient * gradient + FLOOR_VALUE
-    row_sum = of_everyone(jnp.sum(squared, axis=1), ROW)
-    col_sum = of_everyone(jnp.sum(squared, axis=0), COL)
-    new_row = DECAY_RATE * row_moment + (1.0 - DECAY_RATE) * row_sum / FF
-    new_col = DECAY_RATE * col_moment + (1.0 - DECAY_RATE) * col_sum / D
-    second = new_row[:, None] * new_col[None, :]
-    raw_update = gradient / jnp.sqrt(second)
-    loss_total, update_total = lax.psum((loss_local, jnp.sum(raw_update * raw_update)), ALL)
-    update_rms = jnp.sqrt(update_total / (D * FF))
-    update = raw_update / jnp.maximum(1.0, update_rms / CLIP_LEVEL)
-    return (update, new_row, new_col, loss_total / BATCH)
+    return (update, new_row[:ED, 0], new_col[0, :KD], total[0, 1])
 
 
 def solution(mesh):

time: 276 us -> 171 us (0.62)
  blocking collectives: 118 us -> 0 us
  Pallas kernels: 115 us -> 157 us
  waiting for transfers between devices: 12.7 us -> 0 us
  starting transfers between devices: 12.3 us -> 0 us
  local copies, waits for them, and re-layouts: 7.32 us -> 11.2 us
  other arithmetic: 3.51 us -> 0.01 us
    psum x1 -> x0, blocking collectives: 73.3 us -> none  [per_device(): lax.psum((loss_local, jnp.sum(raw_update * raw_update)), ALL)]
    all_to_all x1 -> x0, blocking collectives: 44.6 us -> none  [sum_at_owner(): lax.all_to_all(pieces, axis, split_axis=0, concat_axis=0, tiled=True)]
    pallas_call x1, Pallas kernels: 115 us -> 157 us  [step_kernel(): pl.pallas_call(whole_kernel, out_shape=(jax.ShapeDtypeStruct((ED, KD), F3...]
    all_to_all x2 -> x0, waiting for transfers between devices: 12.7 us -> none  [of_everyone(): lax.all_to_all(copies, axis, split_axis=0, concat_axis=0, tiled=True)]
    all_to_all x2 -> x0, starting transfers between devices: 12.3 us -> none  [of_everyone(): lax.all_to_all(copies, axis, split_axis=0, concat_axis=0, tiled=True)]
    unnamed x10 -> x11, local copies, waits for them, and re-layouts: 0.02 us -> 2.9 us
  transfers between devices with their start and end apart: 2 -> 0, of which waited for: 2 -> 0; matrix products, arithmetic and copies ran while one was open for 0% -> 0% of each run, Pallas kernels for 0% -> 0%
where the time goes in v3:
time: 171 us; the launch traced here: 170 us
  Pallas kernels  157 us (92%)
  local copies, waits for them, and re-layouts  11.2 us (7%)
  between operations  2.03 us (1%)
    pallas_call x1, Pallas kernels, step_kernel(): pl.pallas_call(whole_kernel, out_shape=(jax.ShapeDtypeStruct((ED, KD), F3...  157 us

profile of v3, /device:TPU:1, one launch (start us, length us, event | category | flops | bytes accessed | tf_op | source)
XLA Modules:
  0.0 170.3 jit_solution(321826112343548844)
XLA Ops:
  0.6 2.8 %reshape.24 = bf16[64,4,2,538]{3,2,1,0:T(2,128)(2,1)S(1)} reshape(bf16[64,4304]{1,0:T(8,128)(2,1)} %param.9) | data formatting | bytes 1101824 | tf_op jit(solution)/shard_map/reshape | solution.py:543
  3.5 0.1 copy.13
  3.6 0.0 copy-start
  3.6 0.9 pad.16.hid
  4.5 0.0 copy-done
  4.5 0.0 copy-start.3
  4.5 0.6 pad.17.wp
  5.1 0.0 copy-done.3
  5.2 0.0 copy-start.1
  5.2 0.7 broadcast_in_dim.2.row_moment
  5.8 0.0 copy-done.1
  5.8 0.6 reshape.26.col_moment
  7.8 157.1 %step.1 = (f32[36,538]{1,0:T(8,128)}, f32[40,128]{1,0:T(8,128)}, f32[1,640]{1,0:T(1,128)}, f32[1,128]{1,0:T(1,128)}) custom-call(bf16[8,64,640]{2,1,0:T(8,128)(2,1)} %pad.16.hid, bf16[48,640]{1,0:T(8,128)(2,1)} %pad.17.wp, bf16[64,1152]{1,0:T(8,128)(2,1)} %text.1, bf16[64,1152]{1,0:T(8,128)(2,1)} %pooled.1, f32[40,128]{1,0:T(8,128)} %broadcast_in_dim.2.row_moment, ...), custom_call_target="tpu_custom_call" | custom-call | tf_op jit(solution)/shard_map/step/pallas_call | solution.py:476
  164.9 0.0 copy-start.2
  164.9 0.7 copy-done.2
  165.5 0.6 slice_reduce_fusion.1
  166.1 0.0 copy-start.4
  166.1 0.7 copy-done.4
  166.8 0.6 slice.11
  167.4 1.4 slice_reduce_fusion
  168.7 1.5 copy.17
  (3 shorter events, 0.0 us)
Async XLA Ops:
  3.6 0.9 copy-start
  4.5 0.7 copy-start.3
  5.2 0.7 copy-start.1
  164.9 0.7 copy-start.2
  166.1 0.7 copy-start.4

commit v4 on v2

v4 whole, which is shorter than its diff:
```python
import functools

import jax
import jax.numpy as jnp
from jax import lax
from jax.experimental import pallas as pl
from jax.experimental.pallas import tpu as pltpu
from jax.sharding import Mesh
from jax.sharding import PartitionSpec as P

D = 1152
FF = 4304
NX, NC, NY, NZ = 4, 2, 4, 8
TOK = 64
KD = FF // (NX * NC)
KP = 640
ED = D // (NY * NZ)
EP = 48
WLA = 256
TLA = 512
EG = 40
GLA = 512
ROW = ("x", "c")
COL = ("y", "z")
ALL = ("x", "c", "y", "z")
BATCH = TOK * NX * NC * NY * NZ

EPSILON = 1e-06
DECAY_RATE = 0.8
CLIP_LEVEL = 1.0
FLOOR_VALUE = 1e-30

MESH = pl.DeviceIdType.MESH
F32 = jnp.float32
BF16 = jnp.bfloat16


def mod(value, size):
    return lax.rem(value + 2 * size, size)


class Copies:
    def __init__(self):
        self.sent = []

    def send(self, src, dst, ssem, rsem, device):
        pltpu.make_async_remote_copy(src, dst, ssem, rsem, device_id=device, device_id_type=MESH).start()
        self.sent.append((src, dst, ssem, rsem, device))

    def arrived(self, dst, ssem, rsem, device):
        pltpu.make_async_remote_copy(
            dst, dst, ssem, rsem, device_id=device, device_id_type=MESH
        ).wait_recv()

    def finish(self):
        for src, dst, ssem, rsem, device in self.sent:
            pltpu.make_async_remote_copy(
                src, dst, ssem, rsem, device_id=device, device_id_type=MESH
            ).wait_send()


A0, AP, AM, BP, BM, YP, YM, Y2 = 0, 4, 20, 36, 40, 44, 52, 60
N_MSG = 68
OFFSETS = [0, -1, 1, -2, 2, -3, 3, -4]


class PlaneGather:
    def __init__(self, copies, piece, a, b, la, ssem, rsem, y, z):
        self.copies, self.piece, self.a, self.b, self.la = copies, piece, a, b, la
        self.ssem, self.rsem, self.y, self.z = ssem, rsem, y, z
        self.ys = {o: mod(y + o, NY) for o in range(1 - NY, NY)}
        self.zs = {o: mod(z + o, NZ) for o in range(-(NZ // 2), NZ // 2 + 1)}
        self.sems = [(ssem.at[i], rsem.at[i]) for i in range(N_MSG)]
        self.a_at = {(o, dy): a.at[self.zs[o], self.ys[-dy]] for o in self.zs for dy in range(NY)}
        self.b_at = {(yo, o): b.at[self.ys[yo], self.zs[o]] for o in self.zs for yo in range(-2, 3)}

    def _send(self, src, dst, i, device):
        self.copies.send(src, dst, *self.sems[i], device)

    def _wait(self, dst, i, device):
        sems = self.sems[i] if isinstance(i, int) else (self.ssem.at[i], self.rsem.at[i])
        self.copies.arrived(dst, *sems, device)

    def own(self):
        self.a[self.z, self.y] = self.piece[:, : self.la]
        self.b[self.y, self.z] = self.piece[:, self.la :]

    def _a(self, zo, dy):
        return self.a_at[zo, dy]

    def _b(self, yo, zo):
        return self.b_at[yo, zo]

    def _zdev(self, o):
        return {"z": self.zs[o]}

    def _ydev(self, o):
        return {"y": self.ys[o]}

    @staticmethod
    def _has(sign, s, dy):
        if s < NZ // 2:
            return s >= 1
        return s == NZ // 2 and (dy < NY // 2) == (sign > 0)

    def _ring_a(self, s, dy, sign):
        if not self._has(sign, s, dy):
            return
        src = self._a(-sign * (s - 1), dy)
        dst = src
        if s == 1 and dy == 0:
            src = self.piece.at[:, pl.ds(0, self.la)]
        self._send(src, dst, (AP if sign > 0 else AM) + (s - 1) * 4 + dy, self._zdev(sign))

    def _ring_b(self, s, sign):
        if s > (NZ // 2 if sign > 0 else NZ // 2 - 1):
            return
        dst = self._b(0, -sign * (s - 1))
        src = self.piece.at[:, pl.ds(self.la, self.piece.shape[1] - self.la)] if s == 1 else dst
        self._send(src, dst, (BP if sign > 0 else BM) + s - 1, self._zdev(sign))

    def _spread_b(self, j):
        dst = self._b(0, OFFSETS[j])
        src = self.piece.at[:, pl.ds(self.la, self.piece.shape[1] - self.la)] if j == 0 else dst
        self._send(src, dst, YP + j, self._ydev(1))
        self._send(src, dst, YM + j, self._ydev(-1))

    def _near_b(self, j):
        o = OFFSETS[j]
        self._wait(self._b(-1, o), YP + j, self._ydev(-1))
        if j % 2 == 0:
            self._send(self._b(-1, o), self._b(-1, o), Y2 + j, self._ydev(1))
        self._wait(self._b(1, o), YM + j, self._ydev(1))
        if j % 2 == 1:
            self._send(self._b(1, o), self._b(1, o), Y2 + j, self._ydev(-1))

    def far(self, j):
        o = OFFSETS[j]
        yo = -2 if j % 2 == 0 else 2
        self._wait(self._b(yo, o), Y2 + j, self._ydev(-1 if j % 2 == 0 else 1))

    def far_at(self, j):
        if isinstance(j, int):
            return self.far(j)
        hop = (j + 1) // 2
        zz = mod(self.z + hop * (1 - 2 * lax.rem(j, 2)), NZ)
        self._wait(self.b.at[self.ys[2], zz], Y2 + j, self._ydev(1))

    def start(self):
        for dy in range(1, NY):
            self._send(self.piece.at[:, pl.ds(0, self.la)], self._a(0, 0), A0 + dy - 1, self._ydev(dy))
        for sign in (1, -1):
            self._ring_b(1, sign)
            self._ring_a(1, 0, sign)
        self._spread_b(0)

    def step(self, k):
        for s_sign in (1, -1):
            if k <= (NZ // 2 if s_sign > 0 else NZ // 2 - 1):
                self._wait(self._b(0, -s_sign * k), (BP if s_sign > 0 else BM) + k - 1, self._zdev(-s_sign))
                self._ring_b(k + 1, s_sign)
                self._spread_b(OFFSETS.index(-s_sign * k))
        for dy in range(NY):
            if k == 1:
                if dy == 0:
                    continue
                self._wait(self._a(0, dy), A0 + dy - 1, self._ydev(-dy))
                self._ring_a(1, dy, 1)
                self._ring_a(1, dy, -1)
                continue
            s = k - 1
            for sign in (1, -1):
                if self._has(sign, s, dy):
                    self._wait(
                        self._a(-sign * s, dy), (AP if sign > 0 else AM) + (s - 1) * 4 + dy, self._zdev(-sign)
                    )
                    self._ring_a(s + 1, dy, sign)
        for j, o in enumerate(OFFSETS):
            if abs(o) == k - 1:
                self._near_b(j)


def whole_kernel(
    hidden, weight, text, pooled, row_moment, col_moment, scale_ref, bias_ref,
    update_out, small_out,
    hid, wp, logit_a, logit_b, pg_a, pg_b,
    h_out, mg_out, loss_out,
    wa, wb, wc, ta, tb, tn, part, give, take, share, got, img, unit, length,
    acc, give2, take2, share2, got2,
    grad, far_p, far_m, near_p, near_m, relay_p, relay_m,
    r_far_p, r_far_m, r_near_p, r_near_m, r_relay_p, r_relay_m,
    z_give, z_take, b_give, b_take, yb_give, yb_take,
    row_give, row_take, cy_give, cy_take, cz_give, cz_take,
    s_give, s_take, l_give, l_take, sy_give, sy_take, sz_give, sz_take,
    w_s, w_r, t_s, t_r, h_s, h_r, p_s, p_r, i_s, i_r, u_s, u_r, m_s, m_r,
    g_s, g_r, z_s, z_r, b_s, b_r, yb_s, yb_r, st_s, st_r,
):
    x, c = lax.axis_index("x"), lax.axis_index("c")
    y, z = lax.axis_index("y"), lax.axis_index("z")
    me = c * NX + x
    other = 1 - c

    with jax.named_scope("prep"):
        wp[...] = jnp.zeros_like(wp)
        wp[:ED, :KD] = weight[...].astype(BF16)
        hid[...] = jnp.zeros_like(hid)
        for r in range(NX * NC):
            hid[(r % NC) * NX + r // NC, :, :KD] = hidden[:, KD * r : KD * (r + 1)]
    with jax.named_scope("barrier"):
        barrier = pltpu.get_barrier_semaphore()
        peers = [{"z": mod(z + dz, NZ)} for dz in range(1, NZ)]
        peers += [{"y": mod(y + dy, NY)} for dy in range(1, NY)]
        peers += [
            {"x": mod(x + dx, NX), "c": lax.rem(c + dc, NC)}
            for dx in range(NX) for dc in range(NC) if dx + dc > 0
        ]
        for peer in peers:
            pl.semaphore_signal(barrier, inc=1, device_id=peer, device_id_type=MESH)
        pl.semaphore_wait(barrier, len(peers))

    copies = Copies()
    w = PlaneGather(copies, wp, wa, wb, WLA, w_s, w_r, y, z)
    t = PlaneGather(copies, tn, ta, tb, TLA, t_s, t_r, y, z)

    with jax.named_scope("wstart"):
        w.start()
        row_peers = [(dx, dc) for dx in range(NX) for dc in range(NC) if dx + dc > 0]
        for i, (dx, dc) in enumerate(row_peers):
            xx, cc = mod(x + dx, NX), lax.rem(c + dc, NC)
            copies.send(hid.at[cc * NX + xx], h_out.at[me], h_s.at[i], h_r.at[i], {"x": xx, "c": cc})
        h_out[me] = hid[me]
        w.own()
        tf = text[...].astype(F32)
        tn[...] = (tf / jnp.sqrt(jnp.sum(tf * tf, axis=1, keepdims=True) + EPSILON)).astype(BF16)
    with jax.named_scope("w123"):
        w.step(1)
        w.step(2)
        w.step(3)
    with jax.named_scope("tstart"):
        t.own()
        t.start()
    with jax.named_scope("w45far"):
        w.step(4)
        w.step(5)
        for j in range(8):
            w.far(j)

    with jax.named_scope("compact"):
        r_id = lax.broadcasted_iota(jnp.int32, (4 * ED, 4 * EP), 0)
        c_id = lax.broadcasted_iota(jnp.int32, (4 * ED, 4 * EP), 1)
        pick = jnp.zeros((4 * ED, 4 * EP), F32)
        for g in range(4):
            hit = (r_id >= ED * g) & (r_id < ED * (g + 1)) & (c_id - r_id == (EP - ED) * g)
            pick = jnp.where(hit, 1.0, pick)
        pick = pick.astype(BF16)
        for g in range(8):
            yy, z0 = g // 2, 4 * (g % 2)
            wc[pl.ds(4 * ED * g, 4 * ED), 0:WLA] = jnp.dot(
                pick, wa[z0 : z0 + 4, yy].reshape(4 * EP, WLA), preferred_element_type=F32
            ).astype(BF16)
            wc[pl.ds(4 * ED * g, 4 * ED), WLA:KP] = jnp.dot(
                pick, wb[yy, z0 : z0 + 4].reshape(4 * EP, KP - WLA), preferred_element_type=F32
            ).astype(BF16)

    with jax.named_scope("hwait"):
        for i, (dx, dc) in enumerate(row_peers):
            xx, cc = mod(x - dx, NX), lax.rem(c + dc, NC)
            copies.arrived(h_out.at[cc * NX + xx], h_s.at[i], h_r.at[i], {"x": xx, "c": cc})

    def project(half):
        rows = h_out[pl.ds(half * NX, NX)].reshape(NX * TOK, KP)
        for n in range(3):
            part[pl.ds(half * NX, NX), :, 384 * n : 384 * (n + 1)] = lax.dot_general(
                rows, wc[384 * n : 384 * (n + 1), :], (((1,), (1,)), ((), ())), preferred_element_type=F32
            ).reshape(NX, TOK, 384)

    def reduce_rows(val, gv, tk, sh, gt, ss, rs):
        gv[...] = val[pl.ds(other * NX, NX)].astype(gv.dtype)
        copies.send(gv, tk, ss.at[0], rs.at[0], {"c": other})
        yield
        copies.arrived(tk, ss.at[0], rs.at[0], {"c": other})
        for dx in (2, 1, 3):
            xx = mod(x + dx, NX)
            sh[dx - 1] = (val[c * NX + xx] + tk[xx].astype(F32)).astype(BF16)
        for dx in (2, 1, 3):
            copies.send(sh.at[dx - 1], gt.at[dx - 1], ss.at[dx], rs.at[dx], {"x": mod(x + dx, NX)})
        yield
        total = val[me] + tk[x].astype(F32)
        for dx in (1, 3, 2):
            copies.arrived(gt.at[dx - 1], ss.at[dx], rs.at[dx], {"x": mod(x - dx, NX)})
        for dx in (1, 2, 3):
            total = total + gt[dx - 1].astype(F32)
        yield total

    def share_rows(buf, ss, rs, between=lambda: None):
        copies.send(buf.at[me], buf.at[me], ss.at[4], rs.at[4], {"c": other})
        for dx in (2, 1, 3):
            copies.send(buf.at[me], buf.at[me], ss.at[dx], rs.at[dx], {"x": mod(x + dx, NX)})
        between()
        for dx in (1, 3, 2):
            got_at = buf.at[c * NX + mod(x - dx, NX)]
            copies.arrived(got_at, ss.at[dx], rs.at[dx], {"x": mod(x - dx, NX)})
            copies.send(got_at, got_at, ss.at[4 + dx], rs.at[4 + dx], {"c": other})
        for dx in range(NX):
            copies.arrived(
                buf.at[other * NX + mod(x - dx, NX)], ss.at[4 + dx], rs.at[4 + dx], {"c": other}
            )

    with jax.named_scope("proj1"):
        project(other)
    with jax.named_scope("red1a"):
        red = reduce_rows(part, give, take, share, got, p_s, p_r)
        next(red)
    with jax.named_scope("proj2"):
        project(c)
    with jax.named_scope("t1"):
        t.step(1)
    with jax.named_scope("red1b"):
        next(red)
    with jax.named_scope("t2"):
        t.step(2)
    with jax.named_scope("red1c_norm"):
        mixed = pooled[...].astype(F32) + next(red)
        ln = jnp.sqrt(jnp.sum(mixed * mixed, axis=1, keepdims=True) + EPSILON)
        length[...] = jnp.broadcast_to(ln, length.shape)
        un = mixed / ln
        unit[...] = un
        img[me] = un.astype(BF16)
    with jax.named_scope("imgshare"):
        share_rows(img, i_s, i_r, lambda: t.step(3))
    with jax.named_scope("pairs"):
        scale = scale_ref[0]
        bias = bias_ref[0]
        acc[...] = jnp.zeros_like(acc)
        loss_out[...] = jnp.zeros_like(loss_out)
        tile = NX * TOK
        t_dims = (((1,), (1,)), ((), ()))

        def texts(g):
            return ta[g].reshape(NY * TOK, TLA), tb[:, g].reshape(NY * TOK, D - TLA)

        def logits_of(g, h, out):
            t_a, t_b = texts(g)
            images = img[h * NX : (h + 1) * NX].reshape(tile, D)
            out[...] = lax.dot_general(
                images[:, :TLA], t_a, t_dims, preferred_element_type=F32
            ) + lax.dot_general(images[:, TLA:], t_b, t_dims, preferred_element_type=F32)

        def elementwise(h, src, out, own):
            m = scale * src[...] + bias
            if own:
                col = lax.broadcasted_iota(jnp.int32, (tile, NY * TOK), 1)
                row = lax.broadcasted_iota(jnp.int32, (tile, NY * TOK), 0)
                same = (row - col == TOK * (me - h * NX - y)) & (col >= TOK * y) & (col < TOK * y + TOK)
                m = jnp.where(same, -m, m)
            e = jnp.exp(-jnp.abs(m))
            d = 1.0 + e
            r = 1.0 / d
            soft = jnp.maximum(m, 0.0) + (jnp.log(d) + (e - (d - 1.0)) * r)
            loss_out[...] += jnp.sum(soft.reshape(tile // 8, 8, NY * TOK), axis=0)
            sig = jnp.where(m >= 0.0, r, e * r)
            if own:
                sig = jnp.where(same, -sig, sig)
            out[...] = sig.astype(BF16)

        def to_images(g, h, src):
            t_a, t_b = texts(g)
            pg = src[...]
            rows = slice(h * NX, (h + 1) * NX)
            acc[rows, :, :TLA] += jnp.dot(pg, t_a, preferred_element_type=F32).reshape(NX, TOK, TLA)
            acc[rows, :, TLA:] += jnp.dot(pg, t_b, preferred_element_type=F32).reshape(NX, TOK, D - TLA)

        def group(j):
            hop = (j + 1) // 2
            return mod(z + hop * (1 - 2 * lax.rem(j, 2)), NZ)

        def body(j, carry):
            @pl.when(j == 3)
            def _():
                t.step(4)

            @pl.when(j == 5)
            def _():
                t.step(5)

            t.far_at(j)
            now, last = group(j), group(j - 1)
            logits_of(now, 0, logit_a)
            elementwise(1, logit_b, pg_b, False)
            to_images(last, 0, pg_a)
            logits_of(now, 1, logit_b)
            elementwise(0, logit_a, pg_a, False)
            to_images(last, 1, pg_b)
            return carry

        t.far_at(1)
        first, final = mod(z + OFFSETS[1], NZ), mod(z + OFFSETS[7], NZ)
        logits_of(first, 0, logit_a)
        logits_of(first, 1, logit_b)
        elementwise(0, logit_a, pg_a, False)
        lax.fori_loop(2, NZ, body, 0)
        t.far_at(0)
        logits_of(z, 0, logit_a)
        elementwise(1, logit_b, pg_b, False)
        to_images(final, 0, pg_a)
        logits_of(z, 1, logit_b)
        elementwise(0, logit_a, pg_a, True)
        to_images(final, 1, pg_b)
        elementwise(1, logit_b, pg_b, True)
        to_images(z, 0, pg_a)
        to_images(z, 1, pg_b)

    with jax.named_scope("red2"):
        red = reduce_rows(acc, give2, take2, share2, got2, u_s, u_r)
        next(red)
        next(red)
        ug = (scale * (1.0 / BATCH)) * next(red)
        un = unit[...]
        ln = length[:, 0:1]
        mg_out[me] = ((ug - un * jnp.sum(un * ug, axis=1, keepdims=True)) / ln).astype(BF16)
    with jax.named_scope("mgshare"):
        share_rows(mg_out, m_s, m_r)

    def exchange(give_ref, take_ref, base, value, kind):
        give_ref[...] = value
        sizes = {"row": row_peers, "y": range(1, NY), "z": range(1, NZ)}[kind]
        for i, d in enumerate(sizes):
            if kind == "row":
                device = {"x": mod(x + d[0], NX), "c": lax.rem(c + d[1], NC)}
            else:
                device = {kind: mod((y if kind == "y" else z) + d, NY if kind == "y" else NZ)}
            copies.send(give_ref, take_ref.at[i], st_s.at[base + i], st_r.at[base + i], device)

    def collected(take_ref, base, value, kind):
        sizes = {"row": row_peers, "y": range(1, NY), "z": range(1, NZ)}[kind]
        for i, d in enumerate(sizes):
            if kind == "row":
                device = {"x": mod(x - d[0], NX), "c": lax.rem(c + d[1], NC)}
            else:
                device = {kind: mod((y if kind == "y" else z) - d, NY if kind == "y" else NZ)}
            copies.arrived(take_ref.at[i], st_s.at[base + i], st_r.at[base + i], device)
            value = value + take_ref[i]
        return value

    zi = lax.broadcasted_iota(jnp.int32, (NZ, EG, 384), 0)
    ji = lax.broadcasted_iota(jnp.int32, (NZ, EG, 384), 1)
    li = lax.broadcasted_iota(jnp.int32, (NZ, EG, 384), 2)
    h_all = h_out[...].reshape(NX * NC * TOK, KP)

    def gradient_of(yy):
        choose = jnp.where((ji < ED) & (li == 32 * yy + ED * zi + ji), 1.0, 0.0)
        choose = choose.reshape(NZ * EG, 384).astype(BF16)
        mg = mg_out[:, :, pl.ds(pl.multiple_of(256 * yy, 128), 384)].reshape(NX * NC * TOK, 384)
        mg_t = lax.dot_general(choose, mg, (((1,), (1,)), ((), ())), preferred_element_type=F32).astype(BF16)
        grad[yy] = jnp.dot(mg_t, h_all, preferred_element_type=F32).reshape(NZ, EG, KP)
        b_give[:, yy] = grad[yy, :, :, GLA:].astype(BF16)

    with jax.named_scope("loss1"):
        loss_sum = jnp.sum(jnp.sum(loss_out[...], axis=0, keepdims=True), axis=1, keepdims=True)
        loss_sum = jnp.broadcast_to(loss_sum, (1, 128))
        exchange(l_give, l_take, 34, loss_sum, "row")
    with jax.named_scope("g_far"):
        half = NZ // 2
        y_far, y_up, y_down = mod(y + 2, NY), mod(y + 1, NY), mod(y - 1, NY)
        up, down = {"y": y_up}, {"y": y_down}
        gradient_of(y_far)
        far_p[...] = grad[y_far, :half, :, :GLA].astype(BF16)
        far_m[...] = grad[y_far, half:, :, :GLA].astype(BF16)
        copies.send(far_p, r_far_p, g_s.at[0], g_r.at[0], up)
        copies.send(far_m, r_far_m, g_s.at[1], g_r.at[1], down)
    with jax.named_scope("g_rest"):
        gradient_of(y_up)
        near_p[...] = grad[y_up, half:, :, :GLA].astype(BF16)
        copies.send(near_p, r_near_p, g_s.at[2], g_r.at[2], up)
        gradient_of(y_down)
        near_m[...] = grad[y_down, :half, :, :GLA].astype(BF16)
        copies.send(near_m, r_near_m, g_s.at[3], g_r.at[3], down)
        gradient_of(y)
    with jax.named_scope("g_relay"):
        copies.arrived(r_far_p, g_s.at[0], g_r.at[0], down)
        relay_p[...] = (grad[y_up, :half, :, :GLA] + r_far_p[...].astype(F32)).astype(BF16)
        copies.send(relay_p, r_relay_p, g_s.at[4], g_r.at[4], up)
        copies.arrived(r_far_m, g_s.at[1], g_r.at[1], up)
        relay_m[...] = (grad[y_down, half:, :, :GLA] + r_far_m[...].astype(F32)).astype(BF16)
        copies.send(relay_m, r_relay_m, g_s.at[5], g_r.at[5], down)
        z_order = (4, 3, 5, 2, 6, 1, 7)
        z_near = (1, 7, 2, 6, 3, 5, 4)
        for dz in z_order:
            zz = mod(z + dz, NZ)
            copies.send(b_give.at[zz], b_take.at[dz - 1], b_s.at[dz - 1], b_r.at[dz - 1], {"z": zz})
    with jax.named_scope("loss2"):
        loss_sum = collected(l_take, 34, loss_sum, "row")
        exchange(sy_give, sy_take, 24, loss_sum, "y")
    with jax.named_scope("g_ysum"):
        copies.arrived(r_near_p, g_s.at[2], g_r.at[2], down)
        copies.arrived(r_near_m, g_s.at[3], g_r.at[3], up)
        copies.arrived(r_relay_p, g_s.at[4], g_r.at[4], down)
        copies.arrived(r_relay_m, g_s.at[5], g_r.at[5], up)
        grad[y, :half, :, :GLA] += r_relay_p[...].astype(F32) + r_near_m[...].astype(F32)
        grad[y, half:, :, :GLA] += r_near_p[...].astype(F32) + r_relay_m[...].astype(F32)
        z_give[...] = grad[y, :, :, :GLA].astype(z_give.dtype)
        for dz in z_order:
            zz = mod(z + dz, NZ)
            copies.send(z_give.at[zz], z_take.at[dz - 1], z_s.at[dz - 1], z_r.at[dz - 1], {"z": zz})
    with jax.named_scope("g_bz"):
        part_b = grad[:, pl.ds(z, 1), :, GLA:].reshape(NY, EG, KP - GLA)
        for dz in z_near:
            copies.arrived(b_take.at[dz - 1], b_s.at[dz - 1], b_r.at[dz - 1], {"z": mod(z - dz, NZ)})
            part_b = part_b + b_take[dz - 1].astype(F32)
        yb_give[...] = part_b
        for dy in (2, 1, 3):
            yy = mod(y + dy, NY)
            copies.send(yb_give.at[yy], yb_take.at[dy - 1], yb_s.at[dy - 1], yb_r.at[dy - 1], {"y": yy})
    with jax.named_scope("g_by"):
        right = yb_give[y]
        for dy in (1, 3, 2):
            copies.arrived(yb_take.at[dy - 1], yb_s.at[dy - 1], yb_r.at[dy - 1], {"y": mod(y - dy, NY)})
            right = right + yb_take[dy - 1]
    with jax.named_scope("loss3"):
        loss_sum = collected(sy_take, 24, loss_sum, "y")
        exchange(sz_give, sz_take, 27, loss_sum, "z")
    with jax.named_scope("g_z"):
        left = grad[y, pl.ds(z, 1), :, :GLA].reshape(EG, GLA)
        for dz in z_near:
            copies.arrived(z_take.at[dz - 1], z_s.at[dz - 1], z_r.at[dz - 1], {"z": mod(z - dz, NZ)})
            left = left + z_take[dz - 1].astype(F32)
        grad[y, pl.ds(z, 1), :, :GLA] = left.reshape(1, EG, GLA)
        grad[y, pl.ds(z, 1), :, GLA:] = right.reshape(1, EG, KP - GLA)

    g = grad[y, pl.ds(z, 1)].reshape(EG, KP)
    e_id = lax.broadcasted_iota(jnp.int32, (EG, KP), 0)
    k_id = lax.broadcasted_iota(jnp.int32, (EG, KP), 1)
    squared = jnp.where((e_id < ED) & (k_id < KD), g * g + FLOOR_VALUE, 0.0)

    with jax.named_scope("st_row"):
        e_col = e_id[:, 0:128]
        l_col = k_id[:, 0:128]
        rows = jnp.broadcast_to(jnp.sum(squared, axis=1, keepdims=True), (EG, 128))
        exchange(row_give, row_take, 0, rows, "row")
        cols = jnp.sum(squared, axis=0, keepdims=True)
        rows = collected(row_take, 0, rows, "row")
        row_line = jnp.sum(jnp.where(e_col == l_col, rows, 0.0), axis=0, keepdims=True)[:, :ED]
        row_line = DECAY_RATE * row_moment[...].reshape(1, ED) + (1.0 - DECAY_RATE) * row_line / FF
        new_row = jnp.sum(
            jnp.where(
                e_id[:, :ED] == k_id[:, :ED], jnp.broadcast_to(row_line, (EG, ED)), 0.0
            ), axis=1, keepdims=True
        )
        new_row = jnp.where(e_col[:, 0:1] < ED, new_row, 1.0)
        ratio = jnp.sum(g * g / new_row, axis=0, keepdims=True)
    with jax.named_scope("st_col"):
        cols2 = jnp.concatenate([cols, ratio], axis=1)
        exchange(cy_give, cy_take, 7, cols2, "y")
        cols2 = collected(cy_take, 7, cols2, "y")
        exchange(cz_give, cz_take, 10, cols2, "z")
        cols2 = collected(cz_take, 10, cols2, "z")
    with jax.named_scope("st_tot"):
        cols, ratio = cols2[:, :KP], cols2[:, KP:]
        col_line = DECAY_RATE * col_moment[...].reshape(1, KD) + (1.0 - DECAY_RATE) * cols[:, :KD] / D
        raw_sum = jnp.sum(ratio[:, :KD] / col_line, axis=1, keepdims=True)
        exchange(s_give, s_take, 17, jnp.broadcast_to(raw_sum, (1, 128)), "row")
        raw = g[:ED, :KD] / jnp.sqrt(new_row[:ED] * col_line)
        loss_sum = collected(sz_take, 27, loss_sum, "z")
        small_out[...] = jnp.zeros_like(small_out)
        small_out[0:1, :KD] = col_line
        small_out[1:2, :ED] = row_line
        small_out[2:3, 0:128] = loss_sum * (1.0 / BATCH)
        both = collected(s_take, 17, jnp.broadcast_to(raw_sum, (1, 128)), "row")
    with jax.named_scope("upd"):
        rms = jnp.sqrt(both[:, 0:1] / (D * FF))
        update_out[...] = raw / jnp.maximum(1.0, rms / CLIP_LEVEL)
    with jax.named_scope("finish"):
        copies.finish()


def step_kernel(hidden, weight, text, pooled, row_moment, col_moment, scale, bias):
    vmem = pl.BlockSpec(memory_space=pltpu.VMEM)
    smem = pl.BlockSpec(memory_space=pltpu.SMEM)
    n_row = NX * NC
    dma = pltpu.SemaphoreType.DMA
    return pl.pallas_call(
        whole_kernel,
        out_shape=(
            jax.ShapeDtypeStruct((ED, KD), F32),
            jax.ShapeDtypeStruct((8, KP), F32),
        ),
        in_specs=[vmem] * 6 + [smem] * 2,
        out_specs=(vmem,) * 2,
        scratch_shapes=[
            pltpu.VMEM((n_row, TOK, KP), BF16),
            pltpu.VMEM((EP, KP), BF16),
            pltpu.VMEM((NX * TOK, NY * TOK), F32),
            pltpu.VMEM((NX * TOK, NY * TOK), F32),
            pltpu.VMEM((NX * TOK, NY * TOK), BF16),
            pltpu.VMEM((NX * TOK, NY * TOK), BF16),
            pltpu.VMEM((n_row, TOK, KP), BF16),
            pltpu.VMEM((n_row, TOK, D), BF16),
            pltpu.VMEM((8, NY * TOK), F32),
            pltpu.VMEM((NZ, NY, EP, WLA), BF16),
            pltpu.VMEM((NY, NZ, EP, KP - WLA), BF16),
            pltpu.VMEM((D, KP), BF16),
            pltpu.VMEM((NZ, NY, TOK, TLA), BF16),
            pltpu.VMEM((NY, NZ, TOK, D - TLA), BF16),
            pltpu.VMEM((TOK, D), BF16),
            pltpu.VMEM((n_row, TOK, D), F32),
            pltpu.VMEM((NX, TOK, D), F32),
            pltpu.VMEM((NX, TOK, D), F32),
            pltpu.VMEM((NX - 1, TOK, D), BF16),
            pltpu.VMEM((NX - 1, TOK, D), BF16),
            pltpu.VMEM((n_row, TOK, D), BF16),
            pltpu.VMEM((TOK, D), F32),
            pltpu.VMEM((TOK, 128), F32),
            pltpu.VMEM((n_row, TOK, D), F32),
            pltpu.VMEM((NX, TOK, D), BF16),
            pltpu.VMEM((NX, TOK, D), BF16),
            pltpu.VMEM((NX - 1, TOK, D), BF16),
            pltpu.VMEM((NX - 1, TOK, D), BF16),
            pltpu.VMEM((NY, NZ, EG, KP), F32),
            *[pltpu.VMEM((NZ // 2, EG, GLA), BF16)] * 12,
            pltpu.VMEM((NZ, EG, GLA), BF16),
            pltpu.VMEM((NZ - 1, EG, GLA), BF16),
            pltpu.VMEM((NZ, NY, EG, KP - GLA), BF16),
            pltpu.VMEM((NZ - 1, NY, EG, KP - GLA), BF16),
            pltpu.VMEM((NY, EG, KP - GLA), F32),
            pltpu.VMEM((NY - 1, EG, KP - GLA), F32),
            pltpu.VMEM((EG, 128), F32),
            pltpu.VMEM((n_row - 1, EG, 128), F32),
            pltpu.VMEM((1, 2 * KP), F32),
            pltpu.VMEM((NY - 1, 1, 2 * KP), F32),
            pltpu.VMEM((1, 2 * KP), F32),
            pltpu.VMEM((NZ - 1, 1, 2 * KP), F32),
            pltpu.VMEM((1, 128), F32),
            pltpu.VMEM((n_row - 1, 1, 128), F32),
            pltpu.VMEM((1, 128), F32),
            pltpu.VMEM((n_row - 1, 1, 128), F32),
            pltpu.VMEM((1, 128), F32),
            pltpu.VMEM((NY - 1, 1, 128), F32),
            pltpu.VMEM((1, 128), F32),
            pltpu.VMEM((NZ - 1, 1, 128), F32),
            dma((N_MSG,)), dma((N_MSG,)), dma((N_MSG,)), dma((N_MSG,)),
            dma((8,)), dma((8,)), dma((4,)), dma((4,)), dma((8,)), dma((8,)),
            dma((4,)), dma((4,)), dma((8,)), dma((8,)),
            dma((6,)), dma((6,)), dma((7,)), dma((7,)), dma((7,)), dma((7,)),
            dma((3,)), dma((3,)), dma((41,)), dma((41,)),
        ],
        compiler_params=pltpu.CompilerParams(
            collective_id=0, has_side_effects=True, vmem_limit_bytes=60 * 1024 * 1024
        ),
        name="step",
    )(hidden, weight, text, pooled, row_moment, col_moment, scale, bias)


def per_device(pooled, hidden, text, weight, row_moment, col_moment, log_scale, bias):
    update, small = step_kernel(
        hidden, weight, text, pooled, row_moment, col_moment, jnp.exp(log_scale).reshape(1), bias.reshape(1)
    )
    return (update, small[1, :ED], small[0, :KD], small[2, 0])


def solution(mesh):
    finer = Mesh(mesh.devices.reshape(NX, NC, NY, NZ), ALL)
    return jax.shard_map(
        per_device,
        mesh=finer,
        in_specs=(
            P(ALL, None), P(ALL, None), P(ALL, None), P(COL, ROW), P(COL), P(ROW), P(), P(),
        ),
        out_specs=(P(COL, ROW), P(COL), P(ROW), P()),
        check_vma=False,
    )
```

time: 276 us -> 142 us (0.51)
  blocking collectives: 118 us -> 0 us
  Pallas kernels: 115 us -> 135 us
  waiting for transfers between devices: 12.7 us -> 0 us
  starting transfers between devices: 12.3 us -> 0 us
  other arithmetic: 3.51 us -> 0 us
    psum x1 -> x0, blocking collectives: 73.3 us -> none  [per_device(): lax.psum((loss_local, jnp.sum(raw_update * raw_update)), ALL)]
    all_to_all x1 -> x0, blocking collectives: 44.6 us -> none  [sum_at_owner(): lax.all_to_all(pieces, axis, split_axis=0, concat_axis=0, tiled=True)]
    pallas_call x1, Pallas kernels: 115 us -> 135 us  [step_kernel(): pl.pallas_call(whole_kernel, out_shape=(jax.ShapeDtypeStruct((ED, KD), F3...]
    all_to_all x2 -> x0, waiting for transfers between devices: 12.7 us -> none  [of_everyone(): lax.all_to_all(copies, axis, split_axis=0, concat_axis=0, tiled=True)]
    all_to_all x2 -> x0, starting transfers between devices: 12.3 us -> none  [of_everyone(): lax.all_to_all(copies, axis, split_axis=0, concat_axis=0, tiled=True)]
    reshape x3 -> x0, local copies, waits for them, and re-layouts: 3.3 us -> none  [the longest x2 2.9 us: per_device(): hidden.reshape(TOK, NX, NC, KD).transpose(2, 1, 0, 3)]
  transfers between devices with their start and end apart: 2 -> 0, of which waited for: 2 -> 0; matrix products, arithmetic and copies ran while one was open for 0% -> 0% of each run, Pallas kernels for 0% -> 0%
where the time goes in v4:
time: 142 us
  Pallas kernels  135 us (95%)
  local copies, waits for them, and re-layouts  5.26 us (4%)
  between operations  1.97 us (1%)
    pallas_call x1, Pallas kernels, step_kernel(): pl.pallas_call(whole_kernel, out_shape=(jax.ShapeDtypeStruct((ED, KD), F3...  135 us

profile of v4, /device:TPU:1, one launch (start us, length us, event | category | flops | bytes accessed | tf_op | source)
XLA Modules:
  0.0 142.1 jit_solution(5202906839099481019)
XLA Ops:
  2.0 134.8 %step.1 = (f32[36,538]{1,0:T(8,128)}, f32[8,640]{1,0:T(8,128)}) custom-call(bf16[64,4304]{1,0:T(8,128)(2,1)} %hidden.1, f32[36,538]{1,0:T(8,128)} %weight.1, bf16[64,1152]{1,0:T(8,128)(2,1)} %text.1, bf16[64,1152]{1,0:T(8,128)(2,1)} %pooled.1, f32[36]{0:T(128)} %row_moment.1, f32[538]{0:T(1024)} %col_moment.1, f32[1]{0:T(128)} %bitcast.scale_ref, ...), custom_call_target="tpu_custom_call" | custom-call | tf_op jit(solution)/shard_map/step/pallas_call | solution.py:581
  136.8 1.3 slice_reduce_fusion
  138.1 1.2 slice.11
  139.3 1.2 slice_bitcast_fusion
  140.5 1.5 %copy.15 = f32[36,538]{1,0:T(8,128)} copy(f32[36,538]{1,0:T(8,128)} %get-tuple-element.12) | data formatting | bytes 154944

commit v5 on v4

--- a/solution.py
+++ b/solution.py
@@ -19,7 +19,8 @@
 WLA = 256
 TLA = 512
 EG = 40
-GLA = 512
+GLA = 384
+GLB = 512
 ROW = ("x", "c")
 COL = ("y", "z")
 ALL = ("x", "c", "y", "z")
@@ -39,51 +40,52 @@
     return lax.rem(value + 2 * size, size)
 
 
-class Copies:
-    def __init__(self):
-        self.sent = []
-
-    def send(self, src, dst, ssem, rsem, device):
-        pltpu.make_async_remote_copy(src, dst, ssem, rsem, device_id=device, device_id_type=MESH).start()
-        self.sent.append((src, dst, ssem, rsem, device))
-
-    def arrived(self, dst, ssem, rsem, device):
-        pltpu.make_async_remote_copy(
-            dst, dst, ssem, rsem, device_id=device, device_id_type=MESH
-        ).wait_recv()
-
-    def finish(self):
-        for src, dst, ssem, rsem, device in self.sent:
-            pltpu.make_async_remote_copy(
-                src, dst, ssem, rsem, device_id=device, device_id_type=MESH
-            ).wait_send()
+def send(src, dst, ssem, rsem, device):
+    pltpu.make_async_remote_copy(src, dst, ssem, rsem, device_id=device, device_id_type=MESH).start()
+
+
+def arrived(dst, ssem, rsem, device):
+    pltpu.make_async_remote_copy(dst, dst, ssem, rsem, device_id=device, device_id_type=MESH).wait_recv()
+
+
+def all_sent(ref, ssem, rsem, device):
+    pltpu.make_async_remote_copy(ref, ref, ssem, rsem, device_id=device, device_id_type=MESH).wait_send()
 
 
 A0, AP, AM, BP, BM, YP, YM, Y2 = 0, 4, 20, 36, 40, 44, 52, 60
 N_MSG = 68
+EXCHANGES = (0, 7, 10, 17, 24, 27, 34)
+A_MSG = range(A0, BP)
 OFFSETS = [0, -1, 1, -2, 2, -3, 3, -4]
 
 
 class PlaneGather:
-    def __init__(self, copies, piece, a, b, la, ssem, rsem, y, z):
-        self.copies, self.piece, self.a, self.b, self.la = copies, piece, a, b, la
+    def __init__(self, piece, a, b, la, rows, ssem, rsem, y, z):
+        self.piece, self.a, self.b, self.la, self.rows = piece, a, b, la, pl.ds(0, rows)
+        self.piece_a = piece.at[self.rows, pl.ds(0, la)]
+        self.piece_b = piece.at[self.rows, pl.ds(la, piece.shape[1] - la)]
         self.ssem, self.rsem, self.y, self.z = ssem, rsem, y, z
         self.ys = {o: mod(y + o, NY) for o in range(1 - NY, NY)}
         self.zs = {o: mod(z + o, NZ) for o in range(-(NZ // 2), NZ // 2 + 1)}
-        self.sems = [(ssem.at[i], rsem.at[i]) for i in range(N_MSG)]
-        self.a_at = {(o, dy): a.at[self.zs[o], self.ys[-dy]] for o in self.zs for dy in range(NY)}
-        self.b_at = {(yo, o): b.at[self.ys[yo], self.zs[o]] for o in self.zs for yo in range(-2, 3)}
+        self.sems = [(ssem.at[0 if i in A_MSG else 1], rsem.at[i]) for i in range(N_MSG)]
+        self.a_at = {(o, dy): a.at[self.zs[o] * NY + self.ys[-dy], self.rows] for o in self.zs for dy in range(NY)}
+        self.b_at = {(yo, o): b.at[self.ys[yo] * NZ + self.zs[o], self.rows] for o in self.zs for yo in range(-2, 3)}
 
     def _send(self, src, dst, i, device):
-        self.copies.send(src, dst, *self.sems[i], device)
+        send(src, dst, *self.sems[i], device)
 
     def _wait(self, dst, i, device):
-        sems = self.sems[i] if isinstance(i, int) else (self.ssem.at[i], self.rsem.at[i])
-        self.copies.arrived(dst, *sems, device)
+        sems = self.sems[i] if isinstance(i, int) else (self.ssem.at[1], self.rsem.at[i])
+        arrived(dst, *sems, device)
 
     def own(self):
-        self.a[self.z, self.y] = self.piece[:, : self.la]
-        self.b[self.y, self.z] = self.piece[:, self.la :]
+        self.a[self.z * NY + self.y] = self.piece[:, : self.la]
+        self.b[self.y * NZ + self.z] = self.piece[:, self.la :]
+
+    def finish(self):
+        n = pl.ds(0, NY * NZ - 1)
+        all_sent(self.a.at[n, self.rows], *self.sems[A0], self._zdev(1))
+        all_sent(self.b.at[n, self.rows], *self.sems[BP], self._zdev(1))
 
     def _a(self, zo, dy):
         return self.a_at[zo, dy]
@@ -109,19 +111,19 @@
         src = self._a(-sign * (s - 1), dy)
         dst = src
         if s == 1 and dy == 0:
-            src = self.piece.at[:, pl.ds(0, self.la)]
+            src = self.piece_a
         self._send(src, dst, (AP if sign > 0 else AM) + (s - 1) * 4 + dy, self._zdev(sign))
 
     def _ring_b(self, s, sign):
         if s > (NZ // 2 if sign > 0 else NZ // 2 - 1):
             return
         dst = self._b(0, -sign * (s - 1))
-        src = self.piece.at[:, pl.ds(self.la, self.piece.shape[1] - self.la)] if s == 1 else dst
+        src = self.piece_b if s == 1 else dst
         self._send(src, dst, (BP if sign > 0 else BM) + s - 1, self._zdev(sign))
 
     def _spread_b(self, j):
         dst = self._b(0, OFFSETS[j])
-        src = self.piece.at[:, pl.ds(self.la, self.piece.shape[1] - self.la)] if j == 0 else dst
+        src = self.piece_b if j == 0 else dst
         self._send(src, dst, YP + j, self._ydev(1))
         self._send(src, dst, YM + j, self._ydev(-1))
 
@@ -144,11 +146,11 @@
             return self.far(j)
         hop = (j + 1) // 2
         zz = mod(self.z + hop * (1 - 2 * lax.rem(j, 2)), NZ)
-        self._wait(self.b.at[self.ys[2], zz], Y2 + j, self._ydev(1))
+        self._wait(self.b.at[self.ys[2] * NZ + zz, self.rows], Y2 + j, self._ydev(1))
 
     def start(self):
         for dy in range(1, NY):
-            self._send(self.piece.at[:, pl.ds(0, self.la)], self._a(0, 0), A0 + dy - 1, self._ydev(dy))
+            self._send(self.piece_a, self._a(0, 0), A0 + dy - 1, self._ydev(dy))
         for sign in (1, -1):
             self._ring_b(1, sign)
             self._ring_a(1, 0, sign)
@@ -189,7 +191,7 @@
     acc, give2, take2, share2, got2,
     grad, far_p, far_m, near_p, near_m, relay_p, relay_m,
     r_far_p, r_far_m, r_near_p, r_near_m, r_relay_p, r_relay_m,
-    z_give, z_take, b_give, b_take, yb_give, yb_take,
+    z_give, z_take, tail, b_give, b_take, yb_give, yb_take,
     row_give, row_take, cy_give, cy_take, cz_give, cz_take,
     s_give, s_take, l_give, l_take, sy_give, sy_take, sz_give, sz_take,
     w_s, w_r, t_s, t_r, h_s, h_r, p_s, p_r, i_s, i_r, u_s, u_r, m_s, m_r,
@@ -204,6 +206,8 @@
         wp[...] = jnp.zeros_like(wp)
         wp[:ED, :KD] = weight[...].astype(BF16)
         hid[...] = jnp.zeros_like(hid)
+        wa[...] = jnp.zeros_like(wa)
+        wb[...] = jnp.zeros_like(wb)
         for r in range(NX * NC):
             hid[(r % NC) * NX + r // NC, :, :KD] = hidden[:, KD * r : KD * (r + 1)]
     with jax.named_scope("barrier"):
@@ -218,16 +222,15 @@
             pl.semaphore_signal(barrier, inc=1, device_id=peer, device_id_type=MESH)
         pl.semaphore_wait(barrier, len(peers))
 
-    copies = Copies()
-    w = PlaneGather(copies, wp, wa, wb, WLA, w_s, w_r, y, z)
-    t = PlaneGather(copies, tn, ta, tb, TLA, t_s, t_r, y, z)
+    w = PlaneGather(wp, wa, wb, WLA, EG, w_s, w_r, y, z)
+    t = PlaneGather(tn, ta, tb, TLA, TOK, t_s, t_r, y, z)
 
     with jax.named_scope("wstart"):
         w.start()
         row_peers = [(dx, dc) for dx in range(NX) for dc in range(NC) if dx + dc > 0]
         for i, (dx, dc) in enumerate(row_peers):
             xx, cc = mod(x + dx, NX), lax.rem(c + dc, NC)
-            copies.send(hid.at[cc * NX + xx], h_out.at[me], h_s.at[i], h_r.at[i], {"x": xx, "c": cc})
+            send(hid.at[cc * NX + xx], h_out.at[me], h_s.at[0], h_r.at[i], {"x": xx, "c": cc})
         h_out[me] = hid[me]
         w.own()
         tf = text[...].astype(F32)
@@ -256,16 +259,16 @@
         for g in range(8):
             yy, z0 = g // 2, 4 * (g % 2)
             wc[pl.ds(4 * ED * g, 4 * ED), 0:WLA] = jnp.dot(
-                pick, wa[z0 : z0 + 4, yy].reshape(4 * EP, WLA), preferred_element_type=F32
+                pick, jnp.concatenate([wa[(z0 + k) * NY + yy] for k in range(4)], axis=0), preferred_element_type=F32
             ).astype(BF16)
             wc[pl.ds(4 * ED * g, 4 * ED), WLA:KP] = jnp.dot(
-                pick, wb[yy, z0 : z0 + 4].reshape(4 * EP, KP - WLA), preferred_element_type=F32
+                pick, wb[yy * NZ + z0 : yy * NZ + z0 + 4].reshape(4 * EP, KP - WLA), preferred_element_type=F32
             ).astype(BF16)
 
     with jax.named_scope("hwait"):
         for i, (dx, dc) in enumerate(row_peers):
             xx, cc = mod(x - dx, NX), lax.rem(c + dc, NC)
-            copies.arrived(h_out.at[cc * NX + xx], h_s.at[i], h_r.at[i], {"x": xx, "c": cc})
+            arrived(h_out.at[cc * NX + xx], h_s.at[0], h_r.at[i], {"x": xx, "c": cc})
 
     def project(half):
         rows = h_out[pl.ds(half * NX, NX)].reshape(NX * TOK, KP)
@@ -275,36 +278,39 @@
             ).reshape(NX, TOK, 384)
 
     def reduce_rows(val, gv, tk, sh, gt, ss, rs):
-        gv[...] = val[pl.ds(other * NX, NX)].astype(gv.dtype)
-        copies.send(gv, tk, ss.at[0], rs.at[0], {"c": other})
+        for dx in (2, 1, 3, 0):
+            xx = mod(x + dx, NX)
+            gv[xx] = val[other * NX + xx].astype(gv.dtype)
+            send(gv.at[xx], tk.at[xx], ss.at[0], rs.at[dx], {"c": other})
         yield
-        copies.arrived(tk, ss.at[0], rs.at[0], {"c": other})
         for dx in (2, 1, 3):
             xx = mod(x + dx, NX)
+            arrived(tk.at[xx], ss.at[0], rs.at[dx], {"c": other})
             sh[dx - 1] = (val[c * NX + xx] + tk[xx].astype(F32)).astype(BF16)
-        for dx in (2, 1, 3):
-            copies.send(sh.at[dx - 1], gt.at[dx - 1], ss.at[dx], rs.at[dx], {"x": mod(x + dx, NX)})
+            send(sh.at[dx - 1], gt.at[dx - 1], ss.at[1], rs.at[NX - 1 + dx], {"x": xx})
         yield
+        arrived(tk.at[x], ss.at[0], rs.at[0], {"c": other})
         total = val[me] + tk[x].astype(F32)
         for dx in (1, 3, 2):
-            copies.arrived(gt.at[dx - 1], ss.at[dx], rs.at[dx], {"x": mod(x - dx, NX)})
+            arrived(gt.at[dx - 1], ss.at[1], rs.at[NX - 1 + dx], {"x": mod(x - dx, NX)})
         for dx in (1, 2, 3):
             total = total + gt[dx - 1].astype(F32)
+        all_sent(gv, ss.at[0], rs.at[0], {"c": other})
+        all_sent(sh, ss.at[1], rs.at[NX], {"x": mod(x + 1, NX)})
         yield total
 
     def share_rows(buf, ss, rs, between=lambda: None):
-        copies.send(buf.at[me], buf.at[me], ss.at[4], rs.at[4], {"c": other})
         for dx in (2, 1, 3):
-            copies.send(buf.at[me], buf.at[me], ss.at[dx], rs.at[dx], {"x": mod(x + dx, NX)})
+            send(buf.at[me], buf.at[me], ss.at[0], rs.at[dx], {"x": mod(x + dx, NX)})
+        send(buf.at[me], buf.at[me], ss.at[0], rs.at[4], {"c": other})
         between()
         for dx in (1, 3, 2):
             got_at = buf.at[c * NX + mod(x - dx, NX)]
-            copies.arrived(got_at, ss.at[dx], rs.at[dx], {"x": mod(x - dx, NX)})
-            copies.send(got_at, got_at, ss.at[4 + dx], rs.at[4 + dx], {"c": other})
-        for dx in range(NX):
-            copies.arrived(
-                buf.at[other * NX + mod(x - dx, NX)], ss.at[4 + dx], rs.at[4 + dx], {"c": other}
-            )
+            arrived(got_at, ss.at[0], rs.at[dx], {"x": mod(x - dx, NX)})
+            send(got_at, got_at, ss.at[0], rs.at[4 + dx], {"c": other})
+        for dx in (0, 1, 3, 2):
+            arrived(buf.at[other * NX + mod(x - dx, NX)], ss.at[0], rs.at[4 + dx], {"c": other})
+        all_sent(buf.at[pl.ds(0, 7)], ss.at[0], rs.at[1], {"c": other})
 
     with jax.named_scope("proj1"):
         project(other)
@@ -336,22 +342,25 @@
         tile = NX * TOK
         t_dims = (((1,), (1,)), ((), ()))
 
+        halves = (other, c)
+
         def texts(g):
-            return ta[g].reshape(NY * TOK, TLA), tb[:, g].reshape(NY * TOK, D - TLA)
+            t_b = jnp.concatenate([tb[yy * NZ + g] for yy in range(NY)], axis=0)
+            return ta[pl.ds(g * NY, NY)].reshape(NY * TOK, TLA), t_b
 
         def logits_of(g, h, out):
             t_a, t_b = texts(g)
-            images = img[h * NX : (h + 1) * NX].reshape(tile, D)
+            images = img[pl.ds(halves[h] * NX, NX)].reshape(tile, D)
             out[...] = lax.dot_general(
                 images[:, :TLA], t_a, t_dims, preferred_element_type=F32
             ) + lax.dot_general(images[:, TLA:], t_b, t_dims, preferred_element_type=F32)
 
-        def elementwise(h, src, out, own):
+        def elementwise(src, out, own):
             m = scale * src[...] + bias
             if own:
                 col = lax.broadcasted_iota(jnp.int32, (tile, NY * TOK), 1)
                 row = lax.broadcasted_iota(jnp.int32, (tile, NY * TOK), 0)
-                same = (row - col == TOK * (me - h * NX - y)) & (col >= TOK * y) & (col < TOK * y + TOK)
+                same = (row - col == TOK * (x - y)) & (col >= TOK * y) & (col < TOK * y + TOK)
                 m = jnp.where(same, -m, m)
             e = jnp.exp(-jnp.abs(m))
             d = 1.0 + e
@@ -366,7 +375,7 @@
         def to_images(g, h, src):
             t_a, t_b = texts(g)
             pg = src[...]
-            rows = slice(h * NX, (h + 1) * NX)
+            rows = pl.ds(halves[h] * NX, NX)
             acc[rows, :, :TLA] += jnp.dot(pg, t_a, preferred_element_type=F32).reshape(NX, TOK, TLA)
             acc[rows, :, TLA:] += jnp.dot(pg, t_b, preferred_element_type=F32).reshape(NX, TOK, D - TLA)
 
@@ -386,10 +395,10 @@
             t.far_at(j)
             now, last = group(j), group(j - 1)
             logits_of(now, 0, logit_a)
-            elementwise(1, logit_b, pg_b, False)
+            elementwise(logit_b, pg_b, False)
             to_images(last, 0, pg_a)
             logits_of(now, 1, logit_b)
-            elementwise(0, logit_a, pg_a, False)
+            elementwise(logit_a, pg_a, False)
             to_images(last, 1, pg_b)
             return carry
 
@@ -397,22 +406,21 @@
         first, final = mod(z + OFFSETS[1], NZ), mod(z + OFFSETS[7], NZ)
         logits_of(first, 0, logit_a)
         logits_of(first, 1, logit_b)
-        elementwise(0, logit_a, pg_a, False)
+        elementwise(logit_a, pg_a, False)
         lax.fori_loop(2, NZ, body, 0)
         t.far_at(0)
         logits_of(z, 0, logit_a)
-        elementwise(1, logit_b, pg_b, False)
+        elementwise(logit_b, pg_b, False)
         to_images(final, 0, pg_a)
         logits_of(z, 1, logit_b)
-        elementwise(0, logit_a, pg_a, True)
+        elementwise(logit_a, pg_a, False)
         to_images(final, 1, pg_b)
-        elementwise(1, logit_b, pg_b, True)
         to_images(z, 0, pg_a)
-        to_images(z, 1, pg_b)
-
     with jax.named_scope("red2"):
         red = reduce_rows(acc, give2, take2, share2, got2, u_s, u_r)
         next(red)
+        elementwise(logit_b, pg_b, True)
+        to_images(z, 1, pg_b)
         next(red)
         ug = (scale * (1.0 / BATCH)) * next(red)
         un = unit[...]
@@ -423,23 +431,26 @@
 
     def exchange(give_ref, take_ref, base, value, kind):
         give_ref[...] = value
+        slot = EXCHANGES.index(base)
         sizes = {"row": row_peers, "y": range(1, NY), "z": range(1, NZ)}[kind]
         for i, d in enumerate(sizes):
             if kind == "row":
                 device = {"x": mod(x + d[0], NX), "c": lax.rem(c + d[1], NC)}
             else:
                 device = {kind: mod((y if kind == "y" else z) + d, NY if kind == "y" else NZ)}
-            copies.send(give_ref, take_ref.at[i], st_s.at[base + i], st_r.at[base + i], device)
+            send(give_ref, take_ref.at[i], st_s.at[slot], st_r.at[base + i], device)
 
     def collected(take_ref, base, value, kind):
+        slot = EXCHANGES.index(base)
         sizes = {"row": row_peers, "y": range(1, NY), "z": range(1, NZ)}[kind]
         for i, d in enumerate(sizes):
             if kind == "row":
                 device = {"x": mod(x - d[0], NX), "c": lax.rem(c + d[1], NC)}
             else:
                 device = {kind: mod((y if kind == "y" else z) - d, NY if kind == "y" else NZ)}
-            copies.arrived(take_ref.at[i], st_s.at[base + i], st_r.at[base + i], device)
+            arrived(take_ref.at[i], st_s.at[slot], st_r.at[base + i], device)
             value = value + take_ref[i]
+        all_sent(take_ref, st_s.at[slot], st_r.at[base], device)
         return value
 
     zi = lax.broadcasted_iota(jnp.int32, (NZ, EG, 384), 0)
@@ -447,13 +458,15 @@
     li = lax.broadcasted_iota(jnp.int32, (NZ, EG, 384), 2)
     h_all = h_out[...].reshape(NX * NC * TOK, KP)
 
-    def gradient_of(yy):
+    def gradient_of(dy):
+        yy = mod(y + dy, NY)
         choose = jnp.where((ji < ED) & (li == 32 * yy + ED * zi + ji), 1.0, 0.0)
         choose = choose.reshape(NZ * EG, 384).astype(BF16)
         mg = mg_out[:, :, pl.ds(pl.multiple_of(256 * yy, 128), 384)].reshape(NX * NC * TOK, 384)
         mg_t = lax.dot_general(choose, mg, (((1,), (1,)), ((), ())), preferred_element_type=F32).astype(BF16)
         grad[yy] = jnp.dot(mg_t, h_all, preferred_element_type=F32).reshape(NZ, EG, KP)
-        b_give[:, yy] = grad[yy, :, :, GLA:].astype(BF16)
+        b_give[:, dy] = grad[yy, :, :, GLA:GLB].astype(BF16)
+        tail[:, :, 32 * dy : 32 * dy + 32] = grad[yy, :, :, GLB : GLB + 32]
 
     with jax.named_scope("loss1"):
         loss_sum = jnp.sum(jnp.sum(loss_out[...], axis=0, keepdims=True), axis=1, keepdims=True)
@@ -463,69 +476,78 @@
         half = NZ // 2
         y_far, y_up, y_down = mod(y + 2, NY), mod(y + 1, NY), mod(y - 1, NY)
         up, down = {"y": y_up}, {"y": y_down}
-        gradient_of(y_far)
+        gradient_of(2)
         far_p[...] = grad[y_far, :half, :, :GLA].astype(BF16)
         far_m[...] = grad[y_far, half:, :, :GLA].astype(BF16)
-        copies.send(far_p, r_far_p, g_s.at[0], g_r.at[0], up)
-        copies.send(far_m, r_far_m, g_s.at[1], g_r.at[1], down)
+        send(far_p, r_far_p, g_s.at[0], g_r.at[0], up)
+        send(far_m, r_far_m, g_s.at[1], g_r.at[1], down)
     with jax.named_scope("g_rest"):
-        gradient_of(y_up)
+        gradient_of(1)
         near_p[...] = grad[y_up, half:, :, :GLA].astype(BF16)
-        copies.send(near_p, r_near_p, g_s.at[2], g_r.at[2], up)
-        gradient_of(y_down)
+        send(near_p, r_near_p, g_s.at[2], g_r.at[2], up)
+        gradient_of(3)
         near_m[...] = grad[y_down, :half, :, :GLA].astype(BF16)
-        copies.send(near_m, r_near_m, g_s.at[3], g_r.at[3], down)
-        gradient_of(y)
-    with jax.named_scope("g_relay"):
-        copies.arrived(r_far_p, g_s.at[0], g_r.at[0], down)
-        relay_p[...] = (grad[y_up, :half, :, :GLA] + r_far_p[...].astype(F32)).astype(BF16)
-        copies.send(relay_p, r_relay_p, g_s.at[4], g_r.at[4], up)
-        copies.arrived(r_far_m, g_s.at[1], g_r.at[1], up)
-        relay_m[...] = (grad[y_down, half:, :, :GLA] + r_far_m[...].astype(F32)).astype(BF16)
-        copies.send(relay_m, r_relay_m, g_s.at[5], g_r.at[5], down)
+        send(near_m, r_near_m, g_s.at[3], g_r.at[3], down)
+        gradient_of(0)
+        b_give[:, NY] = tail[...].astype(BF16)
         z_order = (4, 3, 5, 2, 6, 1, 7)
         z_near = (1, 7, 2, 6, 3, 5, 4)
         for dz in z_order:
             zz = mod(z + dz, NZ)
-            copies.send(b_give.at[zz], b_take.at[dz - 1], b_s.at[dz - 1], b_r.at[dz - 1], {"z": zz})
+            send(b_give.at[zz], b_take.at[dz - 1], b_s.at[0], b_r.at[dz - 1], {"z": zz})
+    with jax.named_scope("g_relay"):
+        arrived(r_far_p, g_s.at[0], g_r.at[0], down)
+        relay_p[...] = (grad[y_up, :half, :, :GLA] + r_far_p[...].astype(F32)).astype(BF16)
+        send(relay_p, r_relay_p, g_s.at[4], g_r.at[4], up)
+        arrived(r_far_m, g_s.at[1], g_r.at[1], up)
+        relay_m[...] = (grad[y_down, half:, :, :GLA] + r_far_m[...].astype(F32)).astype(BF16)
+        send(relay_m, r_relay_m, g_s.at[5], g_r.at[5], down)
     with jax.named_scope("loss2"):
         loss_sum = collected(l_take, 34, loss_sum, "row")
         exchange(sy_give, sy_take, 24, loss_sum, "y")
     with jax.named_scope("g_ysum"):
-        copies.arrived(r_near_p, g_s.at[2], g_r.at[2], down)
-        copies.arrived(r_near_m, g_s.at[3], g_r.at[3], up)
-        copies.arrived(r_relay_p, g_s.at[4], g_r.at[4], down)
-        copies.arrived(r_relay_m, g_s.at[5], g_r.at[5], up)
+        arrived(r_near_p, g_s.at[2], g_r.at[2], down)
+        arrived(r_near_m, g_s.at[3], g_r.at[3], up)
+        arrived(r_relay_p, g_s.at[4], g_r.at[4], down)
+        arrived(r_relay_m, g_s.at[5], g_r.at[5], up)
         grad[y, :half, :, :GLA] += r_relay_p[...].astype(F32) + r_near_m[...].astype(F32)
         grad[y, half:, :, :GLA] += r_near_p[...].astype(F32) + r_relay_m[...].astype(F32)
         z_give[...] = grad[y, :, :, :GLA].astype(z_give.dtype)
         for dz in z_order:
             zz = mod(z + dz, NZ)
-            copies.send(z_give.at[zz], z_take.at[dz - 1], z_s.at[dz - 1], z_r.at[dz - 1], {"z": zz})
+            send(z_give.at[zz], z_take.at[dz - 1], z_s.at[0], z_r.at[dz - 1], {"z": zz})
     with jax.named_scope("g_bz"):
-        part_b = grad[:, pl.ds(z, 1), :, GLA:].reshape(NY, EG, KP - GLA)
+        for dy in range(NY):
+            yb_give[dy, 0] = grad[mod(y + dy, NY), pl.ds(z, 1), :, GLA:GLB].reshape(EG, GLB - GLA)
+        last = tail[pl.ds(z, 1)].reshape(EG, 128)
         for dz in z_near:
-            copies.arrived(b_take.at[dz - 1], b_s.at[dz - 1], b_r.at[dz - 1], {"z": mod(z - dz, NZ)})
-            part_b = part_b + b_take[dz - 1].astype(F32)
-        yb_give[...] = part_b
+            arrived(b_take.at[dz - 1], b_s.at[0], b_r.at[dz - 1], {"z": mod(z - dz, NZ)})
+        for dz in z_near:
+            yb_give[:, 0] += b_take[dz - 1, :NY].astype(F32)
+            last = last + b_take[dz - 1, NY].astype(F32)
+        for dy in range(NY):
+            yb_give[dy, 1] = last
         for dy in (2, 1, 3):
             yy = mod(y + dy, NY)
-            copies.send(yb_give.at[yy], yb_take.at[dy - 1], yb_s.at[dy - 1], yb_r.at[dy - 1], {"y": yy})
+            send(yb_give.at[dy], yb_take.at[dy - 1], yb_s.at[0], yb_r.at[dy - 1], {"y": yy})
     with jax.named_scope("g_by"):
-        right = yb_give[y]
+        right = yb_give[0, 0]
+        last = last[:, 0:32]
         for dy in (1, 3, 2):
-            copies.arrived(yb_take.at[dy - 1], yb_s.at[dy - 1], yb_r.at[dy - 1], {"y": mod(y - dy, NY)})
-            right = right + yb_take[dy - 1]
+            arrived(yb_take.at[dy - 1], yb_s.at[0], yb_r.at[dy - 1], {"y": mod(y - dy, NY)})
+            right = right + yb_take[dy - 1, 0]
+            last = last + yb_take[dy - 1, 1][:, 32 * dy : 32 * dy + 32]
     with jax.named_scope("loss3"):
         loss_sum = collected(sy_take, 24, loss_sum, "y")
         exchange(sz_give, sz_take, 27, loss_sum, "z")
     with jax.named_scope("g_z"):
         left = grad[y, pl.ds(z, 1), :, :GLA].reshape(EG, GLA)
         for dz in z_near:
-            copies.arrived(z_take.at[dz - 1], z_s.at[dz - 1], z_r.at[dz - 1], {"z": mod(z - dz, NZ)})
+            arrived(z_take.at[dz - 1], z_s.at[0], z_r.at[dz - 1], {"z": mod(z - dz, NZ)})
             left = left + z_take[dz - 1].astype(F32)
         grad[y, pl.ds(z, 1), :, :GLA] = left.reshape(1, EG, GLA)
-        grad[y, pl.ds(z, 1), :, GLA:] = right.reshape(1, EG, KP - GLA)
+        grad[y, pl.ds(z, 1), :, GLA:GLB] = right.reshape(1, EG, GLB - GLA)
+        grad[y, pl.ds(z, 1), :, GLB : GLB + 32] = last.reshape(1, EG, 32)
 
     g = grad[y, pl.ds(z, 1)].reshape(EG, KP)
     e_id = lax.broadcasted_iota(jnp.int32, (EG, KP), 0)
@@ -570,7 +592,16 @@
         rms = jnp.sqrt(both[:, 0:1] / (D * FF))
         update_out[...] = raw / jnp.maximum(1.0, rms / CLIP_LEVEL)
     with jax.named_scope("finish"):
-        copies.finish()
+        w.finish()
+        t.finish()
+        all_sent(h_out.at[pl.ds(0, 7)], h_s.at[0], h_r.at[0], {"c": other})
+        for k, (ref, device) in enumerate(
+            ((far_p, up), (far_m, down), (near_p, up), (near_m, down), (relay_p, up), (relay_m, down))
+        ):
+            all_sent(ref, g_s.at[k], g_r.at[k], device)
+        all_sent(z_take, z_s.at[0], z_r.at[0], {"z": mod(z + 1, NZ)})
+        all_sent(b_take, b_s.at[0], b_r.at[0], {"z": mod(z + 1, NZ)})
+        all_sent(yb_take, yb_s.at[0], yb_r.at[0], up)
 
 
 def step_kernel(hidden, weight, text, pooled, row_moment, col_moment, scale, bias):
@@ -596,11 +627,11 @@
             pltpu.VMEM((n_row, TOK, KP), BF16),
             pltpu.VMEM((n_row, TOK, D), BF16),
             pltpu.VMEM((8, NY * TOK), F32),
-            pltpu.VMEM((NZ, NY, EP, WLA), BF16),
-            pltpu.VMEM((NY, NZ, EP, KP - WLA), BF16),
+            pltpu.VMEM((NZ * NY, EP, WLA), BF16),
+            pltpu.VMEM((NY * NZ, EP, KP - WLA), BF16),
             pltpu.VMEM((D, KP), BF16),
-            pltpu.VMEM((NZ, NY, TOK, TLA), BF16),
-            pltpu.VMEM((NY, NZ, TOK, D - TLA), BF16),
+            pltpu.VMEM((NZ * NY, TOK, TLA), BF16),
+            pltpu.VMEM((NY * NZ, TOK, D - TLA), BF16),
             pltpu.VMEM((TOK, D), BF16),
             pltpu.VMEM((n_row, TOK, D), F32),
             pltpu.VMEM((NX, TOK, D), F32),
@@ -619,10 +650,11 @@
             *[pltpu.VMEM((NZ // 2, EG, GLA), BF16)] * 12,
             pltpu.VMEM((NZ, EG, GLA), BF16),
             pltpu.VMEM((NZ - 1, EG, GLA), BF16),
-            pltpu.VMEM((NZ, NY, EG, KP - GLA), BF16),
-            pltpu.VMEM((NZ - 1, NY, EG, KP - GLA), BF16),
-            pltpu.VMEM((NY, EG, KP - GLA), F32),
-            pltpu.VMEM((NY - 1, EG, KP - GLA), F32),
+            pltpu.VMEM((NZ, EG, 128), F32),
+            pltpu.VMEM((NZ, NY + 1, EG, 128), BF16),
+            pltpu.VMEM((NZ - 1, NY + 1, EG, 128), BF16),
+            pltpu.VMEM((NY, 2, EG, 128), F32),
+            pltpu.VMEM((NY - 1, 2, EG, 128), F32),
             pltpu.VMEM((EG, 128), F32),
             pltpu.VMEM((n_row - 1, EG, 128), F32),
             pltpu.VMEM((1, 2 * KP), F32),
@@ -637,11 +669,11 @@
             pltpu.VMEM((NY - 1, 1, 128), F32),
             pltpu.VMEM((1, 128), F32),
             pltpu.VMEM((NZ - 1, 1, 128), F32),
-            dma((N_MSG,)), dma((N_MSG,)), dma((N_MSG,)), dma((N_MSG,)),
-            dma((8,)), dma((8,)), dma((4,)), dma((4,)), dma((8,)), dma((8,)),
-            dma((4,)), dma((4,)), dma((8,)), dma((8,)),
-            dma((6,)), dma((6,)), dma((7,)), dma((7,)), dma((7,)), dma((7,)),
-            dma((3,)), dma((3,)), dma((41,)), dma((41,)),
+            dma((2,)), dma((N_MSG,)), dma((2,)), dma((N_MSG,)),
+            dma((1,)), dma((7,)), dma((2,)), dma((7,)), dma((1,)), dma((8,)),
+            dma((2,)), dma((7,)), dma((1,)), dma((8,)),
+            dma((6,)), dma((6,)), dma((1,)), dma((7,)), dma((1,)), dma((7,)),
+            dma((1,)), dma((3,)), dma((7,)), dma((41,)),
         ],
         compiler_params=pltpu.CompilerParams(
             collective_id=0, has_side_effects=True, vmem_limit_bytes=60 * 1024 * 1024
@@ -650,11 +682,31 @@
     )(hidden, weight, text, pooled, row_moment, col_moment, scale, bias)
 
 
+def out_kernel(update_in, small, update, new_row, new_col, loss):
+    update[...] = update_in[...]
+    new_row[...] = small[1:2, :ED].reshape(ED)
+    new_col[...] = small[0:1, :KD].reshape(KD)
+    loss[0] = small[2, 0]
+
+
 def per_device(pooled, hidden, text, weight, row_moment, col_moment, log_scale, bias):
     update, small = step_kernel(
         hidden, weight, text, pooled, row_moment, col_moment, jnp.exp(log_scale).reshape(1), bias.reshape(1)
     )
-    return (update, small[1, :ED], small[0, :KD], small[2, 0])
+    vmem = pl.BlockSpec(memory_space=pltpu.VMEM)
+    update, new_row, new_col, loss = pl.pallas_call(
+        out_kernel,
+        out_shape=(
+            jax.ShapeDtypeStruct((ED, KD), F32),
+            jax.ShapeDtypeStruct((ED,), F32),
+            jax.ShapeDtypeStruct((KD,), F32),
+            jax.ShapeDtypeStruct((1,), F32),
+        ),
+        in_specs=[vmem] * 2,
+        out_specs=(vmem, vmem, vmem, pl.BlockSpec(memory_space=pltpu.SMEM)),
+        name="out",
+    )(update, small)
+    return (update, new_row, new_col, loss.reshape(()))
 
 
 def solution(mesh):

time: 142 us -> 133 us (0.937)
  local copies, waits for them, and re-layouts: 5.26 us -> 0 us
  Pallas kernels: 135 us -> 131 us
    pallas_call x1, Pallas kernels: 135 us -> 129 us  [step_kernel(): pl.pallas_call(whole_kernel, out_shape=(jax.ShapeDtypeStruct((ED, KD), F3...]
    slice x2 -> x0, local copies, waits for them, and re-layouts: 2.53 us -> none  [per_device(): return (update, small[1, :ED], small[0, :KD], small[2, 0])]
    pallas_call x0 -> x1, Pallas kernels: none -> 1.56 us  [per_device(): pl.pallas_call(out_kernel, out_shape=(jax.ShapeDtypeStruct((ED, KD), F32)...]
    unnamed x1 -> x0, local copies, waits for them, and re-layouts: 1.54 us -> none
where the time goes in v5:
time: 133 us
  Pallas kernels  131 us (98%)
  between operations  1.97 us (1%)
    pallas_call x1, Pallas kernels, step_kernel(): pl.pallas_call(whole_kernel, out_shape=(jax.ShapeDtypeStruct((ED, KD), F3...  129 us

profile of v5, /device:TPU:1, one launch (start us, length us, event | category | flops | bytes accessed | tf_op | source)
XLA Modules:
  0.0 132.6 jit_solution(14693565889521322521)
XLA Ops:
  2.0 129.1 %step.1 = (f32[36,538]{1,0:T(8,128)}, f32[8,640]{1,0:T(8,128)}) custom-call(bf16[64,4304]{1,0:T(8,128)(2,1)} %hidden.1, f32[36,538]{1,0:T(8,128)} %weight.1, bf16[64,1152]{1,0:T(8,128)(2,1)} %text.1, bf16[64,1152]{1,0:T(8,128)(2,1)} %pooled.1, f32[36]{0:T(128)} %row_moment.1, f32[538]{0:T(1024)} %col_moment.1, f32[1]{0:T(128)} %bitcast.scale_ref, ...), custom_call_target="tpu_custom_call" | custom-call | tf_op jit(solution)/shard_map/step/pallas_call | solution.py:612
  131.1 1.6 %out.1 = (f32[36,538]{1,0:T(8,128)}, f32[36]{0:T(128)}, f32[538]{0:T(1024)}, f32[1]{0:T(128)}) custom-call(f32[36,538]{1,0:T(8,128)} %get-tuple-element.10.update_in, f32[8,640]{1,0:T(8,128)} %get-tuple-element.11.small), custom_call_target="tpu_custom_call" | custom-call | tf_op jit(solution)/shard_map/out/pallas_call | solution.py:697

commit v6 on v5

--- a/solution.py
+++ b/solution.py
@@ -60,7 +60,8 @@
 
 
 class PlaneGather:
-    def __init__(self, piece, a, b, la, rows, ssem, rsem, y, z):
+    def __init__(self, piece, a, b, la, rows, direct, ssem, rsem, y, z):
+        self.direct = direct
         self.piece, self.a, self.b, self.la, self.rows = piece, a, b, la, pl.ds(0, rows)
         self.piece_a = piece.at[self.rows, pl.ds(0, la)]
         self.piece_b = piece.at[self.rows, pl.ds(la, piece.shape[1] - la)]
@@ -151,8 +152,12 @@
     def start(self):
         for dy in range(1, NY):
             self._send(self.piece_a, self._a(0, 0), A0 + dy - 1, self._ydev(dy))
+        if self.direct:
+            for s, sign in ((4, 1), (3, -1), (3, 1), (2, -1), (2, 1), (1, -1), (1, 1)):
+                self._send(self.piece_b, self._b(0, 0), (BP if sign > 0 else BM) + s - 1, self._zdev(sign * s))
         for sign in (1, -1):
-            self._ring_b(1, sign)
+            if not self.direct:
+                self._ring_b(1, sign)
             self._ring_a(1, 0, sign)
         self._spread_b(0)
 
@@ -160,7 +165,8 @@
         for s_sign in (1, -1):
             if k <= (NZ // 2 if s_sign > 0 else NZ // 2 - 1):
                 self._wait(self._b(0, -s_sign * k), (BP if s_sign > 0 else BM) + k - 1, self._zdev(-s_sign))
-                self._ring_b(k + 1, s_sign)
+                if not self.direct:
+                    self._ring_b(k + 1, s_sign)
                 self._spread_b(OFFSETS.index(-s_sign * k))
         for dy in range(NY):
             if k == 1:
@@ -183,8 +189,9 @@
 
 
 def whole_kernel(
-    hidden, weight, text, pooled, row_moment, col_moment, scale_ref, bias_ref,
+    hidden_in, weight_in, text_in, pooled_in, row_in, col_in, scale_ref, bias_ref,
     update_out, small_out,
+    hidden, weight, text, pooled, row_moment, col_moment, in_s,
     hid, wp, logit_a, logit_b, pg_a, pg_b,
     h_out, mg_out, loss_out,
     wa, wb, wc, ta, tb, tn, part, give, take, share, got, img, unit, length,
@@ -202,15 +209,20 @@
     me = c * NX + x
     other = 1 - c
 
-    with jax.named_scope("prep"):
-        wp[...] = jnp.zeros_like(wp)
-        wp[:ED, :KD] = weight[...].astype(BF16)
-        hid[...] = jnp.zeros_like(hid)
-        wa[...] = jnp.zeros_like(wa)
-        wb[...] = jnp.zeros_like(wb)
-        for r in range(NX * NC):
-            hid[(r % NC) * NX + r // NC, :, :KD] = hidden[:, KD * r : KD * (r + 1)]
-    with jax.named_scope("barrier"):
+    loads = [
+        pltpu.make_async_copy(src, dst, in_s.at[i])
+        for i, (src, dst) in enumerate(
+            (
+                (weight_in, weight), (hidden_in, hidden), (text_in, text), (pooled_in, pooled),
+                (row_in, row_moment), (col_in, col_moment),
+            )
+        )
+    ]
+    for load in loads:
+        load.start()
+    wa[...] = jnp.zeros_like(wa)
+    wb[...] = jnp.zeros_like(wb)
+    with jax.named_scope("signal"):
         barrier = pltpu.get_barrier_semaphore()
         peers = [{"z": mod(z + dz, NZ)} for dz in range(1, NZ)]
         peers += [{"y": mod(y + dy, NY)} for dy in range(1, NY)]
@@ -220,10 +232,19 @@
         ]
         for peer in peers:
             pl.semaphore_signal(barrier, inc=1, device_id=peer, device_id_type=MESH)
+
+    with jax.named_scope("prep"):
+        for load in loads:
+            load.wait()
+        wp[...] = jnp.zeros_like(wp)
+        wp[:ED, :KD] = weight[...].astype(BF16)
+        hid[...] = jnp.zeros_like(hid)
+        for r in range(NX * NC):
+            hid[(r % NC) * NX + r // NC, :, :KD] = hidden[:, KD * r : KD * (r + 1)]
+    with jax.named_scope("barrier"):
         pl.semaphore_wait(barrier, len(peers))
-
-    w = PlaneGather(wp, wa, wb, WLA, EG, w_s, w_r, y, z)
-    t = PlaneGather(tn, ta, tb, TLA, TOK, t_s, t_r, y, z)
+    w = PlaneGather(wp, wa, wb, WLA, EG, False, w_s, w_r, y, z)
+    t = PlaneGather(tn, ta, tb, TLA, TOK, False, t_s, t_r, y, z)
 
     with jax.named_scope("wstart"):
         w.start()
@@ -277,40 +298,52 @@
                 rows, wc[384 * n : 384 * (n + 1), :], (((1,), (1,)), ((), ())), preferred_element_type=F32
             ).reshape(NX, TOK, 384)
 
+    hf_rows = [pl.ds(TOK // 2 * hf, TOK // 2) for hf in range(2)]
+
     def reduce_rows(val, gv, tk, sh, gt, ss, rs):
         for dx in (2, 1, 3, 0):
             xx = mod(x + dx, NX)
             gv[xx] = val[other * NX + xx].astype(gv.dtype)
             send(gv.at[xx], tk.at[xx], ss.at[0], rs.at[dx], {"c": other})
         yield
-        for dx in (2, 1, 3):
-            xx = mod(x + dx, NX)
-            arrived(tk.at[xx], ss.at[0], rs.at[dx], {"c": other})
-            sh[dx - 1] = (val[c * NX + xx] + tk[xx].astype(F32)).astype(BF16)
-            send(sh.at[dx - 1], gt.at[dx - 1], ss.at[1], rs.at[NX - 1 + dx], {"x": xx})
+        for hf, rows in enumerate(hf_rows):
+            for dx in (2, 1, 3):
+                xx = mod(x + dx, NX)
+                if hf == 0:
+                    arrived(tk.at[xx], ss.at[0], rs.at[dx], {"c": other})
+                    sh[dx - 1] = (val[c * NX + xx] + tk[xx].astype(F32)).astype(BF16)
+                send(sh.at[dx - 1, rows], gt.at[dx - 1, rows], ss.at[1], rs.at[3 + 3 * hf + dx], {"x": xx})
         yield
         arrived(tk.at[x], ss.at[0], rs.at[0], {"c": other})
-        total = val[me] + tk[x].astype(F32)
-        for dx in (1, 3, 2):
-            arrived(gt.at[dx - 1], ss.at[1], rs.at[NX - 1 + dx], {"x": mod(x - dx, NX)})
-        for dx in (1, 2, 3):
-            total = total + gt[dx - 1].astype(F32)
+        for hf, rows in enumerate(hf_rows):
+            total = val[me, rows] + tk[x, rows].astype(F32)
+            for dx in (1, 3, 2):
+                arrived(gt.at[dx - 1, rows], ss.at[1], rs.at[3 + 3 * hf + dx], {"x": mod(x - dx, NX)})
+            for dx in (1, 2, 3):
+                total = total + gt[dx - 1, rows].astype(F32)
+            yield total
         all_sent(gv, ss.at[0], rs.at[0], {"c": other})
-        all_sent(sh, ss.at[1], rs.at[NX], {"x": mod(x + 1, NX)})
-        yield total
-
-    def share_rows(buf, ss, rs, between=lambda: None):
-        for dx in (2, 1, 3):
-            send(buf.at[me], buf.at[me], ss.at[0], rs.at[dx], {"x": mod(x + dx, NX)})
-        send(buf.at[me], buf.at[me], ss.at[0], rs.at[4], {"c": other})
-        between()
-        for dx in (1, 3, 2):
-            got_at = buf.at[c * NX + mod(x - dx, NX)]
-            arrived(got_at, ss.at[0], rs.at[dx], {"x": mod(x - dx, NX)})
-            send(got_at, got_at, ss.at[0], rs.at[4 + dx], {"c": other})
-        for dx in (0, 1, 3, 2):
-            arrived(buf.at[other * NX + mod(x - dx, NX)], ss.at[0], rs.at[4 + dx], {"c": other})
+        all_sent(sh, ss.at[1], rs.at[4], {"x": mod(x + 1, NX)})
+        yield
+
+    def share_rows(buf, ss, rs):
+        for hf, rows in enumerate(hf_rows):
+            mine = buf.at[me, rows]
+            for dx in (2, 1, 3):
+                send(mine, mine, ss.at[0], rs.at[8 * hf + dx], {"x": mod(x + dx, NX)})
+            send(mine, mine, ss.at[0], rs.at[8 * hf + 4], {"c": other})
+            yield
+        for hf, rows in enumerate(hf_rows):
+            for dx in (1, 3, 2):
+                got_at = buf.at[c * NX + mod(x - dx, NX), rows]
+                arrived(got_at, ss.at[0], rs.at[8 * hf + dx], {"x": mod(x - dx, NX)})
+                send(got_at, got_at, ss.at[0], rs.at[8 * hf + 4 + dx], {"c": other})
+        for hf, rows in enumerate(hf_rows):
+            for dx in (0, 1, 3, 2):
+                at = buf.at[other * NX + mod(x - dx, NX), rows]
+                arrived(at, ss.at[0], rs.at[8 * hf + 4 + dx], {"c": other})
         all_sent(buf.at[pl.ds(0, 7)], ss.at[0], rs.at[1], {"c": other})
+        yield
 
     with jax.named_scope("proj1"):
         project(other)
@@ -326,16 +359,22 @@
     with jax.named_scope("t2"):
         t.step(2)
     with jax.named_scope("red1c_norm"):
-        mixed = pooled[...].astype(F32) + next(red)
-        ln = jnp.sqrt(jnp.sum(mixed * mixed, axis=1, keepdims=True) + EPSILON)
-        length[...] = jnp.broadcast_to(ln, length.shape)
-        un = mixed / ln
-        unit[...] = un
-        img[me] = un.astype(BF16)
+        give_img = share_rows(img, i_s, i_r)
+        for rows in hf_rows:
+            mixed = pooled[rows].astype(F32) + next(red)
+            ln = jnp.sqrt(jnp.sum(mixed * mixed, axis=1, keepdims=True) + EPSILON)
+            length[rows] = jnp.broadcast_to(ln, (TOK // 2, 128))
+            un = mixed / ln
+            unit[rows] = un
+            img[me, rows] = un.astype(BF16)
+            next(give_img)
+        next(red)
+    with jax.named_scope("t3"):
+        t.step(3)
     with jax.named_scope("imgshare"):
-        share_rows(img, i_s, i_r, lambda: t.step(3))
+        next(give_img)
     with jax.named_scope("pairs"):
-        scale = scale_ref[0]
+        scale = jnp.exp(jnp.broadcast_to(scale_ref[0], (8, 128)))[0:1, 0:1]
         bias = bias_ref[0]
         acc[...] = jnp.zeros_like(acc)
         loss_out[...] = jnp.zeros_like(loss_out)
@@ -386,13 +425,16 @@
         def body(j, carry):
             @pl.when(j == 3)
             def _():
-                t.step(4)
+                with jax.named_scope("p_t4"):
+                    t.step(4)
 
             @pl.when(j == 5)
             def _():
-                t.step(5)
-
-            t.far_at(j)
+                with jax.named_scope("p_t5"):
+                    t.step(5)
+
+            with jax.named_scope("p_far"):
+                t.far_at(j)
             now, last = group(j), group(j - 1)
             logits_of(now, 0, logit_a)
             elementwise(logit_b, pg_b, False)
@@ -422,12 +464,16 @@
         elementwise(logit_b, pg_b, True)
         to_images(z, 1, pg_b)
         next(red)
-        ug = (scale * (1.0 / BATCH)) * next(red)
-        un = unit[...]
-        ln = length[:, 0:1]
-        mg_out[me] = ((ug - un * jnp.sum(un * ug, axis=1, keepdims=True)) / ln).astype(BF16)
+        give_mg = share_rows(mg_out, m_s, m_r)
+        for rows in hf_rows:
+            ug = (scale * (1.0 / BATCH)) * next(red)
+            un = unit[rows]
+            mg = (ug - un * jnp.sum(un * ug, axis=1, keepdims=True)) / length[rows, 0:1]
+            mg_out[me, rows] = mg.astype(BF16)
+            next(give_mg)
+        next(red)
     with jax.named_scope("mgshare"):
-        share_rows(mg_out, m_s, m_r)
+        next(give_mg)
 
     def exchange(give_ref, take_ref, base, value, kind):
         give_ref[...] = value
@@ -615,9 +661,16 @@
             jax.ShapeDtypeStruct((ED, KD), F32),
             jax.ShapeDtypeStruct((8, KP), F32),
         ),
-        in_specs=[vmem] * 6 + [smem] * 2,
+        in_specs=[pl.BlockSpec(memory_space=pl.ANY)] * 6 + [smem] * 2,
         out_specs=(vmem,) * 2,
         scratch_shapes=[
+            pltpu.VMEM((TOK, FF), BF16),
+            pltpu.VMEM((ED, KD), F32),
+            pltpu.VMEM((TOK, D), BF16),
+            pltpu.VMEM((TOK, D), BF16),
+            pltpu.VMEM((ED,), F32),
+            pltpu.VMEM((KD,), F32),
+            dma((6,)),
             pltpu.VMEM((n_row, TOK, KP), BF16),
             pltpu.VMEM((EP, KP), BF16),
             pltpu.VMEM((NX * TOK, NY * TOK), F32),
@@ -670,8 +723,8 @@
             pltpu.VMEM((1, 128), F32),
             pltpu.VMEM((NZ - 1, 1, 128), F32),
             dma((2,)), dma((N_MSG,)), dma((2,)), dma((N_MSG,)),
-            dma((1,)), dma((7,)), dma((2,)), dma((7,)), dma((1,)), dma((8,)),
-            dma((2,)), dma((7,)), dma((1,)), dma((8,)),
+            dma((1,)), dma((7,)), dma((2,)), dma((10,)), dma((1,)), dma((16,)),
+            dma((2,)), dma((10,)), dma((1,)), dma((16,)),
             dma((6,)), dma((6,)), dma((1,)), dma((7,)), dma((1,)), dma((7,)),
             dma((1,)), dma((3,)), dma((7,)), dma((41,)),
         ],
@@ -691,7 +744,7 @@
 
 def per_device(pooled, hidden, text, weight, row_moment, col_moment, log_scale, bias):
     update, small = step_kernel(
-        hidden, weight, text, pooled, row_moment, col_moment, jnp.exp(log_scale).reshape(1), bias.reshape(1)
+        hidden, weight, text, pooled, row_moment, col_moment, log_scale.reshape(1), bias.reshape(1)
     )
     vmem = pl.BlockSpec(memory_space=pltpu.VMEM)
     update, new_row, new_col, loss = pl.pallas_call(

time: 133 us -> 126 us (0.947)
  Pallas kernels: 131 us -> 124 us
    pallas_call x1, Pallas kernels: 129 us -> 123 us  [step_kernel(): pl.pallas_call(whole_kernel, out_shape=(jax.ShapeDtypeStruct((ED, KD), F3...]
where the time goes in v6:
time: 126 us
  Pallas kernels  124 us (98%)
  between operations  1.93 us (2%)
    pallas_call x1, Pallas kernels, step_kernel(): pl.pallas_call(whole_kernel, out_shape=(jax.ShapeDtypeStruct((ED, KD), F3...  123 us

profile of v6, /device:TPU:1, one launch (start us, length us, event | category | flops | bytes accessed | tf_op | source)
XLA Modules:
  0.0 126.2 jit_solution(6491572313083938102)
XLA Ops:
  1.9 122.7 %step.1 = (f32[36,538]{1,0:T(8,128)}, f32[8,640]{1,0:T(8,128)}) custom-call(bf16[64,4304]{1,0:T(8,128)(2,1)} %hidden_in.1, f32[36,538]{1,0:T(8,128)} %weight_in.1, bf16[64,1152]{1,0:T(8,128)(2,1)} %text_in.1, bf16[64,1152]{1,0:T(8,128)(2,1)} %pooled_in.1, f32[36]{0:T(128)} %row_in.1, f32[538]{0:T(1024)} %col_in.1, f32[1]{0:T(128)} %bitcast.3.scale_ref, ...), custom_call_target="tpu_custom_call" | custom-call | tf_op jit(solution)/shard_map/step/pallas_call | solution.py:658
  124.7 1.6 %out.1 = (f32[36,538]{1,0:T(8,128)}, f32[36]{0:T(128)}, f32[538]{0:T(1024)}, f32[1]{0:T(128)}) custom-call(f32[36,538]{1,0:T(8,128)} %get-tuple-element.10.update_in, f32[8,640]{1,0:T(8,128)} %get-tuple-element.11.small), custom_call_target="tpu_custom_call" | custom-call | tf_op jit(solution)/shard_map/out/pallas_call | solution.py:750

commit v7 on v6

--- a/solution.py
+++ b/solution.py
@@ -54,6 +54,7 @@
 
 A0, AP, AM, BP, BM, YP, YM, Y2 = 0, 4, 20, 36, 40, 44, 52, 60
 N_MSG = 68
+B_PLACE = (3, 1, 0, 2)
 EXCHANGES = (0, 7, 10, 17, 24, 27, 34)
 A_MSG = range(A0, BP)
 OFFSETS = [0, -1, 1, -2, 2, -3, 3, -4]
@@ -266,6 +267,9 @@
     with jax.named_scope("w45far"):
         w.step(4)
         w.step(5)
+    with jax.named_scope("t1"):
+        t.step(1)
+    with jax.named_scope("wfar"):
         for j in range(8):
             w.far(j)
 
@@ -352,15 +356,13 @@
         next(red)
     with jax.named_scope("proj2"):
         project(c)
-    with jax.named_scope("t1"):
-        t.step(1)
     with jax.named_scope("red1b"):
         next(red)
     with jax.named_scope("t2"):
         t.step(2)
     with jax.named_scope("red1c_norm"):
         give_img = share_rows(img, i_s, i_r)
-        for rows in hf_rows:
+        for hf, rows in enumerate(hf_rows):
             mixed = pooled[rows].astype(F32) + next(red)
             ln = jnp.sqrt(jnp.sum(mixed * mixed, axis=1, keepdims=True) + EPSILON)
             length[rows] = jnp.broadcast_to(ln, (TOK // 2, 128))
@@ -368,11 +370,13 @@
             unit[rows] = un
             img[me, rows] = un.astype(BF16)
             next(give_img)
+            if hf == 0:
+                t.step(3)
         next(red)
-    with jax.named_scope("t3"):
-        t.step(3)
     with jax.named_scope("imgshare"):
         next(give_img)
+    with jax.named_scope("t4"):
+        t.step(4)
     with jax.named_scope("pairs"):
         scale = jnp.exp(jnp.broadcast_to(scale_ref[0], (8, 128)))[0:1, 0:1]
         bias = bias_ref[0]
@@ -423,11 +427,6 @@
             return mod(z + hop * (1 - 2 * lax.rem(j, 2)), NZ)
 
         def body(j, carry):
-            @pl.when(j == 3)
-            def _():
-                with jax.named_scope("p_t4"):
-                    t.step(4)
-
             @pl.when(j == 5)
             def _():
                 with jax.named_scope("p_t5"):
@@ -511,8 +510,20 @@
         mg = mg_out[:, :, pl.ds(pl.multiple_of(256 * yy, 128), 384)].reshape(NX * NC * TOK, 384)
         mg_t = lax.dot_general(choose, mg, (((1,), (1,)), ((), ())), preferred_element_type=F32).astype(BF16)
         grad[yy] = jnp.dot(mg_t, h_all, preferred_element_type=F32).reshape(NZ, EG, KP)
-        b_give[:, dy] = grad[yy, :, :, GLA:GLB].astype(BF16)
+        b_give[:, B_PLACE[dy]] = grad[yy, :, :, GLA:GLB].astype(BF16)
         tail[:, :, 32 * dy : 32 * dy + 32] = grad[yy, :, :, GLB : GLB + 32]
+
+    z_order = (4, 3, 5, 2, 6, 1, 7)
+    z_near = (1, 7, 2, 6, 3, 5, 4)
+    b_parts = (pl.ds(0, 2), pl.ds(2, 3))
+
+    def give_b(k):
+        for dz in z_order:
+            zz = mod(z + dz, NZ)
+            send(
+                b_give.at[zz, b_parts[k]], b_take.at[dz - 1, b_parts[k]],
+                b_s.at[0], b_r.at[7 * k + dz - 1], {"z": zz},
+            )
 
     with jax.named_scope("loss1"):
         loss_sum = jnp.sum(jnp.sum(loss_out[...], axis=0, keepdims=True), axis=1, keepdims=True)
@@ -531,16 +542,13 @@
         gradient_of(1)
         near_p[...] = grad[y_up, half:, :, :GLA].astype(BF16)
         send(near_p, r_near_p, g_s.at[2], g_r.at[2], up)
+        give_b(0)
         gradient_of(3)
         near_m[...] = grad[y_down, :half, :, :GLA].astype(BF16)
         send(near_m, r_near_m, g_s.at[3], g_r.at[3], down)
         gradient_of(0)
         b_give[:, NY] = tail[...].astype(BF16)
-        z_order = (4, 3, 5, 2, 6, 1, 7)
-        z_near = (1, 7, 2, 6, 3, 5, 4)
-        for dz in z_order:
-            zz = mod(z + dz, NZ)
-            send(b_give.at[zz], b_take.at[dz - 1], b_s.at[0], b_r.at[dz - 1], {"z": zz})
+        give_b(1)
     with jax.named_scope("g_relay"):
         arrived(r_far_p, g_s.at[0], g_r.at[0], down)
         relay_p[...] = (grad[y_up, :half, :, :GLA] + r_far_p[...].astype(F32)).astype(BF16)
@@ -567,9 +575,11 @@
             yb_give[dy, 0] = grad[mod(y + dy, NY), pl.ds(z, 1), :, GLA:GLB].reshape(EG, GLB - GLA)
         last = tail[pl.ds(z, 1)].reshape(EG, 128)
         for dz in z_near:
-            arrived(b_take.at[dz - 1], b_s.at[0], b_r.at[dz - 1], {"z": mod(z - dz, NZ)})
+            for k in range(2):
+                arrived(b_take.at[dz - 1, b_parts[k]], b_s.at[0], b_r.at[7 * k + dz - 1], {"z": mod(z - dz, NZ)})
         for dz in z_near:
-            yb_give[:, 0] += b_take[dz - 1, :NY].astype(F32)
+            for dy in range(NY):
+                yb_give[dy, 0] += b_take[dz - 1, B_PLACE[dy]].astype(F32)
             last = last + b_take[dz - 1, NY].astype(F32)
         for dy in range(NY):
             yb_give[dy, 1] = last
@@ -725,7 +735,7 @@
             dma((2,)), dma((N_MSG,)), dma((2,)), dma((N_MSG,)),
             dma((1,)), dma((7,)), dma((2,)), dma((10,)), dma((1,)), dma((16,)),
             dma((2,)), dma((10,)), dma((1,)), dma((16,)),
-            dma((6,)), dma((6,)), dma((1,)), dma((7,)), dma((1,)), dma((7,)),
+            dma((6,)), dma((6,)), dma((1,)), dma((7,)), dma((1,)), dma((14,)),
             dma((1,)), dma((3,)), dma((7,)), dma((41,)),
         ],
         compiler_params=pltpu.CompilerParams(

time: 126 us -> 123 us (0.976)
  Pallas kernels: 124 us -> 121 us
    pallas_call x1, Pallas kernels: 123 us -> 119 us  [step_kernel(): pl.pallas_call(whole_kernel, out_shape=(jax.ShapeDtypeStruct((ED, KD), F3...]
where the time goes in v7:
time: 123 us
  Pallas kernels  121 us (98%)
  between operations  1.93 us (2%)
    pallas_call x1, Pallas kernels, step_kernel(): pl.pallas_call(whole_kernel, out_shape=(jax.ShapeDtypeStruct((ED, KD), F3...  119 us

profile of v7, /device:TPU:1, one launch (start us, length us, event | category | flops | bytes accessed | tf_op | source)
XLA Modules:
  0.0 122.7 jit_solution(14539137578602438128)
XLA Ops:
  1.9 119.2 %step.1 = (f32[36,538]{1,0:T(8,128)}, f32[8,640]{1,0:T(8,128)}) custom-call(bf16[64,4304]{1,0:T(8,128)(2,1)} %hidden_in.1, f32[36,538]{1,0:T(8,128)} %weight_in.1, bf16[64,1152]{1,0:T(8,128)(2,1)} %text_in.1, bf16[64,1152]{1,0:T(8,128)(2,1)} %pooled_in.1, f32[36]{0:T(128)} %row_in.1, f32[538]{0:T(1024)} %col_in.1, f32[1]{0:T(128)} %bitcast.3.scale_ref, ...), custom_call_target="tpu_custom_call" | custom-call | tf_op jit(solution)/shard_map/step/pallas_call | solution.py:668
  121.2 1.6 %out.1 = (f32[36,538]{1,0:T(8,128)}, f32[36]{0:T(128)}, f32[538]{0:T(1024)}, f32[1]{0:T(128)}) custom-call(f32[36,538]{1,0:T(8,128)} %get-tuple-element.10.update_in, f32[8,640]{1,0:T(8,128)} %get-tuple-element.11.small), custom_call_target="tpu_custom_call" | custom-call | tf_op jit(solution)/shard_map/out/pallas_call | solution.py:760

commit v8 on v7

--- a/solution.py
+++ b/solution.py
@@ -52,8 +52,8 @@
     pltpu.make_async_remote_copy(ref, ref, ssem, rsem, device_id=device, device_id_type=MESH).wait_send()
 
 
-A0, AP, AM, BP, BM, YP, YM, Y2 = 0, 4, 20, 36, 40, 44, 52, 60
-N_MSG = 68
+A0, AP, AM, BP, BM, YP, YM, Y2 = 0, 3, 17, 33, 37, 40, 48, 56
+N_MSG = 64
 B_PLACE = (3, 1, 0, 2)
 EXCHANGES = (0, 7, 10, 17, 24, 27, 34)
 A_MSG = range(A0, BP)
@@ -199,7 +199,7 @@
     acc, give2, take2, share2, got2,
     grad, far_p, far_m, near_p, near_m, relay_p, relay_m,
     r_far_p, r_far_m, r_near_p, r_near_m, r_relay_p, r_relay_m,
-    z_give, z_take, tail, b_give, b_take, yb_give, yb_take,
+    z_give, z_take, choose, tail, b_give, b_take, yb_give, yb_take,
     row_give, row_take, cy_give, cy_take, cz_give, cz_take,
     s_give, s_take, l_give, l_take, sy_give, sy_take, sz_give, sz_take,
     w_s, w_r, t_s, t_r, h_s, h_r, p_s, p_r, i_s, i_r, u_s, u_r, m_s, m_r,
@@ -247,6 +247,16 @@
     w = PlaneGather(wp, wa, wb, WLA, EG, False, w_s, w_r, y, z)
     t = PlaneGather(tn, ta, tb, TLA, TOK, False, t_s, t_r, y, z)
 
+    def project(half, k0, k1):
+        rows = h_out[pl.ds(half * NX, NX), :, k0:k1].reshape(NX * TOK, k1 - k0)
+        for n in range(3):
+            lanes = slice(384 * n, 384 * (n + 1))
+            product = lax.dot_general(
+                rows, wc[lanes, k0:k1], (((1,), (1,)), ((), ())), preferred_element_type=F32
+            ).reshape(NX, TOK, 384)
+            at = pl.ds(half * NX, NX)
+            part[at, :, lanes] = product if k0 == 0 else part[at, :, lanes] + product
+
     with jax.named_scope("wstart"):
         w.start()
         row_peers = [(dx, dc) for dx in range(NX) for dc in range(NC) if dx + dc > 0]
@@ -269,11 +279,12 @@
         w.step(5)
     with jax.named_scope("t1"):
         t.step(1)
-    with jax.named_scope("wfar"):
-        for j in range(8):
-            w.far(j)
-
-    with jax.named_scope("compact"):
+    with jax.named_scope("hwait"):
+        for i, (dx, dc) in enumerate(row_peers):
+            xx, cc = mod(x - dx, NX), lax.rem(c + dc, NC)
+            arrived(h_out.at[cc * NX + xx], h_s.at[0], h_r.at[i], {"x": xx, "c": cc})
+
+    with jax.named_scope("compactA"):
         r_id = lax.broadcasted_iota(jnp.int32, (4 * ED, 4 * EP), 0)
         c_id = lax.broadcasted_iota(jnp.int32, (4 * ED, 4 * EP), 1)
         pick = jnp.zeros((4 * ED, 4 * EP), F32)
@@ -283,24 +294,13 @@
         pick = pick.astype(BF16)
         for g in range(8):
             yy, z0 = g // 2, 4 * (g % 2)
-            wc[pl.ds(4 * ED * g, 4 * ED), 0:WLA] = jnp.dot(
-                pick, jnp.concatenate([wa[(z0 + k) * NY + yy] for k in range(4)], axis=0), preferred_element_type=F32
-            ).astype(BF16)
-            wc[pl.ds(4 * ED * g, 4 * ED), WLA:KP] = jnp.dot(
-                pick, wb[yy * NZ + z0 : yy * NZ + z0 + 4].reshape(4 * EP, KP - WLA), preferred_element_type=F32
-            ).astype(BF16)
-
-    with jax.named_scope("hwait"):
-        for i, (dx, dc) in enumerate(row_peers):
-            xx, cc = mod(x - dx, NX), lax.rem(c + dc, NC)
-            arrived(h_out.at[cc * NX + xx], h_s.at[0], h_r.at[i], {"x": xx, "c": cc})
-
-    def project(half):
-        rows = h_out[pl.ds(half * NX, NX)].reshape(NX * TOK, KP)
-        for n in range(3):
-            part[pl.ds(half * NX, NX), :, 384 * n : 384 * (n + 1)] = lax.dot_general(
-                rows, wc[384 * n : 384 * (n + 1), :], (((1,), (1,)), ((), ())), preferred_element_type=F32
-            ).reshape(NX, TOK, 384)
+            pieces = jnp.concatenate([wa[(z0 + k) * NY + yy] for k in range(4)], axis=0)
+            wc[pl.ds(4 * ED * g, 4 * ED), 0:WLA] = jnp.dot(pick, pieces, preferred_element_type=F32).astype(BF16)
+        for half in range(2):
+            project(half, 0, WLA)
+    with jax.named_scope("wfar"):
+        for j in range(8):
+            w.far(j)
 
     hf_rows = [pl.ds(TOK // 2 * hf, TOK // 2) for hf in range(2)]
 
@@ -342,6 +342,7 @@
                 got_at = buf.at[c * NX + mod(x - dx, NX), rows]
                 arrived(got_at, ss.at[0], rs.at[8 * hf + dx], {"x": mod(x - dx, NX)})
                 send(got_at, got_at, ss.at[0], rs.at[8 * hf + 4 + dx], {"c": other})
+        yield
         for hf, rows in enumerate(hf_rows):
             for dx in (0, 1, 3, 2):
                 at = buf.at[other * NX + mod(x - dx, NX), rows]
@@ -349,13 +350,18 @@
         all_sent(buf.at[pl.ds(0, 7)], ss.at[0], rs.at[1], {"c": other})
         yield
 
+    with jax.named_scope("compactB"):
+        for g in range(8):
+            yy, z0 = g // 2, 4 * (g % 2)
+            pieces = wb[yy * NZ + z0 : yy * NZ + z0 + 4].reshape(4 * EP, KP - WLA)
+            wc[pl.ds(4 * ED * g, 4 * ED), WLA:KP] = jnp.dot(pick, pieces, preferred_element_type=F32).astype(BF16)
     with jax.named_scope("proj1"):
-        project(other)
+        project(other, WLA, KP)
     with jax.named_scope("red1a"):
         red = reduce_rows(part, give, take, share, got, p_s, p_r)
         next(red)
     with jax.named_scope("proj2"):
-        project(c)
+        project(c, WLA, KP)
     with jax.named_scope("red1b"):
         next(red)
     with jax.named_scope("t2"):
@@ -374,6 +380,7 @@
                 t.step(3)
         next(red)
     with jax.named_scope("imgshare"):
+        next(give_img)
         next(give_img)
     with jax.named_scope("t4"):
         t.step(4)
@@ -501,18 +508,31 @@
     zi = lax.broadcasted_iota(jnp.int32, (NZ, EG, 384), 0)
     ji = lax.broadcasted_iota(jnp.int32, (NZ, EG, 384), 1)
     li = lax.broadcasted_iota(jnp.int32, (NZ, EG, 384), 2)
-    h_all = h_out[...].reshape(NX * NC * TOK, KP)
+
+    def product(dy, h):
+        yy = mod(y + dy, NY)
+        at = pl.ds(h * NX, NX)
+        mg = mg_out[at, :, pl.ds(pl.multiple_of(256 * yy, 128), 384)].reshape(NX * TOK, 384)
+        mg_t = lax.dot_general(choose[dy], mg, (((1,), (1,)), ((), ())), preferred_element_type=F32).astype(BF16)
+        rows = h_out[at].reshape(NX * TOK, KP)
+        return jnp.dot(mg_t, rows, preferred_element_type=F32).reshape(NZ, EG, KP)
 
     def gradient_of(dy):
         yy = mod(y + dy, NY)
-        choose = jnp.where((ji < ED) & (li == 32 * yy + ED * zi + ji), 1.0, 0.0)
-        choose = choose.reshape(NZ * EG, 384).astype(BF16)
-        mg = mg_out[:, :, pl.ds(pl.multiple_of(256 * yy, 128), 384)].reshape(NX * NC * TOK, 384)
-        mg_t = lax.dot_general(choose, mg, (((1,), (1,)), ((), ())), preferred_element_type=F32).astype(BF16)
-        grad[yy] = jnp.dot(mg_t, h_all, preferred_element_type=F32).reshape(NZ, EG, KP)
+        if dy == 0:
+            grad[yy] = product(dy, c)
+        grad[yy] += product(dy, other)
         b_give[:, B_PLACE[dy]] = grad[yy, :, :, GLA:GLB].astype(BF16)
         tail[:, :, 32 * dy : 32 * dy + 32] = grad[yy, :, :, GLB : GLB + 32]
 
+    with jax.named_scope("g_own"):
+        for dy in (2, 1, 3, 0):
+            mask = (ji < ED) & (li == 32 * mod(y + dy, NY) + ED * zi + ji)
+            choose[dy] = jnp.where(mask, 1.0, 0.0).reshape(NZ * EG, 384).astype(BF16)
+            if dy > 0:
+                grad[mod(y + dy, NY)] = product(dy, c)
+    with jax.named_scope("mgwait"):
+        next(give_mg)
     z_order = (4, 3, 5, 2, 6, 1, 7)
     z_near = (1, 7, 2, 6, 3, 5, 4)
     b_parts = (pl.ds(0, 2), pl.ds(2, 3))
@@ -713,6 +733,7 @@
             *[pltpu.VMEM((NZ // 2, EG, GLA), BF16)] * 12,
             pltpu.VMEM((NZ, EG, GLA), BF16),
             pltpu.VMEM((NZ - 1, EG, GLA), BF16),
+            pltpu.VMEM((NY, NZ * EG, 384), BF16),
             pltpu.VMEM((NZ, EG, 128), F32),
             pltpu.VMEM((NZ, NY + 1, EG, 128), BF16),
             pltpu.VMEM((NZ - 1, NY + 1, EG, 128), BF16),

time: 123 us -> 121 us (0.984)
  Pallas kernels: 121 us -> 119 us
    pallas_call x1, Pallas kernels: 119 us -> 118 us  [step_kernel(): pl.pallas_call(whole_kernel, out_shape=(jax.ShapeDtypeStruct((ED, KD), F3...]
where the time goes in v8:
time: 121 us
  Pallas kernels  119 us (98%)
  between operations  1.93 us (2%)
    pallas_call x1, Pallas kernels, step_kernel(): pl.pallas_call(whole_kernel, out_shape=(jax.ShapeDtypeStruct((ED, KD), F3...  118 us

profile of v8, /device:TPU:1, one launch (start us, length us, event | category | flops | bytes accessed | tf_op | source)
XLA Modules:
  0.0 121.2 jit_solution(3916569179884881413)
XLA Ops:
  1.9 117.8 %step.1 = (f32[36,538]{1,0:T(8,128)}, f32[8,640]{1,0:T(8,128)}) custom-call(bf16[64,4304]{1,0:T(8,128)(2,1)} %hidden_in.1, f32[36,538]{1,0:T(8,128)} %weight_in.1, bf16[64,1152]{1,0:T(8,128)(2,1)} %text_in.1, bf16[64,1152]{1,0:T(8,128)(2,1)} %pooled_in.1, f32[36]{0:T(128)} %row_in.1, f32[538]{0:T(1024)} %col_in.1, f32[1]{0:T(128)} %bitcast.3.scale_ref, ...), custom_call_target="tpu_custom_call" | custom-call | tf_op jit(solution)/shard_map/step/pallas_call | solution.py:688
  119.7 1.6 %out.1 = (f32[36,538]{1,0:T(8,128)}, f32[36]{0:T(128)}, f32[538]{0:T(1024)}, f32[1]{0:T(128)}) custom-call(f32[36,538]{1,0:T(8,128)} %get-tuple-element.10.update_in, f32[8,640]{1,0:T(8,128)} %get-tuple-element.11.small), custom_call_target="tpu_custom_call" | custom-call | tf_op jit(solution)/shard_map/out/pallas_call | solution.py:781

commit v9 on v8

--- a/solution.py
+++ b/solution.py
@@ -61,8 +61,8 @@
 
 
 class PlaneGather:
-    def __init__(self, piece, a, b, la, rows, direct, ssem, rsem, y, z):
-        self.direct = direct
+    def __init__(self, piece, a, b, la, rows, late, ssem, rsem, y, z):
+        self.late = late
         self.piece, self.a, self.b, self.la, self.rows = piece, a, b, la, pl.ds(0, rows)
         self.piece_a = piece.at[self.rows, pl.ds(0, la)]
         self.piece_b = piece.at[self.rows, pl.ds(la, piece.shape[1] - la)]
@@ -153,21 +153,19 @@
     def start(self):
         for dy in range(1, NY):
             self._send(self.piece_a, self._a(0, 0), A0 + dy - 1, self._ydev(dy))
-        if self.direct:
-            for s, sign in ((4, 1), (3, -1), (3, 1), (2, -1), (2, 1), (1, -1), (1, 1)):
-                self._send(self.piece_b, self._b(0, 0), (BP if sign > 0 else BM) + s - 1, self._zdev(sign * s))
         for sign in (1, -1):
-            if not self.direct:
-                self._ring_b(1, sign)
+            self._ring_b(1, sign)
             self._ring_a(1, 0, sign)
-        self._spread_b(0)
+        if not self.late:
+            self._spread_b(0)
 
     def step(self, k):
+        if self.late and k == 1:
+            self._spread_b(0)
         for s_sign in (1, -1):
             if k <= (NZ // 2 if s_sign > 0 else NZ // 2 - 1):
                 self._wait(self._b(0, -s_sign * k), (BP if s_sign > 0 else BM) + k - 1, self._zdev(-s_sign))
-                if not self.direct:
-                    self._ring_b(k + 1, s_sign)
+                self._ring_b(k + 1, s_sign)
                 self._spread_b(OFFSETS.index(-s_sign * k))
         for dy in range(NY):
             if k == 1:
@@ -185,7 +183,7 @@
                     )
                     self._ring_a(s + 1, dy, sign)
         for j, o in enumerate(OFFSETS):
-            if abs(o) == k - 1:
+            if abs(o) == k - 1 and (j > 0 or not self.late) or (j == 0 and self.late and k == 2):
                 self._near_b(j)
 
 
@@ -245,7 +243,7 @@
     with jax.named_scope("barrier"):
         pl.semaphore_wait(barrier, len(peers))
     w = PlaneGather(wp, wa, wb, WLA, EG, False, w_s, w_r, y, z)
-    t = PlaneGather(tn, ta, tb, TLA, TOK, False, t_s, t_r, y, z)
+    t = PlaneGather(tn, ta, tb, TLA, TOK, True, t_s, t_r, y, z)
 
     def project(half, k0, k1):
         rows = h_out[pl.ds(half * NX, NX), :, k0:k1].reshape(NX * TOK, k1 - k0)
@@ -634,10 +632,10 @@
         e_col = e_id[:, 0:128]
         l_col = k_id[:, 0:128]
         rows = jnp.broadcast_to(jnp.sum(squared, axis=1, keepdims=True), (EG, 128))
-        exchange(row_give, row_take, 0, rows, "row")
+        row_line = jnp.sum(jnp.where(e_col == l_col, rows, 0.0), axis=0, keepdims=True)
+        exchange(row_give, row_take, 0, row_line, "row")
         cols = jnp.sum(squared, axis=0, keepdims=True)
-        rows = collected(row_take, 0, rows, "row")
-        row_line = jnp.sum(jnp.where(e_col == l_col, rows, 0.0), axis=0, keepdims=True)[:, :ED]
+        row_line = collected(row_take, 0, row_line, "row")[:, :ED]
         row_line = DECAY_RATE * row_moment[...].reshape(1, ED) + (1.0 - DECAY_RATE) * row_line / FF
         new_row = jnp.sum(
             jnp.where(
@@ -739,8 +737,8 @@
             pltpu.VMEM((NZ - 1, NY + 1, EG, 128), BF16),
             pltpu.VMEM((NY, 2, EG, 128), F32),
             pltpu.VMEM((NY - 1, 2, EG, 128), F32),
-            pltpu.VMEM((EG, 128), F32),
-            pltpu.VMEM((n_row - 1, EG, 128), F32),
+            pltpu.VMEM((1, 128), F32),
+            pltpu.VMEM((n_row - 1, 1, 128), F32),
             pltpu.VMEM((1, 2 * KP), F32),
             pltpu.VMEM((NY - 1, 1, 2 * KP), F32),
             pltpu.VMEM((1, 2 * KP), F32),

time: 121 us -> 120 us (level)
    pallas_call x1, Pallas kernels: 118 us -> 116 us  [step_kernel(): pl.pallas_call(whole_kernel, out_shape=(jax.ShapeDtypeStruct((ED, KD), F3...]
where the time goes in v9:
time: 120 us; the launch traced here: 119 us
  Pallas kernels  118 us (98%)
  between operations  1.93 us (2%)
    pallas_call x1, Pallas kernels, step_kernel(): pl.pallas_call(whole_kernel, out_shape=(jax.ShapeDtypeStruct((ED, KD), F3...  116 us

profile of v9, /device:TPU:1, one launch (start us, length us, event | category | flops | bytes accessed | tf_op | source)
XLA Modules:
  0.0 119.4 jit_solution(8612366078804724203)
XLA Ops:
  1.9 115.9 %step.1 = (f32[36,538]{1,0:T(8,128)}, f32[8,640]{1,0:T(8,128)}) custom-call(bf16[64,4304]{1,0:T(8,128)(2,1)} %hidden_in.1, f32[36,538]{1,0:T(8,128)} %weight_in.1, bf16[64,1152]{1,0:T(8,128)(2,1)} %text_in.1, bf16[64,1152]{1,0:T(8,128)(2,1)} %pooled_in.1, f32[36]{0:T(128)} %row_in.1, f32[538]{0:T(1024)} %col_in.1, f32[1]{0:T(128)} %bitcast.3.scale_ref, ...), custom_call_target="tpu_custom_call" | custom-call | tf_op jit(solution)/shard_map/step/pallas_call | solution.py:686
  117.9 1.6 %out.1 = (f32[36,538]{1,0:T(8,128)}, f32[36]{0:T(128)}, f32[538]{0:T(1024)}, f32[1]{0:T(128)}) custom-call(f32[36,538]{1,0:T(8,128)} %get-tuple-element.10.update_in, f32[8,640]{1,0:T(8,128)} %get-tuple-element.11.small), custom_call_target="tpu_custom_call" | custom-call | tf_op jit(solution)/shard_map/out/pallas_call | solution.py:779

commit v10 on v9

--- a/solution.py
+++ b/solution.py
@@ -200,7 +200,7 @@
     z_give, z_take, choose, tail, b_give, b_take, yb_give, yb_take,
     row_give, row_take, cy_give, cy_take, cz_give, cz_take,
     s_give, s_take, l_give, l_take, sy_give, sy_take, sz_give, sz_take,
-    w_s, w_r, t_s, t_r, h_s, h_r, p_s, p_r, i_s, i_r, u_s, u_r, m_s, m_r,
+    w_s, w_r, t_s, t_r, h_s, h_r, p_s, p_r, i_s, i_r,
     g_s, g_r, z_s, z_r, b_s, b_r, yb_s, yb_r, st_s, st_r,
 ):
     x, c = lax.axis_index("x"), lax.axis_index("c")
@@ -463,12 +463,12 @@
         to_images(final, 1, pg_b)
         to_images(z, 0, pg_a)
     with jax.named_scope("red2"):
-        red = reduce_rows(acc, give2, take2, share2, got2, u_s, u_r)
+        red = reduce_rows(acc, give2, take2, share2, got2, p_s, p_r)
         next(red)
         elementwise(logit_b, pg_b, True)
         to_images(z, 1, pg_b)
         next(red)
-        give_mg = share_rows(mg_out, m_s, m_r)
+        give_mg = share_rows(mg_out, i_s, i_r)
         for rows in hf_rows:
             ug = (scale * (1.0 / BATCH)) * next(red)
             un = unit[rows]
@@ -753,7 +753,6 @@
             pltpu.VMEM((NZ - 1, 1, 128), F32),
             dma((2,)), dma((N_MSG,)), dma((2,)), dma((N_MSG,)),
             dma((1,)), dma((7,)), dma((2,)), dma((10,)), dma((1,)), dma((16,)),
-            dma((2,)), dma((10,)), dma((1,)), dma((16,)),
             dma((6,)), dma((6,)), dma((1,)), dma((7,)), dma((1,)), dma((14,)),
             dma((1,)), dma((3,)), dma((7,)), dma((41,)),
         ],

time: 120 us -> 119 us (level)
  no operation moved by 1% of the time
where the time goes in v10:
time: 119 us
  Pallas kernels  117 us (98%)
  between operations  1.93 us (2%)
    pallas_call x1, Pallas kernels, step_kernel(): pl.pallas_call(whole_kernel, out_shape=(jax.ShapeDtypeStruct((ED, KD), F3...  116 us

profile of v10, /device:TPU:1, one launch (start us, length us, event | category | flops | bytes accessed | tf_op | source)
XLA Modules:
  0.0 119.2 jit_solution(8280262185281416171)
XLA Ops:
  1.9 115.7 %step.1 = (f32[36,538]{1,0:T(8,128)}, f32[8,640]{1,0:T(8,128)}) custom-call(bf16[64,4304]{1,0:T(8,128)(2,1)} %hidden_in.1, f32[36,538]{1,0:T(8,128)} %weight_in.1, bf16[64,1152]{1,0:T(8,128)(2,1)} %text_in.1, bf16[64,1152]{1,0:T(8,128)(2,1)} %pooled_in.1, f32[36]{0:T(128)} %row_in.1, f32[538]{0:T(1024)} %col_in.1, f32[1]{0:T(128)} %bitcast.3.scale_ref, ...), custom_call_target="tpu_custom_call" | custom-call | tf_op jit(solution)/shard_map/step/pallas_call | solution.py:686
  117.6 1.6 %out.1 = (f32[36,538]{1,0:T(8,128)}, f32[36]{0:T(128)}, f32[538]{0:T(1024)}, f32[1]{0:T(128)}) custom-call(f32[36,538]{1,0:T(8,128)} %get-tuple-element.10.update_in, f32[8,640]{1,0:T(8,128)} %get-tuple-element.11.small), custom_call_target="tpu_custom_call" | custom-call | tf_op jit(solution)/shard_map/out/pallas_call | solution.py:778
